TPU v7x, 32 devices: a whole 2x2x4 slice. The times are simulated.
32 devices in a mesh: grp: 4 (over x, core), gx: 2 (over y), gy: 4 (over z).
Axes of the slice: x: 2, y: 2, z: 4, core: 2. Of those that a mesh axis runs over, the one named last changes fastest.
Arguments:
- pressure: float32 [24, 128, 1024], P(None, ('grp', 'gy'), 'gx'), may hold values from -2 to 0.2
- soil_class: int32 [24, 128, 1024], P(None, ('grp', 'gy'), 'gx'), may hold values from 0 to 11
- capacity_range: float32 [12], replicated, may hold values from 0.25 to 0.45
- inverse_entry: float32 [12], replicated, may hold values from 0.3 to 3
- shape_index: float32 [12], replicated, may hold values from 1.3 to 2.5
- conductivity: float32 [12], replicated, may hold values from 0.05 to 1
- depth: float32 [128, 1024], P('grp', ('gx', 'gy')), may hold values from 0 to 2
- elevation: float32 [128, 1024], P('grp', ('gx', 'gy')), may hold values from -4 to 4
- roughness: float32 [128, 1024], P('grp', ('gx', 'gy')), may hold values from 2 to 8
- rain: float32 [128, 1024], P('grp', ('gx', 'gy')), may hold values from 0.1 to 1
- land_mask: int32 [128, 1024], P('grp', ('gx', 'gy')), may hold values 0 or 1
- channel_mask: int32 [128, 1024], P('grp', ('gx', 'gy')), may hold values 0 or 1
Outputs:
- head: float32 [24, 128, 1024], P(None, ('grp', 'gy'), 'gx')
- water: float32 [128, 1024], P('grp', ('gx', 'gy'))
All inputs are finite; a program needn't handle non-finite values. No bound on the sum of `land_mask` or of `channel_mask` on one device may be relied on, other than what follows from the above.
Results may differ from a plain program's by a relative error of at most 0.0003.
Values sent between devices are 32-bit elements; how exact they have to be, the bound alone decides.
No kernel may reach another device: no remote copies, remote signals or barrier semaphores. Data moves between devices by JAX's collectives and lax.ppermute only.
A program may use at most 64 MiB of HBM per device.

v0:
```python
import jax
import jax.numpy as jnp
from jax import lax
from jax.sharding import PartitionSpec as P

SWEEPS = 2
PASSES = 3


STORAGE = 0.01
LATERAL = 4.0
VERTICAL = 4.0
GRAVITY_STEP = 0.5
SUCTION_FLOOR = 0.01
SLOPE_FLOOR = 0.1
SURFACE_STEP = 0.3
LEAKANCE = 0.5
SOURCE_GAIN = 1.0


def with_halo(shard, sides, width):
    for axis, dim in sides:
        size, length = (lax.axis_size(axis), shard.shape[dim])
        up = [(i, (i + 1) % size) for i in range(size - 1)]
        down = [(j, i) for i, j in up]
        last = lax.slice_in_dim(shard, length - width, length, axis=dim)
        leading = lax.slice_in_dim(shard, 0, width, axis=dim)
        before = lax.ppermute(last, axis, up)
        after = lax.ppermute(leading, axis, down)
        shard = jnp.concatenate([before, shard, after], axis=dim)
    return shard


def lookup(soil_class, tables):
    results = []
    for table in tables:
        filled = jnp.zeros(soil_class.shape, table.dtype)
        for kind_number in range(table.shape[0]):
            filled = jnp.where(soil_class == kind_number, table[kind_number], filled)
        results.append(filled)
    return results


def closures(pressure, capacity_range, inverse_entry, pore_index, conductivity):
    exponent = 1.0 / (1.0 - pore_index)
    scaled = jnp.maximum(-inverse_entry * pressure, SUCTION_FLOOR)
    log_scaled = jnp.log(scaled)
    log_sum = jnp.log1p(jnp.exp(exponent * log_scaled))
    saturation = jnp.exp(-pore_index * log_sum)
    content = capacity_range * saturation
    capacity = STORAGE + capacity_range * pore_index * exponent * inverse_entry * jnp.exp(
        (exponent - 1.0) * log_scaled - (pore_index + 1.0) * log_sum
    )
    conduct = (
        conductivity
        * jnp.sqrt(saturation)
        * jnp.square(1.0 - jnp.exp(pore_index * (exponent * log_scaled - log_sum)))
    )
    return (content, capacity, conduct)


def update_cells(padded, conduct_pad, capacity, content_gap, source):
    layers = padded.shape[0] - 2
    rows = padded.shape[1] - 2
    cols = padded.shape[2] - 2
    center = padded[1:-1, 1:-1, 1:-1]
    own_conduct = conduct_pad[1:-1, 1:-1, 1:-1]
    numerator = capacity * center - content_gap
    denominator = capacity
    neighbours = (
        (1, 0, 1, LATERAL, 0.0),
        (1, 2, 1, LATERAL, 0.0),
        (1, 1, 0, LATERAL, 0.0),
        (1, 1, 2, LATERAL, 0.0),
        (0, 1, 1, VERTICAL, GRAVITY_STEP),
        (2, 1, 1, VERTICAL, -GRAVITY_STEP),
    )
    for first, second, third, weight, offset in neighbours:
        beside = padded[first : first + layers, second : second + rows, third : third + cols]
        beside_conduct = conduct_pad[
            first : first + layers, second : second + rows, third : third + cols
        ]
        face_weight = weight * jnp.sqrt(own_conduct * beside_conduct)
        numerator = numerator + face_weight * (beside + offset)
        denominator = denominator + face_weight
    gained = jnp.concatenate(
        [(SOURCE_GAIN * source)[None], jnp.zeros((layers - 1, rows, cols), source.dtype)], axis=0
    )
    numerator = numerator + gained
    return numerator / denominator


def face_flux(upper_level, lower_level, upper_depth, lower_depth, upper_convey, lower_convey):
    slope = upper_level - lower_level
    upwind = jnp.where(slope >= 0, upper_depth, lower_depth)
    carried = upwind * jnp.cbrt(upwind * upwind)
    return (
        jnp.sqrt(upper_convey * lower_convey)
        * carried
        * slope
        / jnp.sqrt(jnp.maximum(jnp.abs(slope), SLOPE_FLOOR))
    )


def overland(depth_pad, level_pad, convey_pad, leak, top, rain):
    current = depth_pad[1:-1, 1:-1]
    surface = level_pad + depth_pad
    across = face_flux(
        surface[:-1, 1:-1],
        surface[1:, 1:-1],
        depth_pad[:-1, 1:-1],
        depth_pad[1:, 1:-1],
        convey_pad[:-1, 1:-1],
        convey_pad[1:, 1:-1],
    )
    along = face_flux(
        surface[1:-1, :-1],
        surface[1:-1, 1:],
        depth_pad[1:-1, :-1],
        depth_pad[1:-1, 1:],
        convey_pad[1:-1, :-1],
        convey_pad[1:-1, 1:],
    )
    outflow = across[1:] - across[:-1] + (along[:, 1:] - along[:, :-1])
    rate = leak * (current - top)
    return (jnp.maximum(current + SURFACE_STEP * (rain - rate - outflow), 0.0), rate)


def trim_edges(field, margin):
    rows = field.shape[-2]
    cols = field.shape[-1]
    return field[..., margin : rows - margin, margin : cols - margin]


def pad_layers(field):
    return jnp.pad(field, ((1, 1), (0, 0), (0, 0)))


def local(
    pressure,
    soil_class,
    capacity_range,
    inverse_entry,
    shape_index,
    conductivity,
    depth,
    elevation,
    roughness,
    rain,
    land_mask,
    channel_mask,
):
    pore_table = 1.0 - 1.0 / shape_index
    tables = (capacity_range, inverse_entry, pore_table, conductivity)
    range_cells, entry_cells, pore_cells, conduct_cells = lookup(soil_class, tables)
    content0, capacity, conduct = closures(
        pressure, range_cells, entry_cells, pore_cells, conduct_cells
    )
    top_conduct = conduct[0]
    top, top_surface = (
        lax.all_to_all(pressure[0], "gy", split_axis=1, concat_axis=0, tiled=True),
        lax.all_to_all(top_conduct, "gy", split_axis=1, concat_axis=0, tiled=True),
    )
    leak = LEAKANCE * land_mask.astype(jnp.float32) * top_surface
    convey = (1.0 + channel_mask.astype(jnp.float32)) / roughness
    exchange = jnp.zeros_like(depth)
    surface_pad = with_halo(
        jnp.stack([depth, elevation, convey, leak, top, rain]),
        (("grp", 1), (("gx", "gy"), 2)),
        PASSES,
    )
    water = surface_pad[0]
    for pass_number in range(PASSES):
        water, rate = overland(
            water,
            trim_edges(surface_pad[1], pass_number),
            trim_edges(surface_pad[2], pass_number),
            trim_edges(surface_pad[3], pass_number + 1),
            trim_edges(surface_pad[4], pass_number + 1),
            trim_edges(surface_pad[5], pass_number + 1),
        )
        exchange = exchange + SURFACE_STEP * trim_edges(rate, PASSES - pass_number - 1)
    source = lax.all_to_all(exchange, "gy", split_axis=0, concat_axis=1, tiled=True)
    head = pressure
    content = content0
    for sweep_number in range(SWEEPS):
        soil_rim = with_halo(jnp.stack([head, conduct]), ((("grp", "gy"), 2), ("gx", 3)), 1)
        head = update_cells(
            pad_layers(soil_rim[0]), pad_layers(soil_rim[1]), capacity, content - content0, source
        )
        if sweep_number + 1 < SWEEPS:
            content, capacity, conduct = closures(
                head, range_cells, entry_cells, pore_cells, conduct_cells
            )
    return (head, water)


def solution(mesh):
    return jax.shard_map(
        local,
        mesh=mesh,
        in_specs=(
            P(None, ("grp", "gy"), "gx"),
            P(None, ("grp", "gy"), "gx"),
            P(),
            P(),
            P(),
            P(),
            P("grp", ("gx", "gy")),
            P("grp", ("gx", "gy")),
            P("grp", ("gx", "gy")),
            P("grp", ("gx", "gy")),
            P("grp", ("gx", "gy")),
            P("grp", ("gx", "gy")),
        ),
        out_specs=(P(None, ("grp", "gy"), "gx"), P("grp", ("gx", "gy"))),
        check_vma=False,
    )
```

profile of v0, /device:TPU:0, one launch (start us, length us, event | category | flops | bytes accessed | tf_op | source)
XLA Modules:
  0.0 134.9 jit_solution(11352913227923329193)
XLA Ops:
  0.7 1.8 %fusion.114 = (f32[1]{0:T(128)}, f32[1]{0:T(128)}, f32[1]{0:T(128)}, f32[1]{0:T(128)}, f32[1]{0:T(128)}, /*index=5*/f32[1]{0:T(128)}, f32[1]{0:T(128)}, f32[1]{0...) fusion(f32[12]{0:T(128)} %param.15), kind=kLoop, calls=%fused_computation.231 | loop fusion | bytes 96 | tf_op jit(solution)/shard_map/slice | solution.py:39
  2.5 1.8 %fusion.113 = (f32[1]{0:T(128)}, f32[1]{0:T(128)}, f32[1]{0:T(128)}, f32[1]{0:T(128)}, f32[1]{0:T(128)}, /*index=5*/f32[1]{0:T(128)}, f32[1]{0:T(128)}, f32[1]{0...) fusion(f32[12]{0:T(128)} %param.17), kind=kLoop, calls=%fused_computation.230 | loop fusion | bytes 96 | tf_op jit(solution)/shard_map/slice | solution.py:39
  4.9 0.7 fusion.112
  5.6 26.2 %multiply_multiply_fusion = (f32[24,8,512]{2,1,0:T(8,128)S(1)}, f32[24,8,512]{2,1,0:T(8,128)S(1)}, f32[24,8,512]{2,1,0:T(8,128)S(1)}, f32[24,8,512]{2,1,0:T(8,12...) fusion(f32[24,8,512]{2,1,0:T(8,128)} %param.12, ...), kind=kLoop, calls=%fused_computation.100 | loop fusion | flops 6094848 | bytes 3539088 | tf_op jit(solution)/shard_map/mul | solution.py:55
  32.5 6.3 %all-to-all-start = ((f32[8,4,128]{2,0,1:T(8,128)}), f32[8,4,128]{2,0,1:T(8,128)S(1)}, u32[]{:S(2)}, u32[]{:S(2)}) async-start(f32[8,4,128]{2,0,1:T(8,128)} %slice_bitcast_fusion.10), calls=%async_computation | async-start | bytes 32768 | tf_op jit(solution)/shard_map/all_to_all | solution.py:162
  39.5 4.9 %all-to-all-done = f32[8,4,128]{2,0,1:T(8,128)S(1)} async-done(((f32[8,4,128]{2,0,1:T(8,128)}), f32[8,4,128]{2,0,1:T(8,128)S(1)}, u32[]{:S(2)}, u32[]{:S(2)}) %all-to-all-start) | async-done | bytes 16416 | tf_op jit(solution)/shard_map/all_to_all | solution.py:162
  44.4 3.2 %all-to-all-start.1 = ((f32[8,4,128]{2,0,1:T(8,128)}), f32[8,4,128]{2,0,1:T(8,128)S(1)}, u32[]{:S(2)}, u32[]{:S(2)}) async-start(f32[8,4,128]{2,0,1:T(8,128)} %slice_bitcast_fusion.11), calls=%async_computation.1 | async-start | bytes 32768 | tf_op jit(solution)/shard_map/all_to_all | solution.py:161
  47.7 5.6 %all-to-all-done.1 = f32[8,4,128]{2,0,1:T(8,128)S(1)} async-done(((f32[8,4,128]{2,0,1:T(8,128)}), f32[8,4,128]{2,0,1:T(8,128)S(1)}, u32[]{:S(2)}, u32[]{:S(2)}) %all-to-all-start.1) | async-done | bytes 16416 | tf_op jit(solution)/shard_map/all_to_all | solution.py:161
  53.3 1.3 collective-permute-start.5
  54.6 3.0 %collective-permute-start.4 = (f32[6,3,128]{2,1,0:T(4,128)S(1)}, f32[6,3,128]{2,1,0:T(4,128)S(1)}, u32[]{:S(2)}, u32[]{:S(2)}) collective-permute-start(f32[6,3,128]{2,1,0:T(4,128)S(1)} %get-tuple-element.49), channel_id=1, source_target_pairs={{0,8},{8,16},{16,24},{1,9},{9,17},{17,25},{2,10},{10,18},{18,26},{... | collective-permute-start | bytes 27656 | tf_op jit(solution)/shard_map/ppermute | solution.py:28
  57.8 1.3 collective-permute-start.1
  59.1 4.6 %collective-permute-start = (f32[2,24,1,512]{3,2,1,0:T(1,128)S(1)}, f32[2,24,1,512]{3,2,1,0:T(1,128)S(1)}, u32[]{:S(2)}, u32[]{:S(2)}) collective-permute-start(f32[2,24,1,512]{3,2,1,0:T(1,128)S(1)} %get-tuple-element.37), channel_id=1, source_target_pairs={{0,1},{1,2},{2,3},{3,8},{8,9},{9,10},{10,11},{11,16},{16,17},{17,1... | collective-permute-start | bytes 294920 | tf_op jit(solution)/shard_map/ppermute | solution.py:28
  63.8 1.3 collective-permute-start.7
  65.1 4.6 %collective-permute-start.6 = (f32[6,38,3]{2,1,0:T(8,128)S(1)}, f32[6,38,3]{2,1,0:T(8,128)S(1)}, u32[]{:S(2)}, u32[]{:S(2)}) collective-permute-start(f32[6,38,3]{2,1,0:T(8,128)S(1)} %get-tuple-element.47), channel_id=1, source_target_pairs={{0,1},{1,2},{2,3},{3,4},{4,5},{5,6},{6,7},{8,9},{9,10},{10,11},{11... | collective-permute-start | bytes 8216 | tf_op jit(solution)/shard_map/ppermute | solution.py:28
  70.3 2.1 %collective-permute-done.7 = f32[6,38,3]{2,1,0:T(8,128)S(1)} collective-permute-done((f32[6,38,3]{2,1,0:T(8,128)S(1)}, f32[6,38,3]{2,1,0:T(8,128)S(1)}, u32[]{:S(2)}, u32[]{:S(2)}) %collective-permute-start.7) | collective-permute-done | bytes 2768 | tf_op jit(solution)/shard_map/ppermute | solution.py:29
  74.7 1.3 collective-permute-start.3
  76.0 9.4 %collective-permute-start.2 = (f32[2,24,10,1]{3,2,1,0:T(8,128)S(1)}, f32[2,24,10,1]{3,2,1,0:T(8,128)S(1)}, u32[]{:S(2)}, u32[]{:S(2)}) collective-permute-start(f32[2,24,10,1]{3,2,1,0:T(8,128)S(1)} %get-tuple-element.33), channel_id=1, source_target_pairs={{0,4},{1,5},{2,6},{3,7},{8,12},{9,13},{10,14},{11,15},{16,20},{17,... | collective-permute-start | bytes 5768 | tf_op jit(solution)/shard_map/ppermute | solution.py:28
  85.4 0.7 fusion.96
  86.1 3.2 %all-to-all-start.2 = ((f32[4,8,128]{2,1,0:T(8,128)}), f32[4,8,128]{2,1,0:T(8,128)S(1)}, u32[]{:S(2)}, u32[]{:S(2)}) async-start(f32[4,8,128]{2,1,0:T(8,128)} %get-tuple-element.46), calls=%async_computation.2 | async-start | bytes 32768 | tf_op jit(solution)/shard_map/all_to_all | solution.py:183
  89.4 3.5 %collective-permute-done.3 = f32[2,24,10,1]{3,2,1,0:T(8,128)S(1)} collective-permute-done((f32[2,24,10,1]{3,2,1,0:T(8,128)S(1)}, f32[2,24,10,1]{3,2,1,0:T(8,128)S(1)}, u32[]{:S(2)}, u32[]{:S(2)}) %collective-permute-start.3) | collective-permute-done | bytes 1952 | tf_op jit(solution)/shard_map/ppermute | solution.py:29
  92.9 1.2 collective-permute-done.2
  94.1 2.4 %pad_maximum_fusion = f32[2,24,10,514]{3,2,1,0:T(8,128)S(1)} fusion(f32[2,24,10,1]{3,2,1,0:T(8,128)S(1)} %collective-permute-done.3, f32[2,24,1,512]{3,2,1,0:T(1,128)} %copy-done.1, f32[1,24,8,512]{3,2,1,0:T(8,128)S(1)} %bitcast.118, f32[1,24,8,512]{3,2,1,0:T(8,128)S(1)} %bitcast.112, f32[2,24,1,512]{3,2,1,0:T(1,128)} %copy-done.2, ...), kind=kLoop, calls=%fused_computation | loop fusion | flops 1233600 | bytes 1973760 | tf_op jit(solution)/shard_map/concatenate | solution.py:30
  96.6 11.8 %multiply_bitcast_fusion = (f32[1,24,8,512]{3,2,1,0:T(8,128)S(1)}, f32[24,8,512]{2,1,0:T(8,128)S(1)}, f32[24,8,512]{2,1,0:T(8,128)S(1)}) fusion(f32[24,8,512]{2,1,0:T(8,128)S(1)} %get-tuple-element.14, f32[24,8,512]{2,1,0:T(8,128)S(1)} %get-tuple-element.13, f32[24,8,512]{2,1,0:T(8,128)S(1)} %get-tuple-element.12, f32[1,8,512]{2,1,0:T(8,128)S(1)} %bitcast.119, ...), kind=kLoop, calls=%fused_computation.94 | loop fusion | flops 7667712 | bytes 9846832 | tf_op jit(solution)/shard_map/stack | solution.py:187
  108.5 1.3 collective-permute-start.9
  109.8 4.6 %collective-permute-start.8 = (f32[2,24,1,512]{3,2,1,0:T(1,128)S(1)}, f32[2,24,1,512]{3,2,1,0:T(1,128)S(1)}, u32[]{:S(2)}, u32[]{:S(2)}) collective-permute-start(f32[2,24,1,512]{3,2,1,0:T(1,128)S(1)} %get-tuple-element.35), channel_id=1, source_target_pairs={{0,1},{1,2},{2,3},{3,8},{8,9},{9,10},{10,11},{11,16},{16,17},{17,1... | collective-permute-start | bytes 294920 | tf_op jit(solution)/shard_map/ppermute | solution.py:28
  115.0 1.5 %collective-permute-done.8 = f32[2,24,1,512]{3,2,1,0:T(1,128)S(1)} collective-permute-done((f32[2,24,1,512]{3,2,1,0:T(1,128)S(1)}, f32[2,24,1,512]{3,2,1,0:T(1,128)S(1)}, u32[]{:S(2)}, u32[]{:S(2)}) %collective-permute-start.8) | collective-permute-done | bytes 98336 | tf_op jit(solution)/shard_map/ppermute | solution.py:28
  116.9 1.3 collective-permute-start.11
  118.2 4.8 %collective-permute-start.10 = (f32[2,24,10,1]{3,2,1,0:T(8,128)S(1)}, f32[2,24,10,1]{3,2,1,0:T(8,128)S(1)}, u32[]{:S(2)}, u32[]{:S(2)}) collective-permute-start(f32[2,24,10,1]{3,2,1,0:T(8,128)S(1)} %get-tuple-element.31), channel_id=1, source_target_pairs={{0,4},{1,5},{2,6},{3,7},{8,12},{9,13},{10,14},{11,15},{16,20},{17,... | collective-permute-start | bytes 5768 | tf_op jit(solution)/shard_map/ppermute | solution.py:28
  122.9 5.6 %collective-permute-done.11 = f32[2,24,10,1]{3,2,1,0:T(8,128)S(1)} collective-permute-done((f32[2,24,10,1]{3,2,1,0:T(8,128)S(1)}, f32[2,24,10,1]{3,2,1,0:T(8,128)S(1)}, u32[]{:S(2)}, u32[]{:S(2)}) %collective-permute-start.11) | collective-permute-done | bytes 1952 | tf_op jit(solution)/shard_map/ppermute | solution.py:29
  128.5 1.8 %collective-permute-done.10 = f32[2,24,10,1]{3,2,1,0:T(8,128)S(1)} collective-permute-done((f32[2,24,10,1]{3,2,1,0:T(8,128)S(1)}, f32[2,24,10,1]{3,2,1,0:T(8,128)S(1)}, u32[]{:S(2)}, u32[]{:S(2)}) %collective-permute-start.10) | collective-permute-done | bytes 1952 | tf_op jit(solution)/shard_map/ppermute | solution.py:28
  130.3 1.4 %pad_maximum_fusion.1 = f32[2,24,10,514]{3,2,1,0:T(8,128)S(1)} fusion(f32[2,24,10,1]{3,2,1,0:T(8,128)S(1)} %collective-permute-done.11, f32[2,24,1,512]{3,2,1,0:T(1,128)S(1)} %collective-permute-done.9, f32[1,24,8,512]{3,2,1,0:T(8,128)S(1)} %get-tuple-element.5, f32[1,24,8,512]{3,2,1,0:T(8,128)S(1)} %bitcast.115, ...), kind=kLoop, calls=%fused_computation.1 | loop fusion | flops 1233600 | bytes 1973760 | tf_op jit(solution)/shard_map/concatenate | solution.py:30
  131.9 3.1 %fusion.1 = f32[24,8,512]{2,1,0:T(8,128)} fusion(f32[1,8,512]{2,1,0:T(8,128)S(1)} %bitcast.120, f32[24,10,514]{2,1,0:T(8,128)S(1)} %get-tuple-element.28, f32[24,10,514]{2,1,0:T(8,128)S(1)} %get-tuple-element.27, f32[24,8,512]{2,1,0:T(8,128)S(1)} %get-tuple-element.7, f32[24,8,512]{2,1,0:T(8,128)S(1)} %get-tuple-element.14, ...), kind=kLoop, calls=%fused_computation.17 | loop fusion | flops 5996544 | bytes 8273920 | tf_op jit(solution)/shard_map/div | solution.py:90
  (57 shorter events, 6.3 us)
Async XLA Ops:
  0.6 38.3 %copy-start = (f32[24,8,512]{2,1,0:T(8,128)S(1)}, f32[24,8,512]{2,1,0:T(8,128)}, u32[]{:S(2)}) copy-start(f32[24,8,512]{2,1,0:T(8,128)} %param.12) | copy-start | bytes 1179652
  0.6 38.2 %copy-start.7 = (f32[32,128]{1,0:T(8,128)S(1)}, f32[32,128]{1,0:T(8,128)}, u32[]{:S(2)}) copy-start(f32[32,128]{1,0:T(8,128)} %param.18) | copy-start | bytes 49156
  0.7 38.2 %copy-start.8 = (f32[32,128]{1,0:T(8,128)S(1)}, f32[32,128]{1,0:T(8,128)}, u32[]{:S(2)}) copy-start(f32[32,128]{1,0:T(8,128)} %param.19) | copy-start | bytes 49156
  0.7 38.2 %copy-start.4 = (f32[32,128]{1,0:T(8,128)S(1)}, f32[32,128]{1,0:T(8,128)}, u32[]{:S(2)}) copy-start(f32[32,128]{1,0:T(8,128)} %param.20) | copy-start | bytes 49156
  0.7 38.2 %copy-start.5 = (s32[32,128]{1,0:T(8,128)S(1)}, s32[32,128]{1,0:T(8,128)}, u32[]{:S(2)}) copy-start(s32[32,128]{1,0:T(8,128)} %param.23) | copy-start | bytes 49156
  5.6 42.1 %copy-start.6 = (s32[32,128]{1,0:T(8,128)S(1)}, s32[32,128]{1,0:T(8,128)}, u32[]{:S(2)}) copy-start(s32[32,128]{1,0:T(8,128)} %param.22) | copy-start | bytes 49156
  5.6 47.6 %copy-start.9 = (f32[32,128]{1,0:T(8,128)S(1)}, f32[32,128]{1,0:T(8,128)}, u32[]{:S(2)}) copy-start(f32[32,128]{1,0:T(8,128)} %param.21) | copy-start | bytes 49156
  5.6 64.0 %copy-start.3 = (f32[12]{0:T(128)S(1)}, f32[12]{0:T(128)}, u32[]{:S(2)}) copy-start(f32[12]{0:T(128)} %param.14) | copy-start | bytes 148
  32.5 12.0 %all-to-all-start = ((f32[8,4,128]{2,0,1:T(8,128)}), f32[8,4,128]{2,0,1:T(8,128)S(1)}, u32[]{:S(2)}, u32[]{:S(2)}) async-start(f32[8,4,128]{2,0,1:T(8,128)} %slice_bitcast_fusion.10), calls=%async_computation | async-start | bytes 32768 | tf_op jit(solution)/shard_map/all_to_all | solution.py:162
  44.4 8.8 %all-to-all-start.1 = ((f32[8,4,128]{2,0,1:T(8,128)}), f32[8,4,128]{2,0,1:T(8,128)S(1)}, u32[]{:S(2)}, u32[]{:S(2)}) async-start(f32[8,4,128]{2,0,1:T(8,128)} %slice_bitcast_fusion.11), calls=%async_computation.1 | async-start | bytes 32768 | tf_op jit(solution)/shard_map/all_to_all | solution.py:161
  53.3 10.3 %collective-permute-start.5 = (f32[6,3,128]{2,1,0:T(4,128)S(1)}, f32[6,3,128]{2,1,0:T(4,128)S(1)}, u32[]{:S(2)}, u32[]{:S(2)}) collective-permute-start(f32[6,3,128]{2,1,0:T(4,128)S(1)} %get-tuple-element.50), channel_id=1, source_target_pairs={{8,0},{16,8},{24,16},{9,1},{17,9},{25,17},{10,2},{18,10},{26,18},{... | collective-permute-start | bytes 27656 | tf_op jit(solution)/shard_map/ppermute | solution.py:29
  54.6 9.0 %collective-permute-start.4 = (f32[6,3,128]{2,1,0:T(4,128)S(1)}, f32[6,3,128]{2,1,0:T(4,128)S(1)}, u32[]{:S(2)}, u32[]{:S(2)}) collective-permute-start(f32[6,3,128]{2,1,0:T(4,128)S(1)} %get-tuple-element.49), channel_id=1, source_target_pairs={{0,8},{8,16},{16,24},{1,9},{9,17},{17,25},{2,10},{10,18},{18,26},{... | collective-permute-start | bytes 27656 | tf_op jit(solution)/shard_map/ppermute | solution.py:28
  57.8 16.2 %collective-permute-start.1 = (f32[2,24,1,512]{3,2,1,0:T(1,128)S(1)}, f32[2,24,1,512]{3,2,1,0:T(1,128)S(1)}, u32[]{:S(2)}, u32[]{:S(2)}) collective-permute-start(f32[2,24,1,512]{3,2,1,0:T(1,128)S(1)} %get-tuple-element.38), channel_id=1, source_target_pairs={{1,0},{2,1},{3,2},{8,3},{9,8},{10,9},{11,10},{16,11},{17,16},{18,1... | collective-permute-start | bytes 294920 | tf_op jit(solution)/shard_map/ppermute | solution.py:29
  59.1 15.0 %collective-permute-start = (f32[2,24,1,512]{3,2,1,0:T(1,128)S(1)}, f32[2,24,1,512]{3,2,1,0:T(1,128)S(1)}, u32[]{:S(2)}, u32[]{:S(2)}) collective-permute-start(f32[2,24,1,512]{3,2,1,0:T(1,128)S(1)} %get-tuple-element.37), channel_id=1, source_target_pairs={{0,1},{1,2},{2,3},{3,8},{8,9},{9,10},{10,11},{11,16},{16,17},{17,1... | collective-permute-start | bytes 294920 | tf_op jit(solution)/shard_map/ppermute | solution.py:28
  63.8 8.6 %collective-permute-start.7 = (f32[6,38,3]{2,1,0:T(8,128)S(1)}, f32[6,38,3]{2,1,0:T(8,128)S(1)}, u32[]{:S(2)}, u32[]{:S(2)}) collective-permute-start(f32[6,38,3]{2,1,0:T(8,128)S(1)} %get-tuple-element.48), channel_id=1, source_target_pairs={{1,0},{2,1},{3,2},{4,3},{5,4},{6,5},{7,6},{9,8},{10,9},{11,10},{12... | collective-permute-start | bytes 8216 | tf_op jit(solution)/shard_map/ppermute | solution.py:29
  65.1 7.6 %collective-permute-start.6 = (f32[6,38,3]{2,1,0:T(8,128)S(1)}, f32[6,38,3]{2,1,0:T(8,128)S(1)}, u32[]{:S(2)}, u32[]{:S(2)}) collective-permute-start(f32[6,38,3]{2,1,0:T(8,128)S(1)} %get-tuple-element.47), channel_id=1, source_target_pairs={{0,1},{1,2},{2,3},{3,4},{4,5},{5,6},{6,7},{8,9},{9,10},{10,11},{11... | collective-permute-start | bytes 8216 | tf_op jit(solution)/shard_map/ppermute | solution.py:28
  74.0 0.6 copy-start.1
  74.0 0.7 copy-start.2
  74.7 18.2 %collective-permute-start.3 = (f32[2,24,10,1]{3,2,1,0:T(8,128)S(1)}, f32[2,24,10,1]{3,2,1,0:T(8,128)S(1)}, u32[]{:S(2)}, u32[]{:S(2)}) collective-permute-start(f32[2,24,10,1]{3,2,1,0:T(8,128)S(1)} %get-tuple-element.34), channel_id=1, source_target_pairs={{4,0},{5,1},{6,2},{7,3},{12,8},{13,9},{14,10},{15,11},{20,16},{21,... | collective-permute-start | bytes 5768 | tf_op jit(solution)/shard_map/ppermute | solution.py:29
  76.0 18.1 %collective-permute-start.2 = (f32[2,24,10,1]{3,2,1,0:T(8,128)S(1)}, f32[2,24,10,1]{3,2,1,0:T(8,128)S(1)}, u32[]{:S(2)}, u32[]{:S(2)}) collective-permute-start(f32[2,24,10,1]{3,2,1,0:T(8,128)S(1)} %get-tuple-element.33), channel_id=1, source_target_pairs={{0,4},{1,5},{2,6},{3,7},{8,12},{9,13},{10,14},{11,15},{16,20},{17,... | collective-permute-start | bytes 5768 | tf_op jit(solution)/shard_map/ppermute | solution.py:28
  86.1 10.5 %all-to-all-start.2 = ((f32[4,8,128]{2,1,0:T(8,128)}), f32[4,8,128]{2,1,0:T(8,128)S(1)}, u32[]{:S(2)}, u32[]{:S(2)}) async-start(f32[4,8,128]{2,1,0:T(8,128)} %get-tuple-element.46), calls=%async_computation.2 | async-start | bytes 32768 | tf_op jit(solution)/shard_map/all_to_all | solution.py:183
  108.5 6.5 %collective-permute-start.9 = (f32[2,24,1,512]{3,2,1,0:T(1,128)S(1)}, f32[2,24,1,512]{3,2,1,0:T(1,128)S(1)}, u32[]{:S(2)}, u32[]{:S(2)}) collective-permute-start(f32[2,24,1,512]{3,2,1,0:T(1,128)S(1)} %get-tuple-element.36), channel_id=1, source_target_pairs={{1,0},{2,1},{3,2},{8,3},{9,8},{10,9},{11,10},{16,11},{17,16},{18,1... | collective-permute-start | bytes 294920 | tf_op jit(solution)/shard_map/ppermute | solution.py:29
  109.8 6.8 %collective-permute-start.8 = (f32[2,24,1,512]{3,2,1,0:T(1,128)S(1)}, f32[2,24,1,512]{3,2,1,0:T(1,128)S(1)}, u32[]{:S(2)}, u32[]{:S(2)}) collective-permute-start(f32[2,24,1,512]{3,2,1,0:T(1,128)S(1)} %get-tuple-element.35), channel_id=1, source_target_pairs={{0,1},{1,2},{2,3},{3,8},{8,9},{9,10},{10,11},{11,16},{16,17},{17,1... | collective-permute-start | bytes 294920 | tf_op jit(solution)/shard_map/ppermute | solution.py:28
  116.9 11.7 %collective-permute-start.11 = (f32[2,24,10,1]{3,2,1,0:T(8,128)S(1)}, f32[2,24,10,1]{3,2,1,0:T(8,128)S(1)}, u32[]{:S(2)}, u32[]{:S(2)}) collective-permute-start(f32[2,24,10,1]{3,2,1,0:T(8,128)S(1)} %get-tuple-element.32), channel_id=1, source_target_pairs={{4,0},{5,1},{6,2},{7,3},{12,8},{13,9},{14,10},{15,11},{20,16},{21,... | collective-permute-start | bytes 5768 | tf_op jit(solution)/shard_map/ppermute | solution.py:29
  118.2 12.1 %collective-permute-start.10 = (f32[2,24,10,1]{3,2,1,0:T(8,128)S(1)}, f32[2,24,10,1]{3,2,1,0:T(8,128)S(1)}, u32[]{:S(2)}, u32[]{:S(2)}) collective-permute-start(f32[2,24,10,1]{3,2,1,0:T(8,128)S(1)} %get-tuple-element.31), channel_id=1, source_target_pairs={{0,4},{1,5},{2,6},{3,7},{8,12},{9,13},{10,14},{11,15},{16,20},{17,... | collective-permute-start | bytes 5768 | tf_op jit(solution)/shard_map/ppermute | solution.py:28
where the time goes:
time: 138 us; the launch traced here: 135 us
  starting transfers between devices  51.5 us (37%)
  other arithmetic  48.3 us (35%)
  waiting for transfers between devices  27.1 us (20%)
  local copies, waits for them, and re-layouts  6.96 us (5%)
    ppermute x6, starting transfers between devices, with_halo(): before = lax.ppermute(last, axis, up)  30.9 us
    mul x1, other arithmetic, closures(): conductivity * jnp.sqrt(saturation)  26.2 us
    ppermute x6, waiting for transfers between devices, with_halo(): after = lax.ppermute(leading, axis, down)  11.8 us
    another operation x1, other arithmetic, local(): jnp.stack([head, conduct])  11.8 us
    ppermute x6, starting transfers between devices, with_halo(): after = lax.ppermute(leading, axis, down)  7.74 us
    all_to_all x1, starting transfers between devices, local(): lax.all_to_all(top_conduct, 'gy', split_axis=1, concat_axis=0, tiled=True)  6.35 us
    all_to_all x1, waiting for transfers between devices, local(): lax.all_to_all(pressure[0], 'gy', split_axis=1, concat_axis=0, tiled=True)  5.55 us
    slice x4, local copies, waits for them, and re-layouts, lookup(): filled = jnp.where(soil_class == kind_number, table[kind_number], filled)  4.97 us
  transfers between devices with their start and end apart: 15, of which 10 were waited for; matrix products, arithmetic and copies ran while one was open for 4% of the time, Pallas kernels for 0%

commit v1 on v0

v1 whole, which is shorter than its diff:
```python
import jax
import jax.numpy as jnp
from jax import lax
from jax.experimental import pallas as pl
from jax.experimental.pallas import tpu as pltpu
from jax.sharding import PartitionSpec as P

PASSES = 3
STORAGE = 0.01
GRAVITY_STEP = 0.5
SUCTION_FLOOR = 0.01
SLOPE_FLOOR = 0.1
SURFACE_STEP = 0.3
LEAKANCE = 0.5

LANES = 128
SUBS = 8
TOP_LAYERS = 4


def shift(x, axis, step):
    size = lax.axis_size(axis)
    return lax.ppermute(x, axis, [(i, (i + step) % size) for i in range(size)])


def class_tables(capacity_range, inverse_entry, shape_index, conductivity):
    pore = 1.0 - 1.0 / shape_index
    expo = 1.0 / (1.0 - pore)
    rows = [
        -inverse_entry,
        expo,
        pore,
        capacity_range,
        2.0 * jnp.sqrt(conductivity),
        capacity_range * pore * expo * inverse_entry,
        conductivity,
        expo - 1.0,
    ]
    return jnp.pad(jnp.stack(rows), ((0, 0), (0, LANES - shape_index.shape[0])))


def pick(tab_ref, row, idx):
    table = jnp.broadcast_to(tab_ref[row : row + 1, :], idx.shape)
    return jnp.take_along_axis(table, idx, axis=1, mode="promise_in_bounds")


def closure(tab_ref, idx, p):
    logs = jnp.log2(jnp.maximum(pick(tab_ref, 0, idx) * p, SUCTION_FLOOR))
    grown = 1.0 + jnp.exp2(pick(tab_ref, 1, idx) * logs)
    drop = pick(tab_ref, 2, idx) * jnp.log2(grown)
    content = pick(tab_ref, 3, idx) * jnp.exp2(-drop)
    ratio = jnp.exp2(pick(tab_ref, 7, idx) * logs - drop)
    capacity = STORAGE + pick(tab_ref, 5, idx) * ratio / grown
    root = pick(tab_ref, 4, idx) * jnp.exp2(-0.25 * drop) * jnp.abs(1.0 - ratio)
    return content, capacity, root


def lateral(x):
    rows, width = x.shape
    return (
        pltpu.roll(x, 1, 0)
        + pltpu.roll(x, rows - 1, 0)
        + pltpu.roll(x, 1, 1)
        + pltpu.roll(x, width - 1, 1)
    )


def chunks(width):
    return [slice(i, i + LANES) for i in range(0, width, LANES)]


def soil_mask(flags_ref, rows, width, own_rows, own_cols):
    r = lax.broadcasted_iota(jnp.int32, (rows, width), 0)
    c = lax.broadcasted_iota(jnp.int32, (rows, width), 1)
    above = jnp.where(r >= rows - 2, flags_ref[0], 0)
    below = jnp.where((r >= own_rows) & (r < own_rows + 2), flags_ref[1], 0)
    left = jnp.where(c >= width - 2, flags_ref[2], 0)
    right = jnp.where((c >= own_cols) & (c < own_cols + 2), flags_ref[3], 0)
    in_rows = jnp.where(r < own_rows, 1, above + below)
    in_cols = jnp.where(c < own_cols, 1, left + right)
    return (in_rows * in_cols).astype(jnp.float32)


def soil_sweeps(layers, p_ref, c_ref, tab_ref, mask_ref, s, gain, out):
    _, rows, width = p_ref.shape
    h_ref, q_ref, n_ref, d_ref, h2_ref, q2_ref, n2_ref, d2_ref, k_ref = s
    zero = jnp.zeros((rows, width), jnp.float32)
    for ref in (h_ref, q_ref, h2_ref, q2_ref):
        ref[0] = zero
        ref[layers + 1] = zero

    def first(z, carry):
        for ch in chunks(width):
            p = p_ref[z, :, ch]
            content, capacity, root = closure(tab_ref, c_ref[z, :, ch], p)
            root = root * mask_ref[:, ch]
            h_ref[z + 1, :, ch] = root
            q_ref[z + 1, :, ch] = root * p
            n_ref[z, :, ch] = capacity * p
            d_ref[z, :, ch] = capacity
            k_ref[z, :, ch] = content
        return carry

    lax.fori_loop(0, layers, first, 0)

    def sums(z, h, q):
        mid, over, under = h[z + 1], h[z], h[z + 2]
        weights = lateral(mid) + over + under
        flows = lateral(q[z + 1]) + q[z] + q[z + 2] + GRAVITY_STEP * (over - under)
        return mid, weights, flows

    def second(z, carry):
        mid, weights, flows = sums(z, h_ref, q_ref)
        top = n_ref[z] + mid * flows
        if gain is not None:
            top = top + jnp.where(z == 0, 1.0, 0.0) * gain
        q2_ref[z + 1] = top / (d_ref[z] + mid * weights)
        for ch in chunks(width):
            p = q2_ref[z + 1, :, ch]
            content, capacity, root = closure(tab_ref, c_ref[z, :, ch], p)
            root = root * mask_ref[:, ch]
            h2_ref[z + 1, :, ch] = root
            q2_ref[z + 1, :, ch] = root * p
            n2_ref[z, :, ch] = capacity * p - (content - k_ref[z, :, ch])
            d2_ref[z, :, ch] = capacity
        return carry

    lax.fori_loop(0, layers, second, 0)

    def third(z, carry):
        mid, weights, flows = sums(z, h2_ref, q2_ref)
        top = n2_ref[z] + mid * flows
        if gain is not None:
            top = top + jnp.where(z == 0, 1.0, 0.0) * gain
        out(z, top / (d2_ref[z] + mid * weights))
        return carry

    return third


def soil_scratch(layers, rows, width):
    tall = pltpu.VMEM((layers + 2, rows, width), jnp.float32)
    flat = pltpu.VMEM((layers, rows, width), jnp.float32)
    return [tall, tall, flat, flat, tall, tall, flat, flat, flat]


def soil_kernel(flags_ref, tab_ref, p_in, c_in, up_in, down_in, left_in, right_in, out_ref, pe_out, ce_out, pe, ce, mask_ref, *s):
    layers, own, cols = p_in.shape
    _, rows, width = pe.shape
    lane = lax.broadcasted_iota(jnp.int32, (rows, LANES), 1)
    pad = jnp.zeros((rows - own, cols), jnp.float32)

    def build(z, carry):
        for f, (src, dst) in enumerate(((p_in, pe), (c_in, ce))):
            kind = dst.dtype
            dst[z, own:, :cols] = pad.astype(kind)
            dst[z, :own, :cols] = src[z]
            dst[z, own : own + 2, :cols] = down_in[f, z].astype(kind)
            dst[z, rows - 2 :, :cols] = up_in[f, z].astype(kind)
            edge = jnp.zeros((rows, LANES), jnp.float32)
            for col in range(2):
                edge = jnp.where(lane == col, pltpu.roll(right_in[f, col], (LANES + col - z) % LANES, 1), edge)
                spot = LANES - 2 + col
                edge = jnp.where(lane == spot, pltpu.roll(left_in[f, col], (LANES + spot - z) % LANES, 1), edge)
            dst[z, :, cols:] = edge.astype(kind)
        return carry

    lax.fori_loop(0, layers, build, 0)
    mask_ref[...] = soil_mask(flags_ref, rows, width, own, cols)

    def out(z, p):
        out_ref[z] = p[:own, :cols]

    third = soil_sweeps(layers, pe, ce, tab_ref, mask_ref, s, None, out)
    lax.fori_loop(0, layers, third, 0)
    pe_out[...] = pe[:TOP_LAYERS]
    ce_out[...] = ce[:TOP_LAYERS]


def soil_interior(flags, tables, pressure, soil_class, up, down, left, right):
    layers, own, cols = pressure.shape
    rows, width = own + SUBS, cols + LANES
    return pl.pallas_call(
        soil_kernel,
        out_shape=(
            jax.ShapeDtypeStruct(pressure.shape, jnp.float32),
            jax.ShapeDtypeStruct((TOP_LAYERS, rows, width), jnp.float32),
            jax.ShapeDtypeStruct((TOP_LAYERS, rows, width), jnp.int32),
        ),
        in_specs=[pl.BlockSpec(memory_space=pltpu.SMEM)] + [pl.BlockSpec(memory_space=pltpu.VMEM)] * 7,
        out_specs=[pl.BlockSpec(memory_space=pltpu.VMEM)] * 3,
        scratch_shapes=[
            pltpu.VMEM((layers, rows, width), jnp.float32),
            pltpu.VMEM((layers, rows, width), jnp.int32),
            pltpu.VMEM((rows, width), jnp.float32),
        ]
        + soil_scratch(layers, rows, width),
        name="soil_interior",
    )(flags, tables, pressure, soil_class, up, down, left, right)


def last_kernel(
    spot_ref, flags_ref, tab_ref, surf_ref, tops_ref, pe, ce, head_in, head_out, water_ref,
    ex_ref, w_ref, mask_ref, new_ref, sem, *s, own, own_rows, own_cols,
):
    del head_in
    _, rows, width = surf_ref.shape
    block_rows, block_cols = rows - SUBS, width - LANES
    r = lax.broadcasted_iota(jnp.int32, (rows, width), 0)
    c = lax.broadcasted_iota(jnp.int32, (rows, width), 1)
    row_ok = jnp.where(r < block_rows, 1, jnp.where(r >= rows - 3, spot_ref[2], jnp.where(r < block_rows + 3, spot_ref[3], 0)))
    col_ok = jnp.where(c < block_cols, 1, jnp.where(c >= width - 3, flags_ref[2], jnp.where(c < block_cols + 3, flags_ref[3], 0)))
    inside = (row_ok * col_ok).astype(jnp.float32)
    level = surf_ref[1]
    convey = jnp.sqrt(surf_ref[2]) * inside
    leak = surf_ref[3]
    rain = surf_ref[4]
    top = tops_ref[0]

    def across(x):
        return pltpu.roll(x, rows - 1, 0)

    def along(x):
        return pltpu.roll(x, width - 1, 1)

    gates = [convey * across(convey), convey * along(convey)]
    parts = []
    for ch in chunks(width):
        _, _, root = closure(tab_ref, tops_ref[1, :, ch].astype(jnp.int32), top[:, ch])
        parts.append(0.25 * root * root)
    leak = leak * jnp.concatenate(parts, axis=1)
    water = surf_ref[0]
    exchange = jnp.zeros_like(water)
    for _ in range(PASSES):
        surface = level + water
        power = jnp.where(water > 0.0, jnp.exp2((5.0 / 3.0) * jnp.log2(jnp.maximum(water, 1e-30))), 0.0)
        outflow = jnp.zeros_like(water)
        for axis, gate, beside in ((0, gates[0], across), (1, gates[1], along)):
            slope = surface - beside(surface)
            carried = jnp.where(slope >= 0.0, power, beside(power))
            flux = gate * carried * slope * lax.rsqrt(jnp.maximum(jnp.abs(slope), SLOPE_FLOOR))
            outflow = outflow + flux - pltpu.roll(flux, 1, axis)
        rate = leak * (water - top)
        exchange = exchange + SURFACE_STEP * rate
        water = jnp.maximum(water + SURFACE_STEP * (rain - rate - outflow), 0.0)
    ex_ref[...] = exchange
    w_ref[...] = water
    water_ref[...] = w_ref[:block_rows, :block_cols]
    first = pl.multiple_of(spot_ref[0], SUBS)
    after = pl.multiple_of(spot_ref[0] + own, SUBS)
    before = pl.multiple_of(spot_ref[1], SUBS)
    sub = lax.broadcasted_iota(jnp.int32, (SUBS, width), 0)
    rim = jnp.where(sub == SUBS - 1, ex_ref[pl.ds(before, SUBS), :], jnp.where(sub == 0, ex_ref[pl.ds(after, SUBS), :], 0.0))
    gain = jnp.concatenate([ex_ref[pl.ds(first, own), :], rim], axis=0)
    mask_ref[...] = soil_mask(flags_ref, own + SUBS, width, own, block_cols)

    def out(z, p):
        new_ref[z] = p[:own, :block_cols]

    third = soil_sweeps(TOP_LAYERS, pe, ce, tab_ref, mask_ref, s, gain, out)
    lax.fori_loop(0, TOP_LAYERS - 2, third, 0)
    copy = pltpu.make_async_copy(new_ref, head_out.at[: TOP_LAYERS - 2], sem)
    copy.start()
    copy.wait()


def finish(spot, flags, tables, surf, tops, pe, ce, head):
    _, rows, width = surf.shape
    own = head.shape[1]
    block = (rows - SUBS, width - LANES)

    def body(*refs):
        last_kernel(*refs, own=own, own_rows=block[0], own_cols=block[1])

    vmem = pl.BlockSpec(memory_space=pltpu.VMEM)
    smem = pl.BlockSpec(memory_space=pltpu.SMEM)
    return pl.pallas_call(
        body,
        out_shape=(
            jax.ShapeDtypeStruct(head.shape, jnp.float32),
            jax.ShapeDtypeStruct(block, jnp.float32),
        ),
        in_specs=[smem, smem] + [vmem] * 5 + [pl.BlockSpec(memory_space=pl.ANY)],
        out_specs=[pl.BlockSpec(memory_space=pl.ANY), vmem],
        scratch_shapes=[
            pltpu.VMEM((rows, width), jnp.float32),
            pltpu.VMEM((rows, width), jnp.float32),
            pltpu.VMEM((own + SUBS, width), jnp.float32),
            pltpu.VMEM((TOP_LAYERS - 2, own, block[1]), jnp.float32),
            pltpu.SemaphoreType.DMA,
        ]
        + soil_scratch(TOP_LAYERS, own + SUBS, width),
        input_output_aliases={7: 0},
        name="surface_and_top",
    )(spot, flags, tables, surf, tops, pe, ce, head)


def lane_rows(size):
    return -(-size // LANES)


def as_lanes(x):
    if x.shape[-1] % LANES:
        x = jnp.pad(x.reshape(-1), (0, -x.size % LANES))
    return x.reshape(-1, LANES)


def from_lanes(x, shape):
    if shape[-1] % LANES:
        size = 1
        for length in shape:
            size *= length
        x = x.reshape(-1)[:size]
    return x.reshape(shape)


def gx_trade(right, left):
    if lax.axis_size("gx") == 2:
        got = shift(jnp.where(lax.axis_index("gx") == 0, right, left), "gx", 1)
        return got, got
    return shift(right, "gx", 1), shift(left, "gx", -1)


def cyclic_rows(mid, above, below, gap):
    hole = jnp.zeros(mid.shape[:-2] + (gap, mid.shape[-1]), mid.dtype)
    return jnp.concatenate([mid, below, hole, above], axis=-2)


def local(
    pressure, soil_class, capacity_range, inverse_entry, shape_index, conductivity,
    depth, elevation, roughness, rain, land_mask, channel_mask,
):
    ng, nx, ny = (lax.axis_size(a) for a in ("grp", "gx", "gy"))
    ig, ix, iy = (lax.axis_index(a) for a in ("grp", "gx", "gy"))
    layers, own, cols = pressure.shape
    srows, scols = depth.shape
    tables = class_tables(capacity_range, inverse_entry, shape_index, conductivity)
    convey = (1.0 + channel_mask.astype(jnp.float32)) / roughness
    surf = jnp.stack([depth, elevation, convey, LEAKANCE * land_mask.astype(jnp.float32), rain])
    cells = soil_class.astype(jnp.float32)
    tops = jnp.stack([pressure[0], cells[0]])
    both = jnp.stack([pressure, cells])

    def pack(s, t):
        return jnp.concatenate([as_lanes(s), as_lanes(t)], axis=0)

    def unpack(m):
        cut = lane_rows(15 * scols)
        return from_lanes(m[:cut], (5, 3, scols)), from_lanes(m[cut:], (2, 2, cols))

    s_above, t_above = unpack(shift(pack(surf[:, -3:], tops[:, -2:]), "grp", 1))
    s_below, t_below = unpack(shift(pack(surf[:, :3], tops[:, :2]), "grp", -1))
    up = shift(both[:, :, -2:], ("grp", "gy"), 1)
    down = shift(both[:, :, :2], ("grp", "gy"), -1)

    surf_rows = cyclic_rows(surf, s_above, s_below, 2)
    tops_rows = jnp.concatenate([tops, t_below, t_above], axis=1)

    def edges(cut):
        a = surf_rows[:, :, cut(3)].transpose(0, 2, 1).reshape(15, -1)
        b = tops_rows[:, :, cut(2)].transpose(0, 2, 1).reshape(4, -1)
        return a, b

    def pack2(a, b):
        return jnp.concatenate([a, jnp.pad(b, ((0, 0), (0, a.shape[1] - b.shape[1])))], axis=0)

    m_left, m_right = gx_trade(pack2(*edges(lambda n: slice(-n, None))), pack2(*edges(lambda n: slice(0, n))))

    mine = jnp.concatenate(
        [
            as_lanes(surf_rows),
            as_lanes(tops_rows),
            jnp.pad(jnp.concatenate([m_left, m_right]), ((0, 0), (0, -m_left.shape[1] % LANES))).reshape(-1, LANES),
        ]
    )
    every = lax.all_gather(mine, "gy", axis=0, tiled=False)
    n1 = lane_rows(surf_rows.size)
    n2 = n1 + lane_rows(tops_rows.size)
    e_surf = jax.vmap(lambda m: from_lanes(m, (5, srows + SUBS, scols)))(every[:, :n1]).transpose(1, 2, 0, 3).reshape(5, srows + SUBS, ny * scols)
    e_tops = every[:, n1:n2].reshape(ny, 2, own + 4, cols)
    e_m = every[:, n2:].reshape(ny, 2, 19, -1)
    main = e_tops[:, :, :own].transpose(1, 0, 2, 3).reshape(2, srows, cols)
    zeros = jnp.zeros((2, 4, cols), jnp.float32)
    f_tops = jnp.concatenate([main, e_tops[0, :, own : own + 2], zeros, e_tops[-1, :, own + 2 :]], axis=1)

    height = srows + SUBS
    c_left = e_m[-1, 0, :15, :height].reshape(5, 3, height).transpose(0, 2, 1)
    c_right = e_m[0, 1, :15, :height].reshape(5, 3, height).transpose(0, 2, 1)
    hole = jnp.zeros((5, height, LANES - 6), jnp.float32)
    blocks = jnp.concatenate([e_surf, c_right, hole, c_left], axis=2)

    def tops_edge(side):
        t = e_m[:, side, 15:, : own + 4].reshape(ny, 2, 2, own + 4)
        mid = t[..., :own].transpose(1, 0, 3, 2).reshape(2, srows, 2)
        low = t[0, :, :, own : own + 2].transpose(0, 2, 1)
        high = t[-1, :, :, own + 2 :].transpose(0, 2, 1)
        return jnp.concatenate([mid, low, jnp.zeros((2, 4, 2), jnp.float32), high], axis=1)

    top_blocks = jnp.concatenate(
        [f_tops, tops_edge(1), jnp.zeros((2, height, LANES - 4), jnp.float32), tops_edge(0)], axis=2
    )

    soil_rows = cyclic_rows(both, up, down, SUBS - 4)

    def soil_edge(cut):
        a = soil_rows[:, :, :, cut].transpose(0, 3, 2, 1)
        return jnp.pad(a, ((0, 0), (0, 0), (0, 0), (0, LANES - layers)))

    left, right = gx_trade(soil_edge(slice(-2, None)), soil_edge(slice(0, 2)))

    tile = ig * ny + iy
    flags = jnp.stack([tile > 0, tile < ng * ny - 1, ix > 0, ix < nx - 1]).astype(jnp.int32)
    spot = jnp.stack([iy * own, jnp.where(iy > 0, iy * own - SUBS, srows), (ig > 0).astype(jnp.int32), (ig < ng - 1).astype(jnp.int32)])
    head, pe, ce = soil_interior(flags, tables, pressure, soil_class, up, down, left, right)
    head, water = finish(spot, flags, tables, blocks, top_blocks, pe, ce, head)
    return head, lax.dynamic_slice_in_dim(water, iy * scols, scols, axis=1)


def solution(mesh):
    soil = P(None, ("grp", "gy"), "gx")
    ground = P("grp", ("gx", "gy"))
    return jax.shard_map(
        local,
        mesh=mesh,
        in_specs=(soil, soil, P(), P(), P(), P()) + (ground,) * 6,
        out_specs=(soil, ground),
        check_vma=False,
    )
```

time: 138 us -> 80.4 us (0.58); the launches traced: 135 us -> 79.6 us
  starting transfers between devices: 51.5 us -> 9.56 us
  other arithmetic: 48.3 us -> 12.6 us
  waiting for transfers between devices: 27.1 us -> 1 us
  Pallas kernels: 0 us -> 24.6 us
  blocking collectives: 0 us -> 17.5 us
  local copies, waits for them, and re-layouts: 6.96 us -> 13.3 us
    ppermute x12 -> x6, starting transfers between devices: 38.6 us -> 9.56 us  [shift(): return lax.ppermute(x, axis, [(i, (i + step) % size) for i in range(size)])]
    mul x1 -> x0, other arithmetic: 26.2 us -> none  [closures(): conductivity * jnp.sqrt(saturation)]
    pallas_call x0 -> x2, Pallas kernels: none -> 24.6 us  [the longest x1 18.9 us: soil_interior(): pl.pallas_call(soil_kernel, out_shape=(jax.ShapeDtypeStruct(pressure.shap...]
    all_gather x0 -> x1, blocking collectives: none -> 17.5 us  [local(): every = lax.all_gather(mine, 'gy', axis=0, tiled=False)]
    ppermute x12 -> x6, waiting for transfers between devices: 16.6 us -> 1 us  [shift(): return lax.ppermute(x, axis, [(i, (i + step) % size) for i in range(size)])]
    all_to_all x3 -> x0, starting transfers between devices: 12.8 us -> none  [the longest x1 6.35 us: local(): lax.all_to_all(top_conduct, 'gy', split_axis=1, concat_axis=0, tiled=True)]
    all_to_all x3 -> x0, waiting for transfers between devices: 10.5 us -> none  [the longest x1 5.55 us: local(): lax.all_to_all(pressure[0], 'gy', split_axis=1, concat_axis=0, tiled=True)]
    another operation x1 -> x6, other arithmetic: 11.8 us -> 5.46 us  [the longest x3 3.45 us: local(): both = jnp.stack([pressure, cells])]
  transfers between devices with their start and end apart: 15 -> 6, of which waited for: 10 -> 1; matrix products, arithmetic and copies ran while one was open for 4% -> 19% of each run, Pallas kernels for 0% -> 0%
where the time goes in v1:
time: 80.4 us; the launch traced here: 79.6 us
  Pallas kernels  24.6 us (31%)
  blocking collectives  17.5 us (22%)
  local copies, waits for them, and re-layouts  13.3 us (17%)
  other arithmetic  12.6 us (16%)
  starting transfers between devices  9.56 us (12%)
  waiting for transfers between devices  1 us (1%)
  between operations  0.99 us (1%)
    pallas_call x1, Pallas kernels, soil_interior(): pl.pallas_call(soil_kernel, out_shape=(jax.ShapeDtypeStruct(pressure.shap...  18.9 us
    all_gather x1, blocking collectives, local(): every = lax.all_gather(mine, 'gy', axis=0, tiled=False)  17.5 us
    ppermute x6, starting transfers between devices, shift(): return lax.ppermute(x, axis, [(i, (i + step) % size) for i in range(size)])  9.56 us
    pallas_call x1, Pallas kernels, finish(): pl.pallas_call(body, out_shape=(jax.ShapeDtypeStruct(head.shape, jnp.floa...  5.64 us
    another operation x3, other arithmetic, local(): both = jnp.stack([pressure, cells])  3.45 us
    concatenate x2, other arithmetic, cyclic_rows(): return jnp.concatenate([mid, below, hole, above], axis=-2)  3.31 us
    another operation x1, local copies, waits for them, and re-layouts, local(): both = jnp.stack([pressure, cells])  2.76 us
    ppermute x4, local copies, waits for them, and re-layouts, shift(): return lax.ppermute(x, axis, [(i, (i + step) % size) for i in range(size)])  2.73 us
  transfers between devices with their start and end apart: 6, of which 1 were waited for; matrix products, arithmetic and copies ran while one was open for 19% of the time, Pallas kernels for 0%

profile of v1, /device:TPU:0, one launch (start us, length us, event | category | flops | bytes accessed | tf_op | source)
XLA Modules:
  0.0 79.6 jit_solution(7672441524339261106)
XLA Ops:
  0.7 1.1 %convert_bitcast_fusion = (f32[1,24,8,512]{3,2,1,0:T(8,128)S(1)}, f32[24,8,512]{2,1,0:T(8,128)S(1)}) fusion(s32[24,8,512]{2,1,0:T(8,128)} %c_in.1), kind=kLoop, calls=%fused_computation.55 | loop fusion | flops 98304 | bytes 1179648 | tf_op jit(solution)/shard_map/stack | solution.py:342
  1.7 0.7 slice.103
  2.5 0.7 bitcast_dynamic-update-slice_fusion.4
  3.2 0.7 bitcast_dynamic-update-slice_fusion.3
  3.9 0.7 bitcast_dynamic-update-slice_fusion.2
  4.7 0.7 bitcast_dynamic-update-slice_fusion.1
  5.4 0.7 bitcast_dynamic-update-slice_fusion
  6.1 2.5 %collective-permute-start = (f32[31,128]{1,0:T(8,128)S(1)}, f32[31,128]{1,0:T(8,128)S(1)}, u32[]{:S(2)}, u32[]{:S(2)}) collective-permute-start(f32[31,128]{1,0:T(8,128)S(1)} %pad_maximum_fusion.6), channel_id=1, source_target_pairs={{0,24},{8,0},{16,8},{24,16},{1,25},{9,1},{17,9},{25,17},{2,26},{10... | collective-permute-start | bytes 47624 | tf_op jit(solution)/shard_map/ppermute | solution.py:23
  8.7 1.3 %fusion.1 = (f32[2,24,2,512]{3,2,1,0:T(2,128)S(1)}, f32[2,24,2,512]{3,2,1,0:T(2,128)S(1)}) fusion(f32[1,24,8,512]{3,2,1,0:T(8,128)} %bitcast.96, f32[1,24,8,512]{3,2,1,0:T(8,128)S(1)} %get-tuple-element.21), kind=kLoop, calls=%fused_computation.10 | loop fusion | flops 98304 | bytes 1179648 | tf_op jit(solution)/shard_map/stack | solution.py:342
  10.1 4.8 %collective-permute-start.4 = (f32[2,24,2,512]{3,1,2,0:T(8,128)S(1)}, f32[2,24,2,512]{3,1,2,0:T(8,128)S(1)}, u32[]{:S(2)}, u32[]{:S(2)}) collective-permute-start(f32[2,24,2,512]{3,1,2,0:T(8,128)S(1)} %copy.118), channel_id=1, source_target_pairs={{0,27},{1,0},{2,1},{3,2},{8,3},{9,8},{10,9},{11,10},{16,11},{17,16... | collective-permute-start | bytes 589832 | tf_op jit(solution)/shard_map/ppermute | solution.py:23
  15.0 1.1 %pad_maximum_fusion.1 = f32[2,24,8,512]{3,2,1,0:T(8,128)S(1)} fusion(f32[1,24,8,512]{3,2,1,0:T(8,128)S(1)} %get-tuple-element.21, f32[1,24,8,512]{3,2,1,0:T(8,128)} %bitcast.97), kind=kLoop, calls=%fused_computation.3 | loop fusion | flops 196608 | bytes 1572864 | tf_op jit(solution)/shard_map/stack | solution.py:342
  16.1 0.7 add_bitcast_fusion
  16.8 0.7 multiply_bitcast_fusion
  17.5 0.6 add_convert_fusion.flags_ref.refs_1_
  18.9 1.6 %collective-permute-start.2 = (f32[19,40]{1,0:T(8,128)S(1)}, f32[19,40]{1,0:T(8,128)S(1)}, u32[]{:S(2)}, u32[]{:S(2)}) collective-permute-start(f32[19,40]{1,0:T(8,128)S(1)} %fusion.2), channel_id=1, source_target_pairs={{0,4},{4,0},{1,5},{5,1},{2,6},{6,2},{3,7},{7,3},{8,12},{12,8},{9,1... | collective-permute-start | bytes 9128 | tf_op jit(solution)/shard_map/ppermute | solution.py:23
  20.5 0.6 pad_add_fusion.refs_0_
  21.5 2.8 %copy.106 = f32[2,24,8,512]{1,2,3,0:T(8,128)} copy(f32[2,24,8,512]{3,2,1,0:T(8,128)S(1)} %pad_maximum_fusion.1) | data formatting | bytes 1572864 | tf_op jit(solution)/shard_map/stack | solution.py:342
  24.3 0.6 pad.22.tab_ref.refs_2_
  24.9 17.5 %all-gather.1 = f32[4,334,128]{2,1,0:T(8,128)S(1)} all-gather(f32[1,334,128]{2,1,0:T(8,128)S(1)} %maximum_bitcast_fusion), channel_id=2, replica_groups=mesh['grp'=4,'gx'=2,'gy'=4] {'gy'}, dimensions={0}, use_global_device_ids=true | all-gather | bytes 855040 | tf_op jit(solution)/shard_map/all_gather | solution.py:376
  43.8 0.9 %pad_maximum_fusion.2.refs_3_ = f32[5,40,640]{2,1,0:T(8,128)} fusion(f32[5,40,3]{2,1,0:T(8,128)S(1)} %bitcast.102, f32[5,40,3]{2,1,0:T(8,128)S(1)} %bitcast.101, f32[5,40,512]{2,1,0:T(8,128)S(1)} %reshape.82, f32[640]{0:T(1024)S(1)} %pad.51.clone), kind=kLoop, calls=%fused_computation.6 | loop fusion | flops 384000 | bytes 928960 | tf_op jit(solution)/shard_map/concatenate | solution.py:390
  44.7 0.5 copy.107
  45.3 0.5 copy.108
  45.8 3.2 %pad_maximum_fusion = f32[2,24,16,512]{1,2,3,0:T(8,128)S(1)} fusion(f32[2,24,2,512]{1,2,3,0:T(2,128)S(1)} %copy.108, f32[2,24,2,512]{1,2,3,0:T(2,128)S(1)} %copy.107, f32[2,24,8,512]{1,2,3,0:T(8,128)} %copy.106, f32[16]{0:T(128)S(1)} %pad.30.clone), kind=kLoop, calls=%fused_computation | loop fusion | flops 1179648 | bytes 2752576 | tf_op jit(solution)/shard_map/concatenate | solution.py:326
  49.1 0.6 collective-permute-start.5
  49.7 0.8 pad_maximum_fusion.3.refs_4_
  50.4 0.8 %copy.109.up_in = f32[2,24,2,512]{3,2,1,0:T(2,128)} copy(f32[2,24,2,512]{3,1,2,0:T(8,128)S(1)} %collective-permute-done.3) | data formatting | bytes 393216 | tf_op jit(solution)/shard_map/ppermute | solution.py:23
  51.2 0.8 %copy.110.down_in = f32[2,24,2,512]{3,2,1,0:T(2,128)} copy(f32[2,24,2,512]{3,1,2,0:T(8,128)S(1)} %collective-permute-done.4) | data formatting | bytes 393216 | tf_op jit(solution)/shard_map/ppermute | solution.py:23
  52.1 1.0 %collective-permute-done.5.left_in.right_in = f32[2,2,16,128]{3,2,1,0:T(8,128)S(1)} collective-permute-done((f32[2,2,16,128]{3,2,1,0:T(8,128)S(1)}, f32[2,2,16,128]{3,2,1,0:T(8,128)S(1)}, u32[]{:S(2)}, u32[]{:S(2)}) %collective-permute-start.5) | collective-permute-done | bytes 32800 | tf_op jit(solution)/shard_map/ppermute | solution.py:23
  53.1 0.6 copy-done
  53.7 18.9 %soil_interior.1 = (f32[24,8,512]{2,1,0:T(8,128)}, f32[4,16,640]{2,1,0:T(8,128)}, s32[4,16,640]{2,1,0:T(8,128)}) custom-call(s32[4]{0:T(128)} %add_convert_fusion.flags_ref.refs_1_, f32[8,128]{1,0:T(8,128)} %pad.22.tab_ref.refs_2_, f32[24,8,512]{2,1,0:T(8,128)} %p_in.1, s32[24,8,512]{2,1,0:T(8,128)} %c_in.1, f32[2,24,2,512]{3,2,1,0:T(2,128)} %copy.109.up_in, ...), custom_call_target="tpu_custom_call" | custom-call | tf_op jit(solution)/shard_map/soil_interior/pallas_call | solution.py:183
  72.6 5.6 %surface_and_top.1 = (f32[24,8,512]{2,1,0:T(8,128)}, f32[32,512]{1,0:T(8,128)}) custom-call(s32[4]{0:T(128)} %pad_add_fusion.refs_0_, s32[4]{0:T(128)} %add_convert_fusion.flags_ref.refs_1_, f32[8,128]{1,0:T(8,128)} %pad.22.tab_ref.refs_2_, f32[5,40,640]{2,1,0:T(8,128)} %pad_maximum_fusion.2.refs_3_, ...), custom_call_target="tpu_custom_call", output_to_operand_aliasing={{0}: (7, {})} | custom-call | tf_op jit(solution)/shard_map/surface_and_top/pallas_call | solution.py:277
  78.3 1.3 %constant_dynamic-slice_fusion = f32[32,128]{1,0:T(8,128)} fusion(f32[32,512]{1,0:T(8,128)} %get-tuple-element.11, s32[]{:T(128)S(6)} %select_n.28), kind=kLoop, calls=%fused_computation.54 | loop fusion | bytes 32772 | tf_op jit(solution)/shard_map/dynamic_slice | solution.py:416
  (83 shorter events, 2.8 us)
Async XLA Ops:
  0.6 23.6 %copy-start.1 = (f32[12]{0:T(128)S(1)}, f32[12]{0:T(128)}, u32[]{:S(2)}) copy-start(f32[12]{0:T(128)} %param.14) | copy-start | bytes 148
  0.6 23.6 %copy-start.2 = (f32[12]{0:T(128)S(1)}, f32[12]{0:T(128)}, u32[]{:S(2)}) copy-start(f32[12]{0:T(128)} %param.17) | copy-start | bytes 148
  6.1 12.0 %collective-permute-start = (f32[31,128]{1,0:T(8,128)S(1)}, f32[31,128]{1,0:T(8,128)S(1)}, u32[]{:S(2)}, u32[]{:S(2)}) collective-permute-start(f32[31,128]{1,0:T(8,128)S(1)} %pad_maximum_fusion.6), channel_id=1, source_target_pairs={{0,24},{8,0},{16,8},{24,16},{1,25},{9,1},{17,9},{25,17},{2,26},{10... | collective-permute-start | bytes 47624 | tf_op jit(solution)/shard_map/ppermute | solution.py:23
  8.6 9.5 %collective-permute-start.1 = (f32[31,128]{1,0:T(8,128)S(1)}, f32[31,128]{1,0:T(8,128)S(1)}, u32[]{:S(2)}, u32[]{:S(2)}) collective-permute-start(f32[31,128]{1,0:T(8,128)S(1)} %pad_maximum_fusion.7), channel_id=1, source_target_pairs={{0,8},{8,16},{16,24},{24,0},{1,9},{9,17},{17,25},{25,1},{2,10},{10... | collective-permute-start | bytes 47624 | tf_op jit(solution)/shard_map/ppermute | solution.py:23
  10.1 34.6 %collective-permute-start.4 = (f32[2,24,2,512]{3,1,2,0:T(8,128)S(1)}, f32[2,24,2,512]{3,1,2,0:T(8,128)S(1)}, u32[]{:S(2)}, u32[]{:S(2)}) collective-permute-start(f32[2,24,2,512]{3,1,2,0:T(8,128)S(1)} %copy.118), channel_id=1, source_target_pairs={{0,27},{1,0},{2,1},{3,2},{8,3},{9,8},{10,9},{11,10},{16,11},{17,16... | collective-permute-start | bytes 589832 | tf_op jit(solution)/shard_map/ppermute | solution.py:23
  15.0 30.3 %collective-permute-start.3 = (f32[2,24,2,512]{3,1,2,0:T(8,128)S(1)}, f32[2,24,2,512]{3,1,2,0:T(8,128)S(1)}, u32[]{:S(2)}, u32[]{:S(2)}) collective-permute-start(f32[2,24,2,512]{3,1,2,0:T(8,128)S(1)} %copy.117), channel_id=1, source_target_pairs={{0,1},{1,2},{2,3},{3,8},{8,9},{9,10},{10,11},{11,16},{16,17},{17,1... | collective-permute-start | bytes 589832 | tf_op jit(solution)/shard_map/ppermute | solution.py:23
  18.9 6.0 %collective-permute-start.2 = (f32[19,40]{1,0:T(8,128)S(1)}, f32[19,40]{1,0:T(8,128)S(1)}, u32[]{:S(2)}, u32[]{:S(2)}) collective-permute-start(f32[19,40]{1,0:T(8,128)S(1)} %fusion.2), channel_id=1, source_target_pairs={{0,4},{4,0},{1,5},{5,1},{2,6},{6,2},{3,7},{7,3},{8,12},{12,8},{9,1... | collective-permute-start | bytes 9128 | tf_op jit(solution)/shard_map/ppermute | solution.py:23
  49.1 4.0 %collective-permute-start.5 = (f32[2,2,16,128]{3,2,1,0:T(8,128)S(1)}, f32[2,2,16,128]{3,2,1,0:T(8,128)S(1)}, u32[]{:S(2)}, u32[]{:S(2)}) collective-permute-start(f32[2,2,16,128]{3,2,1,0:T(8,128)S(1)} %pad_select_fusion), channel_id=1, source_target_pairs={{0,4},{4,0},{1,5},{5,1},{2,6},{6,2},{3,7},{7,3},{8,12},{12,8},{9,1... | collective-permute-start | bytes 98312 | tf_op jit(solution)/shard_map/ppermute | solution.py:23
  53.1 0.6 copy-start

commit v2 on v1

--- a/solution.py
+++ b/solution.py
@@ -144,11 +144,62 @@
     return [tall, tall, flat, flat, tall, tall, flat, flat, flat]
 
 
-def soil_kernel(flags_ref, tab_ref, p_in, c_in, up_in, down_in, left_in, right_in, out_ref, pe_out, ce_out, pe, ce, mask_ref, *s):
+def soil_pack_kernel(p_ref, c_ref, next_ref, prev_ref):
+    layers, own, _ = p_ref.shape
+    for z in range(layers):
+        next_ref[0, z] = p_ref[z, own - 2 :, :]
+        next_ref[1, z] = c_ref[z, own - 2 :, :].astype(jnp.float32)
+        prev_ref[0, z] = p_ref[z, :2, :]
+        prev_ref[1, z] = c_ref[z, :2, :].astype(jnp.float32)
+
+
+def soil_pack(pressure, soil_class):
+    layers, _, cols = pressure.shape
+    shape = jax.ShapeDtypeStruct((2, layers, 2, cols), jnp.float32)
+    return pl.pallas_call(soil_pack_kernel, out_shape=(shape, shape), name="soil_pack")(pressure, soil_class)
+
+
+def soil_edge_kernel(p_first, c_first, p_last, c_last, up_first, up_last, down_first, down_last, out_ref, box):
+    layers, own, _ = p_first.shape
+    rows = box.shape[1]
+    out = []
+    for side in ((p_last, c_last, up_last, down_last), (p_first, c_first, up_first, down_first)):
+        for f in range(2):
+            for z in range(layers):
+                box[z, :own] = side[f][z].astype(jnp.float32)
+                box[z, own : own + 2] = side[3][f, z]
+                box[z, own + 2 : rows - 2] = jnp.zeros((rows - own - 4, LANES), jnp.float32)
+                box[z, rows - 2 :] = side[2][f, z]
+            turned = box[...].reshape(layers * rows, LANES).T
+            out.append(turned[LANES - 2 :] if len(out) < 2 else turned[:2])
+    out_ref[...] = jnp.concatenate(out, axis=0)
+
+
+def soil_edge(pressure, soil_class, up, down):
+    layers, own, cols = pressure.shape
+    rows = own + SUBS
+    last = cols // LANES - 1
+    tile = [pl.BlockSpec((layers, own, LANES), lambda _, i=i: (0, 0, i)) for i in (0, 0, last, last)]
+    halo = [pl.BlockSpec((2, layers, 2, LANES), lambda _, i=i: (0, 0, 0, i)) for i in (0, last, 0, last)]
+    return pl.pallas_call(
+        soil_edge_kernel,
+        out_shape=jax.ShapeDtypeStruct((8, layers * rows), jnp.float32),
+        grid=(1,),
+        in_specs=tile + halo,
+        scratch_shapes=[pltpu.VMEM((layers, rows, LANES), jnp.float32)],
+        name="soil_edge",
+    )(pressure, soil_class, pressure, soil_class, up, up, down, down)
+
+
+def soil_kernel(flags_ref, tab_ref, p_in, c_in, up_in, down_in, edge_in, out_ref, pe_out, ce_out, pe, ce, mask_ref, turn, *s):
     layers, own, cols = p_in.shape
     _, rows, width = pe.shape
-    lane = lax.broadcasted_iota(jnp.int32, (rows, LANES), 1)
     pad = jnp.zeros((rows - own, cols), jnp.float32)
+    turn[...] = jnp.zeros_like(turn)
+    for f, dst in enumerate((pe, ce)):
+        turn[LANES - 2 :, :] = edge_in[2 * f : 2 * f + 2, :]
+        turn[:2, :] = edge_in[4 + 2 * f : 6 + 2 * f, :]
+        dst[:, :, cols:] = turn[...].T.reshape(layers, rows, LANES).astype(dst.dtype)
 
     def build(z, carry):
         for f, (src, dst) in enumerate(((p_in, pe), (c_in, ce))):
@@ -157,12 +208,6 @@
             dst[z, :own, :cols] = src[z]
             dst[z, own : own + 2, :cols] = down_in[f, z].astype(kind)
             dst[z, rows - 2 :, :cols] = up_in[f, z].astype(kind)
-            edge = jnp.zeros((rows, LANES), jnp.float32)
-            for col in range(2):
-                edge = jnp.where(lane == col, pltpu.roll(right_in[f, col], (LANES + col - z) % LANES, 1), edge)
-                spot = LANES - 2 + col
-                edge = jnp.where(lane == spot, pltpu.roll(left_in[f, col], (LANES + spot - z) % LANES, 1), edge)
-            dst[z, :, cols:] = edge.astype(kind)
         return carry
 
     lax.fori_loop(0, layers, build, 0)
@@ -177,7 +222,7 @@
     ce_out[...] = ce[:TOP_LAYERS]
 
 
-def soil_interior(flags, tables, pressure, soil_class, up, down, left, right):
+def soil_interior(flags, tables, pressure, soil_class, up, down, edge):
     layers, own, cols = pressure.shape
     rows, width = own + SUBS, cols + LANES
     return pl.pallas_call(
@@ -187,23 +232,172 @@
             jax.ShapeDtypeStruct((TOP_LAYERS, rows, width), jnp.float32),
             jax.ShapeDtypeStruct((TOP_LAYERS, rows, width), jnp.int32),
         ),
-        in_specs=[pl.BlockSpec(memory_space=pltpu.SMEM)] + [pl.BlockSpec(memory_space=pltpu.VMEM)] * 7,
+        in_specs=[pl.BlockSpec(memory_space=pltpu.SMEM)] + [pl.BlockSpec(memory_space=pltpu.VMEM)] * 6,
         out_specs=[pl.BlockSpec(memory_space=pltpu.VMEM)] * 3,
         scratch_shapes=[
             pltpu.VMEM((layers, rows, width), jnp.float32),
             pltpu.VMEM((layers, rows, width), jnp.int32),
             pltpu.VMEM((rows, width), jnp.float32),
+            pltpu.VMEM((LANES, layers * rows), jnp.float32),
         ]
         + soil_scratch(layers, rows, width),
         name="soil_interior",
-    )(flags, tables, pressure, soil_class, up, down, left, right)
+    )(flags, tables, pressure, soil_class, up, down, edge)
+
+
+def surface_pack_kernel(p_ref, c_ref, depth, level, rough, rain, land, channel, main_ref, next_ref, prev_ref):
+    height, width = depth.shape
+    _, own, cols = p_ref.shape
+    fields = (
+        depth[...],
+        level[...],
+        (1.0 + channel[...].astype(jnp.float32)) / rough[...],
+        LEAKANCE * land[...].astype(jnp.float32),
+        rain[...],
+    )
+    for f, x in enumerate(fields):
+        main_ref[f * height : (f + 1) * height, :] = x
+        next_ref[3 * f : 3 * f + 3, :] = x[height - 3 :]
+        prev_ref[3 * f : 3 * f + 3, :] = x[:3]
+    base = 5 * height
+    for f, x in enumerate((p_ref[0], c_ref[0].astype(jnp.float32))):
+        for j, ch in enumerate(chunks(cols)):
+            main_ref[base : base + own, :] = x[:, ch]
+            base += own
+            at = EDGE_ROWS + 2 * (f * (cols // LANES) + j)
+            next_ref[at : at + 2, :] = x[own - 2 :, ch]
+            prev_ref[at : at + 2, :] = x[:2, ch]
+
+
+EDGE_ROWS = 16
+
+
+def surface_pack(pressure, soil_class, depth, level, rough, rain, land, channel):
+    _, own, cols = pressure.shape
+    height = depth.shape[0]
+    top = pl.BlockSpec((1, own, cols), lambda _: (0, 0, 0))
+    strip = EDGE_ROWS + 4 * cols // LANES
+    f32 = jnp.float32
+    return pl.pallas_call(
+        surface_pack_kernel,
+        out_shape=(
+            jax.ShapeDtypeStruct((5 * height + 2 * own * cols // LANES, LANES), f32),
+            jax.ShapeDtypeStruct((strip, LANES), f32),
+            jax.ShapeDtypeStruct((strip, LANES), f32),
+        ),
+        grid=(1,),
+        in_specs=[top, top] + [pl.BlockSpec(memory_space=pltpu.VMEM)] * 6,
+        name="surface_pack",
+    )(pressure, soil_class, depth, level, rough, rain, land, channel)
+
+
+def surface_edge_kernel(main_ref, above_ref, below_ref, out_ref, box, *, height, own, cols):
+    n = cols // LANES
+    tall = height + SUBS
+    box[...] = jnp.zeros_like(box)
+    for side, j in enumerate((n - 1, 0)):
+        for f in range(2):
+            at = (2 * side + f) * 2 * SUBS
+            src = 5 * height + (f * n + j) * own
+            strip = EDGE_ROWS + 2 * (f * n + j)
+            box[at : at + own, :] = main_ref[src : src + own, :]
+            box[at + own : at + own + 2, :] = below_ref[strip : strip + 2, :]
+            box[at + own + 2 : at + own + 4, :] = above_ref[strip : strip + 2, :]
+    for f in range(5):
+        at = LANES + f * tall
+        box[at : at + height, :] = main_ref[f * height : (f + 1) * height, :]
+        box[at + height : at + height + 3, :] = below_ref[3 * f : 3 * f + 3, :]
+        box[at + tall - 3 : at + tall, :] = above_ref[3 * f : 3 * f + 3, :]
+    turned = box[...].T
+    edges = jnp.concatenate([turned[LANES - 3 :], turned[:3], jnp.zeros((2, turned.shape[1]), jnp.float32)], axis=0)
+    for j, ch in enumerate(chunks(turned.shape[1])):
+        out_ref[j * SUBS : (j + 1) * SUBS, :] = edges[:, ch]
+
+
+def surface_edge(main, above, below, height, own, cols):
+    wide = LANES + 5 * (height + SUBS)
+    wide += -wide % LANES
+
+    def body(*refs):
+        surface_edge_kernel(*refs, height=height, own=own, cols=cols)
+
+    return pl.pallas_call(
+        body,
+        out_shape=jax.ShapeDtypeStruct((wide // LANES * SUBS, LANES), jnp.float32),
+        scratch_shapes=[pltpu.VMEM((wide, LANES), jnp.float32)],
+        name="surface_edge",
+    )(main, above, below)
+
+
+def assemble(spot_ref, mains, strips, surf_ref, tops_ref, turn, own, height, count):
+    _, rows, width = surf_ref.shape
+    cols = width - LANES
+    n = cols // LANES
+    tall = height + SUBS
+    strip = EDGE_ROWS + 4 * n
+    lane = lax.broadcasted_iota(jnp.int32, (SUBS, LANES), 1)
+    surf_ref[...] = jnp.zeros_like(surf_ref)
+    tops_ref[...] = jnp.zeros_like(tops_ref)
+    turn[...] = jnp.zeros_like(turn)
+    for s in range(count):
+        main, extra = mains[s], strips[s]
+        who = spot_ref[4 + s]
+        at = pl.multiple_of(who * LANES, LANES)
+        first = pl.multiple_of(who * own, own)
+        above, below = 0, strip
+        for f in range(5):
+            surf_ref[f, :height, pl.ds(at, LANES)] = main[f * height : (f + 1) * height, :]
+            surf_ref[f, height : height + 3, pl.ds(at, LANES)] = extra[below + 3 * f : below + 3 * f + 3, :]
+            surf_ref[f, rows - 3 :, pl.ds(at, LANES)] = extra[above + 3 * f : above + 3 * f + 3, :]
+        for f in range(2):
+            for j in range(n):
+                src = 5 * height + (f * n + j) * own
+                tops_ref[f, pl.ds(first, own), j * LANES : (j + 1) * LANES] = main[src : src + own, :]
+        turn[LANES - 3 :, :LANES] = extra[2 * strip : 2 * strip + 3, :]
+        turn[:3, :LANES] = extra[2 * strip + 3 : 2 * strip + 6, :]
+        block = turn[:, :LANES].T
+        for f in range(2):
+            after = block[2 * (2 + f) * SUBS :][: 2 * SUBS]
+            before = block[2 * f * SUBS :][: 2 * SUBS]
+            two = jnp.where(lane >= LANES - 2, before[:SUBS], jnp.where(lane < 2, after[:SUBS], 0.0))
+            more = jnp.where(lane >= LANES - 2, before[SUBS:], jnp.where(lane < 2, after[SUBS:], 0.0))
+            tops_ref[f, pl.ds(first, own), cols:] = two
+
+            @pl.when(who == 0)
+            def _(f=f, more=more, extra=extra):
+                tops_ref[f, height : height + 2, cols:] = more[:2]
+                for j in range(n):
+                    src = below + EDGE_ROWS + 2 * (f * n + j)
+                    tops_ref[f, height : height + 2, j * LANES : (j + 1) * LANES] = extra[src : src + 2, :]
+
+            @pl.when(who == count - 1)
+            def _(f=f, more=more, extra=extra):
+                tops_ref[f, rows - 2 :, cols:] = more[2:4]
+                for j in range(n):
+                    src = above + EDGE_ROWS + 2 * (f * n + j)
+                    tops_ref[f, rows - 2 :, j * LANES : (j + 1) * LANES] = extra[src : src + 2, :]
+
+        @pl.when(who == count - 1)
+        def _(extra=extra):
+            for j in range(1, turn.shape[1] // LANES):
+                src = 2 * strip + j * SUBS
+                turn[LANES - 3 :, j * LANES : (j + 1) * LANES] = extra[src : src + 3, :]
+
+        @pl.when(who == 0)
+        def _(extra=extra):
+            for j in range(1, turn.shape[1] // LANES):
+                src = 2 * strip + j * SUBS
+                turn[:3, j * LANES : (j + 1) * LANES] = extra[src + 3 : src + 6, :]
+
+    block = turn[:, LANES:].T
+    for f in range(5):
+        surf_ref[f, :, cols:] = block[f * tall : (f + 1) * tall]
 
 
 def last_kernel(
-    spot_ref, flags_ref, tab_ref, surf_ref, tops_ref, pe, ce, head_in, head_out, water_ref,
-    ex_ref, w_ref, mask_ref, new_ref, sem, *s, own, own_rows, own_cols,
+    spot_ref, flags_ref, tab_ref, surf_ref, tops_ref, pe, ce, head_out, water_ref,
+    ex_ref, w_ref, mask_ref, new_ref, sem, *s, own,
 ):
-    del head_in
     _, rows, width = surf_ref.shape
     block_rows, block_cols = rows - SUBS, width - LANES
     r = lax.broadcasted_iota(jnp.int32, (rows, width), 0)
@@ -245,7 +439,11 @@
         water = jnp.maximum(water + SURFACE_STEP * (rain - rate - outflow), 0.0)
     ex_ref[...] = exchange
     w_ref[...] = water
-    water_ref[...] = w_ref[:block_rows, :block_cols]
+    if water_ref.shape[1] % LANES:
+        water_ref[...] = w_ref[:block_rows, :block_cols]
+    else:
+        mine = pl.multiple_of(spot_ref[4] * water_ref.shape[1], LANES)
+        water_ref[...] = w_ref[:block_rows, pl.ds(mine, water_ref.shape[1])]
     first = pl.multiple_of(spot_ref[0], SUBS)
     after = pl.multiple_of(spot_ref[0] + own, SUBS)
     before = pl.multiple_of(spot_ref[1], SUBS)
@@ -264,25 +462,43 @@
     copy.wait()
 
 
-def finish(spot, flags, tables, surf, tops, pe, ce, head):
-    _, rows, width = surf.shape
+def finish(spot, flags, tables, fields, pe, ce, head, block, count):
     own = head.shape[1]
-    block = (rows - SUBS, width - LANES)
-
-    def body(*refs):
-        last_kernel(*refs, own=own, own_rows=block[0], own_cols=block[1])
-
+    whole = count == 0
+    rows, width = block[0] + SUBS, block[1] + LANES
+    n = len(fields)
+
+    def body(spot_ref, flags_ref, tab_ref, *refs):
+        given, (pe_ref, ce_ref, _, head_out, water_ref), (box, turn), rest = refs[:n], refs[n : n + 5], refs[n + 5 : n + 7], refs[n + 7 :]
+        if whole:
+            surf, tops = given
+        else:
+            surf, tops = box
+            assemble(spot_ref, given[:count], given[count:], surf, tops, turn, own, block[0], count)
+        last_kernel(spot_ref, flags_ref, tab_ref, surf, tops, pe_ref, ce_ref, head_out, water_ref, *rest, own=own)
+
+    def scratch_body(*refs):
+        cut = 3 + n + 5
+        body(*refs[:cut], refs[cut : cut + 2], refs[cut + 2], *refs[cut + 3 :])
+
+    tall = LANES + 5 * (block[0] + SUBS)
+    tall += -tall % LANES
+    small = (1, SUBS, LANES)
     vmem = pl.BlockSpec(memory_space=pltpu.VMEM)
     smem = pl.BlockSpec(memory_space=pltpu.SMEM)
+    water = block if whole else (block[0], LANES)
     return pl.pallas_call(
-        body,
+        scratch_body,
         out_shape=(
             jax.ShapeDtypeStruct(head.shape, jnp.float32),
-            jax.ShapeDtypeStruct(block, jnp.float32),
+            jax.ShapeDtypeStruct(water, jnp.float32),
         ),
-        in_specs=[smem, smem] + [vmem] * 5 + [pl.BlockSpec(memory_space=pl.ANY)],
+        in_specs=[smem, smem] + [vmem] * (n + 3) + [pl.BlockSpec(memory_space=pl.ANY)],
         out_specs=[pl.BlockSpec(memory_space=pl.ANY), vmem],
         scratch_shapes=[
+            pltpu.VMEM(small if whole else (5, rows, width), jnp.float32),
+            pltpu.VMEM(small if whole else (2, rows, width), jnp.float32),
+            pltpu.VMEM((SUBS, LANES) if whole else (LANES, tall), jnp.float32),
             pltpu.VMEM((rows, width), jnp.float32),
             pltpu.VMEM((rows, width), jnp.float32),
             pltpu.VMEM((own + SUBS, width), jnp.float32),
@@ -290,9 +506,9 @@
             pltpu.SemaphoreType.DMA,
         ]
         + soil_scratch(TOP_LAYERS, own + SUBS, width),
-        input_output_aliases={7: 0},
+        input_output_aliases={n + 5: 0},
         name="surface_and_top",
-    )(spot, flags, tables, surf, tops, pe, ce, head)
+    )(spot, flags, tables, *fields, pe, ce, head)
 
 
 def lane_rows(size):
@@ -314,16 +530,87 @@
     return x.reshape(shape)
 
 
-def gx_trade(right, left):
+def gx_trade(edges, half):
+    got = shift(edges, "gx", 1)
     if lax.axis_size("gx") == 2:
-        got = shift(jnp.where(lax.axis_index("gx") == 0, right, left), "gx", 1)
-        return got, got
-    return shift(right, "gx", 1), shift(left, "gx", -1)
+        return got
+    return jnp.where(half, got, shift(edges, "gx", -1))
 
 
 def cyclic_rows(mid, above, below, gap):
     hole = jnp.zeros(mid.shape[:-2] + (gap, mid.shape[-1]), mid.dtype)
     return jnp.concatenate([mid, below, hole, above], axis=-2)
+
+
+def block_general(pressure, soil_class, depth, elevation, roughness, rain, land_mask, channel_mask):
+    ny = lax.axis_size("gy")
+    _, own, cols = pressure.shape
+    srows, scols = depth.shape
+    convey = (1.0 + channel_mask.astype(jnp.float32)) / roughness
+    surf = jnp.stack([depth, elevation, convey, LEAKANCE * land_mask.astype(jnp.float32), rain])
+    tops = jnp.stack([pressure[0], soil_class[0].astype(jnp.float32)])
+
+    def pack(s, t):
+        return jnp.concatenate([as_lanes(s), as_lanes(t)], axis=0)
+
+    def unpack(m):
+        cut = lane_rows(15 * scols)
+        return from_lanes(m[:cut], (5, 3, scols)), from_lanes(m[cut:], (2, 2, cols))
+
+    s_above, t_above = unpack(shift(pack(surf[:, -3:], tops[:, -2:]), "grp", 1))
+    s_below, t_below = unpack(shift(pack(surf[:, :3], tops[:, :2]), "grp", -1))
+    surf_rows = cyclic_rows(surf, s_above, s_below, 2)
+    tops_rows = jnp.concatenate([tops, t_below, t_above], axis=1)
+
+    def edges(cut):
+        a = surf_rows[:, :, cut(3)].transpose(0, 2, 1).reshape(15, -1)
+        b = tops_rows[:, :, cut(2)].transpose(0, 2, 1).reshape(4, -1)
+        return jnp.concatenate([a, jnp.pad(b, ((0, 0), (0, a.shape[1] - b.shape[1])))], axis=0)
+
+    out = jnp.concatenate([edges(lambda n: slice(-n, None)), edges(lambda n: slice(0, n))])
+    got = gx_trade(out, lax.broadcasted_iota(jnp.int32, out.shape, 0) < 19)
+    mine = jnp.concatenate(
+        [as_lanes(surf_rows), as_lanes(tops_rows), jnp.pad(got, ((0, 0), (0, -got.shape[1] % LANES))).reshape(-1, LANES)]
+    )
+    every = lax.all_gather(mine, "gy", axis=0, tiled=False)
+    n1 = lane_rows(surf_rows.size)
+    n2 = n1 + lane_rows(tops_rows.size)
+    e_surf = jax.vmap(lambda m: from_lanes(m, (5, srows + SUBS, scols)))(every[:, :n1])
+    e_surf = e_surf.transpose(1, 2, 0, 3).reshape(5, srows + SUBS, ny * scols)
+    e_tops = every[:, n1:n2].reshape(ny, 2, own + 4, cols)
+    e_m = every[:, n2:].reshape(ny, 2, 19, -1)
+    main = e_tops[:, :, :own].transpose(1, 0, 2, 3).reshape(2, srows, cols)
+    zeros = jnp.zeros((2, 4, cols), jnp.float32)
+    f_tops = jnp.concatenate([main, e_tops[0, :, own : own + 2], zeros, e_tops[-1, :, own + 2 :]], axis=1)
+    height = srows + SUBS
+    c_left = e_m[-1, 0, :15, :height].reshape(5, 3, height).transpose(0, 2, 1)
+    c_right = e_m[0, 1, :15, :height].reshape(5, 3, height).transpose(0, 2, 1)
+    hole = jnp.zeros((5, height, LANES - 6), jnp.float32)
+    blocks = jnp.concatenate([e_surf, c_right, hole, c_left], axis=2)
+
+    def tops_edge(side):
+        t = e_m[:, side, 15:, : own + 4].reshape(ny, 2, 2, own + 4)
+        mid = t[..., :own].transpose(1, 0, 3, 2).reshape(2, srows, 2)
+        low = t[0, :, :, own : own + 2].transpose(0, 2, 1)
+        high = t[-1, :, :, own + 2 :].transpose(0, 2, 1)
+        return jnp.concatenate([mid, low, jnp.zeros((2, 4, 2), jnp.float32), high], axis=1)
+
+    return blocks, jnp.concatenate(
+        [f_tops, tops_edge(1), jnp.zeros((2, height, LANES - 4), jnp.float32), tops_edge(0)], axis=2
+    )
+
+
+def block_parts(pressure, soil_class, depth, elevation, roughness, rain, land_mask, channel_mask):
+    ny = lax.axis_size("gy")
+    _, own, cols = pressure.shape
+    main, after, before = surface_pack(pressure, soil_class, depth, elevation, roughness, rain, land_mask, channel_mask)
+    above = shift(after, "grp", 1)
+    below = shift(before, "grp", -1)
+    mains = [main] + [shift(main, "gy", step) for step in range(1, ny)]
+    edge = surface_edge(main, above, below, depth.shape[0], own, cols)
+    edge = gx_trade(edge, lax.broadcasted_iota(jnp.int32, edge.shape, 0) % SUBS < 3)
+    strip = jnp.concatenate([above, below, edge], axis=0)
+    return mains + [strip] + [shift(strip, "gy", step) for step in range(1, ny)]
 
 
 def local(
@@ -332,88 +619,31 @@
 ):
     ng, nx, ny = (lax.axis_size(a) for a in ("grp", "gx", "gy"))
     ig, ix, iy = (lax.axis_index(a) for a in ("grp", "gx", "gy"))
-    layers, own, cols = pressure.shape
+    _, own, cols = pressure.shape
     srows, scols = depth.shape
+    ground = (depth, elevation, roughness, rain, land_mask, channel_mask)
     tables = class_tables(capacity_range, inverse_entry, shape_index, conductivity)
-    convey = (1.0 + channel_mask.astype(jnp.float32)) / roughness
-    surf = jnp.stack([depth, elevation, convey, LEAKANCE * land_mask.astype(jnp.float32), rain])
-    cells = soil_class.astype(jnp.float32)
-    tops = jnp.stack([pressure[0], cells[0]])
-    both = jnp.stack([pressure, cells])
-
-    def pack(s, t):
-        return jnp.concatenate([as_lanes(s), as_lanes(t)], axis=0)
-
-    def unpack(m):
-        cut = lane_rows(15 * scols)
-        return from_lanes(m[:cut], (5, 3, scols)), from_lanes(m[cut:], (2, 2, cols))
-
-    s_above, t_above = unpack(shift(pack(surf[:, -3:], tops[:, -2:]), "grp", 1))
-    s_below, t_below = unpack(shift(pack(surf[:, :3], tops[:, :2]), "grp", -1))
-    up = shift(both[:, :, -2:], ("grp", "gy"), 1)
-    down = shift(both[:, :, :2], ("grp", "gy"), -1)
-
-    surf_rows = cyclic_rows(surf, s_above, s_below, 2)
-    tops_rows = jnp.concatenate([tops, t_below, t_above], axis=1)
-
-    def edges(cut):
-        a = surf_rows[:, :, cut(3)].transpose(0, 2, 1).reshape(15, -1)
-        b = tops_rows[:, :, cut(2)].transpose(0, 2, 1).reshape(4, -1)
-        return a, b
-
-    def pack2(a, b):
-        return jnp.concatenate([a, jnp.pad(b, ((0, 0), (0, a.shape[1] - b.shape[1])))], axis=0)
-
-    m_left, m_right = gx_trade(pack2(*edges(lambda n: slice(-n, None))), pack2(*edges(lambda n: slice(0, n))))
-
-    mine = jnp.concatenate(
-        [
-            as_lanes(surf_rows),
-            as_lanes(tops_rows),
-            jnp.pad(jnp.concatenate([m_left, m_right]), ((0, 0), (0, -m_left.shape[1] % LANES))).reshape(-1, LANES),
-        ]
-    )
-    every = lax.all_gather(mine, "gy", axis=0, tiled=False)
-    n1 = lane_rows(surf_rows.size)
-    n2 = n1 + lane_rows(tops_rows.size)
-    e_surf = jax.vmap(lambda m: from_lanes(m, (5, srows + SUBS, scols)))(every[:, :n1]).transpose(1, 2, 0, 3).reshape(5, srows + SUBS, ny * scols)
-    e_tops = every[:, n1:n2].reshape(ny, 2, own + 4, cols)
-    e_m = every[:, n2:].reshape(ny, 2, 19, -1)
-    main = e_tops[:, :, :own].transpose(1, 0, 2, 3).reshape(2, srows, cols)
-    zeros = jnp.zeros((2, 4, cols), jnp.float32)
-    f_tops = jnp.concatenate([main, e_tops[0, :, own : own + 2], zeros, e_tops[-1, :, own + 2 :]], axis=1)
-
-    height = srows + SUBS
-    c_left = e_m[-1, 0, :15, :height].reshape(5, 3, height).transpose(0, 2, 1)
-    c_right = e_m[0, 1, :15, :height].reshape(5, 3, height).transpose(0, 2, 1)
-    hole = jnp.zeros((5, height, LANES - 6), jnp.float32)
-    blocks = jnp.concatenate([e_surf, c_right, hole, c_left], axis=2)
-
-    def tops_edge(side):
-        t = e_m[:, side, 15:, : own + 4].reshape(ny, 2, 2, own + 4)
-        mid = t[..., :own].transpose(1, 0, 3, 2).reshape(2, srows, 2)
-        low = t[0, :, :, own : own + 2].transpose(0, 2, 1)
-        high = t[-1, :, :, own + 2 :].transpose(0, 2, 1)
-        return jnp.concatenate([mid, low, jnp.zeros((2, 4, 2), jnp.float32), high], axis=1)
-
-    top_blocks = jnp.concatenate(
-        [f_tops, tops_edge(1), jnp.zeros((2, height, LANES - 4), jnp.float32), tops_edge(0)], axis=2
-    )
-
-    soil_rows = cyclic_rows(both, up, down, SUBS - 4)
-
-    def soil_edge(cut):
-        a = soil_rows[:, :, :, cut].transpose(0, 3, 2, 1)
-        return jnp.pad(a, ((0, 0), (0, 0), (0, 0), (0, LANES - layers)))
-
-    left, right = gx_trade(soil_edge(slice(-2, None)), soil_edge(slice(0, 2)))
-
     tile = ig * ny + iy
     flags = jnp.stack([tile > 0, tile < ng * ny - 1, ix > 0, ix < nx - 1]).astype(jnp.int32)
-    spot = jnp.stack([iy * own, jnp.where(iy > 0, iy * own - SUBS, srows), (ig > 0).astype(jnp.int32), (ig < ng - 1).astype(jnp.int32)])
-    head, pe, ce = soil_interior(flags, tables, pressure, soil_class, up, down, left, right)
-    head, water = finish(spot, flags, tables, blocks, top_blocks, pe, ce, head)
-    return head, lax.dynamic_slice_in_dim(water, iy * scols, scols, axis=1)
+    spot = [iy * own, jnp.where(iy > 0, iy * own - SUBS, srows), (ig > 0).astype(jnp.int32), (ig < ng - 1).astype(jnp.int32)]
+    spot = jnp.stack(spot + [(iy - step) % ny for step in range(ny)])
+
+    even = scols == LANES and own == SUBS
+    if even:
+        fields = block_parts(pressure, soil_class, *ground)
+    else:
+        fields = block_general(pressure, soil_class, *ground)
+
+    after, before = soil_pack(pressure, soil_class)
+    up = shift(after, ("grp", "gy"), 1)
+    down = shift(before, ("grp", "gy"), -1)
+    edge = soil_edge(pressure, soil_class, up, down)
+    edge = gx_trade(edge, lax.broadcasted_iota(jnp.int32, edge.shape, 0) < 4)
+    head, pe, ce = soil_interior(flags, tables, pressure, soil_class, up, down, edge)
+    head, water = finish(spot, flags, tables, fields, pe, ce, head, (srows, cols), ny if even else 0)
+    if not even:
+        water = lax.dynamic_slice_in_dim(water, iy * scols, scols, axis=1)
+    return head, water
 
 
 def solution(mesh):

time: 80.4 us -> 60.1 us (0.75)
  blocking collectives: 17.5 us -> 0 us
  other arithmetic: 12.6 us -> 0.63 us
  starting transfers between devices: 9.56 us -> 20.4 us
  local copies, waits for them, and re-layouts: 13.3 us -> 4.7 us
  Pallas kernels: 24.6 us -> 30.3 us
  waiting for transfers between devices: 1 us -> 2.78 us
    all_gather x1 -> x0, blocking collectives: 17.5 us -> none  [local(): every = lax.all_gather(mine, 'gy', axis=0, tiled=False)]
    ppermute x6 -> x12, starting transfers between devices: 9.56 us -> 20.4 us  [shift(): return lax.ppermute(x, axis, [(i, (i + step) % size) for i in range(size)])]
    pallas_call x1 -> x5, Pallas kernels: 5.64 us -> 13.2 us  [the longest x1 6.21 us: finish(): pl.pallas_call(scratch_body, out_shape=(jax.ShapeDtypeStruct(head.shape,...]
    concatenate x9 -> x0, other arithmetic: 5.1 us -> none  [the longest x2 3.31 us: cyclic_rows(): return jnp.concatenate([mid, below, hole, above], axis=-2)]
    another operation x4 -> x0, other arithmetic: 4.09 us -> none  [the longest x3 3.45 us: local(): both = jnp.stack([pressure, cells])]
    another operation x7 -> x1, local copies, waits for them, and re-layouts: 3.73 us -> 0.67 us  [local(): spot = jnp.stack(spot + [(iy - step) % ny for step in range(ny)])]
    ppermute x4 -> x0, local copies, waits for them, and re-layouts: 2.73 us -> none  [shift(): return lax.ppermute(x, axis, [(i, (i + step) % size) for i in range(size)])]
    pallas_call x1, Pallas kernels: 18.9 us -> 17.1 us  [soil_interior(): pl.pallas_call(soil_kernel, out_shape=(jax.ShapeDtypeStruct(pressure.shap...]
  transfers between devices with their start and end apart: 6 -> 12, of which waited for: 1 -> 2; matrix products, arithmetic and copies ran while one was open for 19% -> 4% of each run, Pallas kernels for 0% -> 38%
where the time goes in v2:
time: 60.1 us; the launch traced here: 59.6 us
  Pallas kernels  30.3 us (50%)
  starting transfers between devices  20.4 us (34%)
  local copies, waits for them, and re-layouts  4.7 us (8%)
  waiting for transfers between devices  2.78 us (5%)
  between operations  0.81 us (1%)
  other arithmetic  0.63 us (1%)
    ppermute x12, starting transfers between devices, shift(): return lax.ppermute(x, axis, [(i, (i + step) % size) for i in range(size)])  20.4 us
    pallas_call x1, Pallas kernels, soil_interior(): pl.pallas_call(soil_kernel, out_shape=(jax.ShapeDtypeStruct(pressure.shap...  17.1 us
    pallas_call x1, Pallas kernels, finish(): pl.pallas_call(scratch_body, out_shape=(jax.ShapeDtypeStruct(head.shape,...  6.21 us
    unnamed x38, local copies, waits for them, and re-layouts  3.4 us
    ppermute x12, waiting for transfers between devices, shift(): return lax.ppermute(x, axis, [(i, (i + step) % size) for i in range(size)])  2.78 us
    pallas_call x1, Pallas kernels, soil_edge(): pl.pallas_call(soil_edge_kernel, out_shape=jax.ShapeDtypeStruct((8, layer...  1.96 us
    pallas_call x1, Pallas kernels, soil_pack(): pl.pallas_call(soil_pack_kernel, out_shape=(shape, shape), name='soil_pack')  1.93 us
    pallas_call x1, Pallas kernels, surface_edge(): pl.pallas_call(body, out_shape=jax.ShapeDtypeStruct((wide // LANES * SUBS...  1.66 us
  transfers between devices with their start and end apart: 12, of which 2 were waited for; matrix products, arithmetic and copies ran while one was open for 4% of the time, Pallas kernels for 38%

profile of v2, /device:TPU:0, one launch (start us, length us, event | category | flops | bytes accessed | tf_op | source)
XLA Modules:
  0.0 59.6 jit_solution(13512564846529329411)
XLA Ops:
  0.6 1.5 %surface_pack.1 = (f32[224,128]{1,0:T(8,128)}, f32[32,128]{1,0:T(8,128)}, f32[32,128]{1,0:T(8,128)}) custom-call(f32[24,8,512]{2,1,0:T(8,128)} %p_in.1, s32[24,8,512]{2,1,0:T(8,128)} %c_in.1, f32[32,128]{1,0:T(8,128)} %depth.1, f32[32,128]{1,0:T(8,128)} %level.1, f32[32,128]{1,0:T(8,128)} %rough.1, f32[32,128]{1,0:T(8,128)} %rain.1, s32[32,128]{1,0:T(8,128)} %land.1, ...), custom_call_target="tpu_custom_call" | custom-call | tf_op jit(solution)/shard_map/surface_pack/pallas_call | solution.py:281
  2.1 5.1 %collective-permute-start.2 = (f32[224,128]{1,0:T(8,128)}, f32[224,128]{1,0:T(8,128)S(1)}, u32[]{:S(2)}, u32[]{:S(2)}) collective-permute-start(f32[224,128]{1,0:T(8,128)} %get-tuple-element.10.refs_0_.refs_3_), channel_id=1, source_target_pairs={{0,3},{1,0},{2,1},{3,2},{4,7},{5,4},{6,5},{7,6},{8,11},{9,8},{10,9... | collective-permute-start | bytes 344072 | tf_op jit(solution)/shard_map/ppermute | solution.py:23
  7.2 1.7 %collective-permute-start.4 = (f32[32,128]{1,0:T(8,128)}, f32[32,128]{1,0:T(8,128)S(1)}, u32[]{:S(2)}, u32[]{:S(2)}) collective-permute-start(f32[32,128]{1,0:T(8,128)} %get-tuple-element.12), channel_id=1, source_target_pairs={{0,24},{8,0},{16,8},{24,16},{1,25},{9,1},{17,9},{25,17},{2,26},{10... | collective-permute-start | bytes 49160 | tf_op jit(solution)/shard_map/ppermute | solution.py:23
  9.0 1.9 %soil_pack.1 = (f32[2,24,2,512]{3,2,1,0:T(2,128)}, f32[2,24,2,512]{3,2,1,0:T(2,128)}) custom-call(f32[24,8,512]{2,1,0:T(8,128)} %p_in.1, s32[24,8,512]{2,1,0:T(8,128)} %c_in.1), custom_call_target="tpu_custom_call" | custom-call | tf_op jit(solution)/shard_map/soil_pack/pallas_call | solution.py:159
  10.9 1.0 %collective-permute-start.9 = (f32[2,24,2,512]{3,2,1,0:T(2,128)}, f32[2,24,2,512]{3,2,1,0:T(2,128)S(1)}, u32[]{:S(2)}, u32[]{:S(2)}) collective-permute-start(f32[2,24,2,512]{3,2,1,0:T(2,128)} %get-tuple-element.13), channel_id=1, source_target_pairs={{0,1},{1,2},{2,3},{3,8},{8,9},{9,10},{10,11},{11,16},{16,17},{17,1... | collective-permute-start | bytes 589832 | tf_op jit(solution)/shard_map/ppermute | solution.py:23
  11.9 0.0 copy-start.7
  11.9 3.5 %collective-permute-start.10 = (f32[2,24,2,512]{3,2,1,0:T(2,128)}, f32[2,24,2,512]{3,2,1,0:T(2,128)S(1)}, u32[]{:S(2)}, u32[]{:S(2)}) collective-permute-start(f32[2,24,2,512]{3,2,1,0:T(2,128)} %get-tuple-element.14), channel_id=1, source_target_pairs={{0,27},{1,0},{2,1},{3,2},{8,3},{9,8},{10,9},{11,10},{16,11},{17,16... | collective-permute-start | bytes 589832 | tf_op jit(solution)/shard_map/ppermute | solution.py:23
  15.4 0.6 %copy-done.8 = f32[32,128]{1,0:T(8,128)} copy-done((f32[32,128]{1,0:T(8,128)}, f32[32,128]{1,0:T(8,128)S(1)}, u32[]{:S(2)}) %copy-start.8) | copy-done | bytes 16408
  16.0 1.7 %surface_edge.1 = f32[24,128]{1,0:T(8,128)} custom-call(f32[224,128]{1,0:T(8,128)} %get-tuple-element.10.refs_0_.refs_3_, f32[32,128]{1,0:T(8,128)} %copy-done.7, f32[32,128]{1,0:T(8,128)} %copy-done.8), custom_call_target="tpu_custom_call" | custom-call | tf_op jit(solution)/shard_map/surface_edge/pallas_call | solution.py:324
  17.7 1.5 %collective-permute-start.5 = (f32[24,128]{1,0:T(8,128)}, f32[24,128]{1,0:T(8,128)S(1)}, u32[]{:S(2)}, u32[]{:S(2)}) collective-permute-start(f32[24,128]{1,0:T(8,128)} %surface_edge.1), channel_id=1, source_target_pairs={{0,4},{4,0},{1,5},{5,1},{2,6},{6,2},{3,7},{7,3},{8,12},{12,8},{9,1... | collective-permute-start | bytes 36872 | tf_op jit(solution)/shard_map/ppermute | solution.py:23
  19.2 0.7 %constant_dynamic-update-slice_fusion.2 = f32[88,128]{1,0:T(8,128)S(1)} fusion(f32[32,128]{1,0:T(8,128)} %copy-done.7), kind=kLoop, calls=%fused_computation.2 | loop fusion | bytes 32768
  19.9 1.7 %collective-permute-done.5 = f32[24,128]{1,0:T(8,128)S(1)} collective-permute-done((f32[24,128]{1,0:T(8,128)}, f32[24,128]{1,0:T(8,128)S(1)}, u32[]{:S(2)}, u32[]{:S(2)}) %collective-permute-start.5) | collective-permute-done | bytes 12320 | tf_op jit(solution)/shard_map/ppermute | solution.py:23
  21.6 5.2 %collective-permute-start.8 = (f32[88,128]{1,0:T(8,128)S(1)}, f32[88,128]{1,0:T(8,128)S(1)}, u32[]{:S(2)}, u32[]{:S(2)}) collective-permute-start(f32[88,128]{1,0:T(8,128)S(1)} %constant_dynamic-update-slice_fusion.refs_7_), channel_id=1, source_target_pairs={{0,3},{1,0},{2,1},{3,2},{4,7},{5,4},{6,5},{7,6},{8,11},{9,8},{10,9... | collective-permute-start | bytes 135176 | tf_op jit(solution)/shard_map/ppermute | solution.py:23
  26.8 0.7 %copy-done.1 = f32[2,24,2,512]{3,2,1,0:T(2,128)} copy-done((f32[2,24,2,512]{3,2,1,0:T(2,128)}, f32[2,24,2,512]{3,2,1,0:T(2,128)S(1)}, u32[]{:S(2)}) %copy-start.1) | copy-done | bytes 196632
  27.5 2.0 %soil_edge.1 = f32[8,384]{1,0:T(8,128)} custom-call(f32[24,8,512]{2,1,0:T(8,128)} %p_in.1, s32[24,8,512]{2,1,0:T(8,128)} %c_in.1, f32[24,8,512]{2,1,0:T(8,128)} %p_in.1, s32[24,8,512]{2,1,0:T(8,128)} %c_in.1, f32[2,24,2,512]{3,2,1,0:T(2,128)} %copy-done, f32[2,24,2,512]{3,2,1,0:T(2,128)} %copy-done, f32[2,24,2,512]{3,2,1,0:T(2,128)} %copy-done.1, ...), custom_call_target="tpu_custom_call" | custom-call | tf_op jit(solution)/shard_map/soil_edge/pallas_call | solution.py:184
  29.5 1.5 %collective-permute-start.11 = (f32[8,384]{1,0:T(8,128)}, f32[8,384]{1,0:T(8,128)S(1)}, u32[]{:S(2)}, u32[]{:S(2)}) collective-permute-start(f32[8,384]{1,0:T(8,128)} %soil_edge.1), channel_id=1, source_target_pairs={{0,4},{4,0},{1,5},{5,1},{2,6},{6,2},{3,7},{7,3},{8,12},{12,8},{9,1... | collective-permute-start | bytes 36872 | tf_op jit(solution)/shard_map/ppermute | solution.py:23
  31.0 0.6 %copy-done.14 = f32[12]{0:T(128)S(1)} copy-done((f32[12]{0:T(128)S(1)}, f32[12]{0:T(128)}, u32[]{:S(2)}) %copy-start.14) | copy-done | bytes 72
  31.6 0.0 copy-done.15
  31.6 0.0 copy-done.17
  31.7 0.6 collective-permute-start.7
  32.3 1.1 %collective-permute-done.11.edge_in = f32[8,384]{1,0:T(8,128)S(1)} collective-permute-done((f32[8,384]{1,0:T(8,128)}, f32[8,384]{1,0:T(8,128)S(1)}, u32[]{:S(2)}, u32[]{:S(2)}) %collective-permute-start.11) | collective-permute-done | bytes 12320 | tf_op jit(solution)/shard_map/ppermute | solution.py:23
  33.4 0.3 collective-permute-start.6
  33.7 0.6 %add_convert_fusion.flags_ref.refs_1_ = s32[4]{0:T(128)} fusion(pred[1]{0:T(512)(128)(4,1)} %bitcast.11, pred[1]{0:T(512)(128)(4,1)} %bitcast.10, pred[1]{0:T(512)(128)(4,1)} %bitcast.9, pred[1]{0:T(512)(128)(4,1)} %bitcast.8), kind=kLoop, calls=%fused_computation.3 | loop fusion | flops 16 | bytes 20 | tf_op jit(solution)/shard_map/convert_element_type | solution.py:627
  34.3 0.6 %pad.4.tab_ref.refs_2_ = f32[8,128]{1,0:T(8,128)} pad(f32[8,12]{1,0:T(8,128)S(1)} %stack.99, f32[]{:T(128)} %constant.63.clone.1), padding=0_0x0_116 | pad | bytes 4484 | tf_op jit(solution)/shard_map/jit(_pad)/pad | solution.py:39
  34.9 0.7 %stack.85.refs_0_ = s32[8]{0:T(128)} concatenate(s32[1]{0:T(128)} %bitcast, s32[1]{0:T(128)} %bitcast.1, s32[1]{0:T(128)} %bitcast.2, s32[1]{0:T(128)} %bitcast.3, s32[1]{0:T(128)} %bitcast.4, s32[1]{0:T(128)} %bitcast.5, s32[1]{0:T(128)} %bitcast.6, s32[1]{0:T(128)} %bitcast.7), dimensions={0} | concatenate | bytes 64 | tf_op jit(solution)/shard_map/stack | solution.py:629
  35.6 17.1 %soil_interior.1 = (f32[24,8,512]{2,1,0:T(8,128)}, f32[4,16,640]{2,1,0:T(8,128)}, s32[4,16,640]{2,1,0:T(8,128)}) custom-call(s32[4]{0:T(128)} %add_convert_fusion.flags_ref.refs_1_, f32[8,128]{1,0:T(8,128)} %pad.4.tab_ref.refs_2_, f32[24,8,512]{2,1,0:T(8,128)} %p_in.1, s32[24,8,512]{2,1,0:T(8,128)} %c_in.1, f32[2,24,2,512]{3,2,1,0:T(2,128)} %copy-done, ...), custom_call_target="tpu_custom_call" | custom-call | tf_op jit(solution)/shard_map/soil_interior/pallas_call | solution.py:228
  52.8 0.5 copy-done.11
  53.3 0.0 copy-done.12
  53.3 0.0 copy-done.3
  53.4 0.0 copy-done.4
  53.4 0.0 copy-done.5
  53.4 6.2 %surface_and_top.1 = (f32[24,8,512]{2,1,0:T(8,128)}, f32[32,128]{1,0:T(8,128)}) custom-call(s32[8]{0:T(128)} %stack.85.refs_0_, s32[4]{0:T(128)} %add_convert_fusion.flags_ref.refs_1_, f32[8,128]{1,0:T(8,128)} %pad.4.tab_ref.refs_2_, f32[224,128]{1,0:T(8,128)} %get-tuple-element.10.refs_0_.refs_3_, ...), custom_call_target="tpu_custom_call", output_to_operand_aliasing={{0}: (13, {})} | custom-call | tf_op jit(solution)/shard_map/surface_and_top/pallas_call | solution.py:490
  (43 shorter events, 0.1 us)
Async XLA Ops:
  2.1 50.6 %collective-permute-start.2 = (f32[224,128]{1,0:T(8,128)}, f32[224,128]{1,0:T(8,128)S(1)}, u32[]{:S(2)}, u32[]{:S(2)}) collective-permute-start(f32[224,128]{1,0:T(8,128)} %get-tuple-element.10.refs_0_.refs_3_), channel_id=1, source_target_pairs={{0,3},{1,0},{2,1},{3,2},{4,7},{5,4},{6,5},{7,6},{8,11},{9,8},{10,9... | collective-permute-start | bytes 344072 | tf_op jit(solution)/shard_map/ppermute | solution.py:23
  7.2 45.5 %collective-permute-start.1 = (f32[224,128]{1,0:T(8,128)}, f32[224,128]{1,0:T(8,128)S(1)}, u32[]{:S(2)}, u32[]{:S(2)}) collective-permute-start(f32[224,128]{1,0:T(8,128)} %get-tuple-element.10.refs_0_.refs_3_), channel_id=1, source_target_pairs={{0,2},{1,3},{2,0},{3,1},{4,6},{5,7},{6,4},{7,5},{8,10},{9,11},{10,... | collective-permute-start | bytes 344072 | tf_op jit(solution)/shard_map/ppermute | solution.py:23
  7.2 4.7 %collective-permute-start.3 = (f32[32,128]{1,0:T(8,128)}, f32[32,128]{1,0:T(8,128)S(1)}, u32[]{:S(2)}, u32[]{:S(2)}) collective-permute-start(f32[32,128]{1,0:T(8,128)} %get-tuple-element.11), channel_id=1, source_target_pairs={{0,8},{8,16},{16,24},{24,0},{1,9},{9,17},{17,25},{25,1},{2,10},{10... | collective-permute-start | bytes 49160 | tf_op jit(solution)/shard_map/ppermute | solution.py:23
  7.2 8.2 %collective-permute-start.4 = (f32[32,128]{1,0:T(8,128)}, f32[32,128]{1,0:T(8,128)S(1)}, u32[]{:S(2)}, u32[]{:S(2)}) collective-permute-start(f32[32,128]{1,0:T(8,128)} %get-tuple-element.12), channel_id=1, source_target_pairs={{0,24},{8,0},{16,8},{24,16},{1,25},{9,1},{17,9},{25,17},{2,26},{10... | collective-permute-start | bytes 49160 | tf_op jit(solution)/shard_map/ppermute | solution.py:23
  10.9 1.0 %copy-start.16 = (f32[12]{0:T(128)S(1)}, f32[12]{0:T(128)}, u32[]{:S(2)}) copy-start(f32[12]{0:T(128)} %param.16) | copy-start | bytes 148
  10.9 10.7 %copy-start.2 = (f32[224,128]{1,0:T(8,128)S(1)}, f32[224,128]{1,0:T(8,128)}, u32[]{:S(2)}) copy-start(f32[224,128]{1,0:T(8,128)} %get-tuple-element.10.refs_0_.refs_3_) | copy-start | bytes 344068
  10.9 10.7 %collective-permute-start.9 = (f32[2,24,2,512]{3,2,1,0:T(2,128)}, f32[2,24,2,512]{3,2,1,0:T(2,128)S(1)}, u32[]{:S(2)}, u32[]{:S(2)}) collective-permute-start(f32[2,24,2,512]{3,2,1,0:T(2,128)} %get-tuple-element.13), channel_id=1, source_target_pairs={{0,1},{1,2},{2,3},{3,8},{8,9},{9,10},{10,11},{11,16},{16,17},{17,1... | collective-permute-start | bytes 589832 | tf_op jit(solution)/shard_map/ppermute | solution.py:23
  11.9 3.5 %copy-start.7 = (f32[32,128]{1,0:T(8,128)}, f32[32,128]{1,0:T(8,128)S(1)}, u32[]{:S(2)}) copy-start(f32[32,128]{1,0:T(8,128)S(1)} %collective-permute-done.3.refs_1_) | copy-start | bytes 49156
  11.9 14.9 %collective-permute-start.10 = (f32[2,24,2,512]{3,2,1,0:T(2,128)}, f32[2,24,2,512]{3,2,1,0:T(2,128)S(1)}, u32[]{:S(2)}, u32[]{:S(2)}) collective-permute-start(f32[2,24,2,512]{3,2,1,0:T(2,128)} %get-tuple-element.14), channel_id=1, source_target_pairs={{0,27},{1,0},{2,1},{3,2},{8,3},{9,8},{10,9},{11,10},{16,11},{17,16... | collective-permute-start | bytes 589832 | tf_op jit(solution)/shard_map/ppermute | solution.py:23
  15.4 0.6 %copy-start.8 = (f32[32,128]{1,0:T(8,128)}, f32[32,128]{1,0:T(8,128)S(1)}, u32[]{:S(2)}) copy-start(f32[32,128]{1,0:T(8,128)S(1)} %collective-permute-done.4.refs_2_) | copy-start | bytes 49156
  17.7 2.2 %copy-start.9 = (f32[32,128]{1,0:T(8,128)S(1)}, f32[32,128]{1,0:T(8,128)}, u32[]{:S(2)}) copy-start(f32[32,128]{1,0:T(8,128)} %copy-done.8) | copy-start | bytes 49156
  17.7 3.9 %collective-permute-start.5 = (f32[24,128]{1,0:T(8,128)}, f32[24,128]{1,0:T(8,128)S(1)}, u32[]{:S(2)}, u32[]{:S(2)}) collective-permute-start(f32[24,128]{1,0:T(8,128)} %surface_edge.1), channel_id=1, source_target_pairs={{0,4},{4,0},{1,5},{5,1},{2,6},{6,2},{3,7},{7,3},{8,12},{12,8},{9,1... | collective-permute-start | bytes 36872 | tf_op jit(solution)/shard_map/ppermute | solution.py:23
  21.6 31.1 %collective-permute-start = (f32[224,128]{1,0:T(8,128)S(1)}, f32[224,128]{1,0:T(8,128)S(1)}, u32[]{:S(2)}, u32[]{:S(2)}) collective-permute-start(f32[224,128]{1,0:T(8,128)S(1)} %copy-done.2), channel_id=1, source_target_pairs={{0,1},{1,2},{2,3},{3,0},{4,5},{5,6},{6,7},{7,4},{8,9},{9,10},{10,1... | collective-permute-start | bytes 344072 | tf_op jit(solution)/shard_map/ppermute | solution.py:23
  21.6 11.8 %copy-start.6 = (f32[88,128]{1,0:T(8,128)}, f32[88,128]{1,0:T(8,128)S(1)}, u32[]{:S(2)}) copy-start(f32[88,128]{1,0:T(8,128)S(1)} %constant_dynamic-update-slice_fusion.refs_7_) | copy-start | bytes 135172
  21.6 5.2 %copy-start = (f32[2,24,2,512]{3,2,1,0:T(2,128)}, f32[2,24,2,512]{3,2,1,0:T(2,128)S(1)}, u32[]{:S(2)}) copy-start(f32[2,24,2,512]{3,2,1,0:T(2,128)S(1)} %collective-permute-done.9.up_first.up_last.up_in) | copy-start | bytes 589828
  21.6 10.1 %collective-permute-start.8 = (f32[88,128]{1,0:T(8,128)S(1)}, f32[88,128]{1,0:T(8,128)S(1)}, u32[]{:S(2)}, u32[]{:S(2)}) collective-permute-start(f32[88,128]{1,0:T(8,128)S(1)} %constant_dynamic-update-slice_fusion.refs_7_), channel_id=1, source_target_pairs={{0,3},{1,0},{2,1},{3,2},{4,7},{5,4},{6,5},{7,6},{8,11},{9,8},{10,9... | collective-permute-start | bytes 135176 | tf_op jit(solution)/shard_map/ppermute | solution.py:23
  26.8 0.7 %copy-start.1 = (f32[2,24,2,512]{3,2,1,0:T(2,128)}, f32[2,24,2,512]{3,2,1,0:T(2,128)S(1)}, u32[]{:S(2)}) copy-start(f32[2,24,2,512]{3,2,1,0:T(2,128)S(1)} %collective-permute-done.10.down_first.down_last.down_in) | copy-start | bytes 589828
  29.5 3.9 %collective-permute-start.11 = (f32[8,384]{1,0:T(8,128)}, f32[8,384]{1,0:T(8,128)S(1)}, u32[]{:S(2)}, u32[]{:S(2)}) collective-permute-start(f32[8,384]{1,0:T(8,128)} %soil_edge.1), channel_id=1, source_target_pairs={{0,4},{4,0},{1,5},{5,1},{2,6},{6,2},{3,7},{7,3},{8,12},{12,8},{9,1... | collective-permute-start | bytes 36872 | tf_op jit(solution)/shard_map/ppermute | solution.py:23
  31.0 0.7 %copy-start.14 = (f32[12]{0:T(128)S(1)}, f32[12]{0:T(128)}, u32[]{:S(2)}) copy-start(f32[12]{0:T(128)} %param.14) | copy-start | bytes 148
  31.0 0.7 %copy-start.15 = (f32[12]{0:T(128)S(1)}, f32[12]{0:T(128)}, u32[]{:S(2)}) copy-start(f32[12]{0:T(128)} %param.17) | copy-start | bytes 148
  31.0 0.7 %copy-start.17 = (f32[12]{0:T(128)S(1)}, f32[12]{0:T(128)}, u32[]{:S(2)}) copy-start(f32[12]{0:T(128)} %param.15) | copy-start | bytes 148
  31.7 2.6 %copy-start.10 = (f32[88,128]{1,0:T(8,128)}, f32[88,128]{1,0:T(8,128)S(1)}, u32[]{:S(2)}) copy-start(f32[88,128]{1,0:T(8,128)S(1)} %collective-permute-done.8.refs_10_) | copy-start | bytes 135172
  31.7 21.0 %collective-permute-start.7 = (f32[88,128]{1,0:T(8,128)S(1)}, f32[88,128]{1,0:T(8,128)S(1)}, u32[]{:S(2)}, u32[]{:S(2)}) collective-permute-start(f32[88,128]{1,0:T(8,128)S(1)} %constant_dynamic-update-slice_fusion.refs_7_), channel_id=1, source_target_pairs={{0,2},{1,3},{2,0},{3,1},{4,6},{5,7},{6,4},{7,5},{8,10},{9,11},{10,... | collective-permute-start | bytes 135176 | tf_op jit(solution)/shard_map/ppermute | solution.py:23
  33.4 0.9 %copy-start.13 = (f32[8,384]{1,0:T(8,128)}, f32[8,384]{1,0:T(8,128)S(1)}, u32[]{:S(2)}) copy-start(f32[8,384]{1,0:T(8,128)S(1)} %collective-permute-done.11.edge_in) | copy-start | bytes 36868
  33.4 19.3 %collective-permute-start.6 = (f32[88,128]{1,0:T(8,128)S(1)}, f32[88,128]{1,0:T(8,128)S(1)}, u32[]{:S(2)}, u32[]{:S(2)}) collective-permute-start(f32[88,128]{1,0:T(8,128)S(1)} %constant_dynamic-update-slice_fusion.refs_7_), channel_id=1, source_target_pairs={{0,1},{1,2},{2,3},{3,0},{4,5},{5,6},{6,7},{7,4},{8,9},{9,10},{10,1... | collective-permute-start | bytes 135176 | tf_op jit(solution)/shard_map/ppermute | solution.py:23
  52.7 0.6 %copy-start.11 = (f32[88,128]{1,0:T(8,128)}, f32[88,128]{1,0:T(8,128)S(1)}, u32[]{:S(2)}) copy-start(f32[88,128]{1,0:T(8,128)S(1)} %collective-permute-done.7.refs_9_) | copy-start | bytes 135172
  52.7 0.6 %copy-start.12 = (f32[88,128]{1,0:T(8,128)}, f32[88,128]{1,0:T(8,128)S(1)}, u32[]{:S(2)}) copy-start(f32[88,128]{1,0:T(8,128)S(1)} %collective-permute-done.6.refs_8_) | copy-start | bytes 135172
  52.7 0.7 %copy-start.3 = (f32[224,128]{1,0:T(8,128)}, f32[224,128]{1,0:T(8,128)S(1)}, u32[]{:S(2)}) copy-start(f32[224,128]{1,0:T(8,128)S(1)} %collective-permute-done.2.refs_6_) | copy-start | bytes 344068
  52.7 0.7 %copy-start.4 = (f32[224,128]{1,0:T(8,128)}, f32[224,128]{1,0:T(8,128)S(1)}, u32[]{:S(2)}) copy-start(f32[224,128]{1,0:T(8,128)S(1)} %collective-permute-done.1.refs_5_) | copy-start | bytes 344068
  52.7 0.7 %copy-start.5 = (f32[224,128]{1,0:T(8,128)}, f32[224,128]{1,0:T(8,128)S(1)}, u32[]{:S(2)}) copy-start(f32[224,128]{1,0:T(8,128)S(1)} %collective-permute-done.refs_4_) | copy-start | bytes 344068

commit v3 on v2

--- a/solution.py
+++ b/solution.py
@@ -15,7 +15,7 @@
 
 LANES = 128
 SUBS = 8
-TOP_LAYERS = 4
+TOP_LAYERS = 2
 
 
 def shift(x, axis, step):
@@ -25,34 +25,37 @@
 
 def class_tables(capacity_range, inverse_entry, shape_index, conductivity):
     pore = 1.0 - 1.0 / shape_index
-    expo = 1.0 / (1.0 - pore)
-    rows = [
-        -inverse_entry,
-        expo,
-        pore,
-        capacity_range,
-        2.0 * jnp.sqrt(conductivity),
-        capacity_range * pore * expo * inverse_entry,
-        conductivity,
-        expo - 1.0,
+    rows = [-inverse_entry, 1.0 / (1.0 - pore), pore, capacity_range, 2.0 * jnp.sqrt(conductivity)]
+    return jnp.pad(jnp.stack(rows), ((0, SUBS - len(rows)), (0, LANES - shape_index.shape[0])))
+
+
+def params(tab_ref, idx):
+    return [
+        jnp.take_along_axis(jnp.broadcast_to(tab_ref[i : i + 1, :], idx.shape), idx, axis=1, mode="promise_in_bounds")
+        for i in range(5)
     ]
-    return jnp.pad(jnp.stack(rows), ((0, 0), (0, LANES - shape_index.shape[0])))
-
-
-def pick(tab_ref, row, idx):
-    table = jnp.broadcast_to(tab_ref[row : row + 1, :], idx.shape)
-    return jnp.take_along_axis(table, idx, axis=1, mode="promise_in_bounds")
-
-
-def closure(tab_ref, idx, p):
-    logs = jnp.log2(jnp.maximum(pick(tab_ref, 0, idx) * p, SUCTION_FLOOR))
-    grown = 1.0 + jnp.exp2(pick(tab_ref, 1, idx) * logs)
-    drop = pick(tab_ref, 2, idx) * jnp.log2(grown)
-    content = pick(tab_ref, 3, idx) * jnp.exp2(-drop)
-    ratio = jnp.exp2(pick(tab_ref, 7, idx) * logs - drop)
-    capacity = STORAGE + pick(tab_ref, 5, idx) * ratio / grown
-    root = pick(tab_ref, 4, idx) * jnp.exp2(-0.25 * drop) * jnp.abs(1.0 - ratio)
+
+
+def closure(given, p):
+    entry, expo, pore, span, scale = given
+    logs = jnp.log2(jnp.maximum(entry * p, SUCTION_FLOOR))
+    total = jnp.log2(1.0 + jnp.exp2(expo * logs))
+    drop = pore * total
+    less = expo - 1.0
+    power = less * logs - drop
+    ratio = jnp.exp2(power)
+    content = span * jnp.exp2(-drop)
+    capacity = STORAGE - (span * entry * less) * jnp.exp2(power - total)
+    root = scale * jnp.exp2(-0.25 * drop) * jnp.abs(1.0 - ratio)
     return content, capacity, root
+
+
+def chunks(width):
+    return [slice(i, i + LANES) for i in range(0, width, LANES)]
+
+
+def wide(parts):
+    return [jnp.concatenate(x, axis=1) for x in zip(*parts)]
 
 
 def lateral(x):
@@ -63,10 +66,6 @@
         + pltpu.roll(x, 1, 1)
         + pltpu.roll(x, width - 1, 1)
     )
-
-
-def chunks(width):
-    return [slice(i, i + LANES) for i in range(0, width, LANES)]
 
 
 def soil_mask(flags_ref, rows, width, own_rows, own_cols):
@@ -81,19 +80,50 @@
     return (in_rows * in_cols).astype(jnp.float32)
 
 
-def soil_sweeps(layers, p_ref, c_ref, tab_ref, mask_ref, s, gain, out):
-    _, rows, width = p_ref.shape
-    h_ref, q_ref, n_ref, d_ref, h2_ref, q2_ref, n2_ref, d2_ref, k_ref = s
-    zero = jnp.zeros((rows, width), jnp.float32)
+def soil_rows(p_ref, c_ref, next_ref, prev_ref):
+    _, own, _ = p_ref.shape
+    for f, x in enumerate((p_ref, c_ref)):
+        for r in range(2):
+            next_ref[f, r] = x[:, own - 2 + r, :].astype(jnp.float32)
+            prev_ref[f, r] = x[:, r, :].astype(jnp.float32)
+
+
+def soil_columns(p_first, c_first, p_last, c_last, up_first, up_last, down_first, down_last, box):
+    layers, own, _ = p_first.shape
+    rows = box.shape[1]
+    out = []
+    for side in ((p_last, c_last, up_last, down_last), (p_first, c_first, up_first, down_first)):
+        for f in range(2):
+            box[:, 2 : 2 + own, :] = side[f][...].astype(jnp.float32)
+            box[:, own + 4 :, :] = jnp.zeros((layers, rows - own - 4, LANES), jnp.float32)
+            for r in range(2):
+                box[:, r, :] = side[2][f, r]
+                box[:, own + 2 + r, :] = side[3][f, r]
+            turned = box[...].reshape(layers * rows, LANES).T
+            out.append(turned[LANES - 2 :] if len(out) < 2 else turned[:2])
+    return jnp.concatenate(out, axis=0)
+
+
+def soil_kernel(
+    flags_ref, tab_ref, p_in, c_in, up_in, down_in, got, sent, out_ref, top_out, class_out, next_out,
+    h_ref, q_ref, n_ref, d_ref, k_ref, h2_ref, q2_ref, n2_ref, d2_ref, given, corner, turn, near, near2, pe, ce,
+):
+    layers, own, cols = p_in.shape
+    rows = own + SUBS
+    span = layers * rows
+    f32 = jnp.float32
+    ok = [flags_ref[i] for i in range(4)]
     for ref in (h_ref, q_ref, h2_ref, q2_ref):
-        ref[0] = zero
-        ref[layers + 1] = zero
+        ref[0] = jnp.zeros((own, cols), f32)
+        ref[layers + 1] = jnp.zeros((own, cols), f32)
 
     def first(z, carry):
-        for ch in chunks(width):
-            p = p_ref[z, :, ch]
-            content, capacity, root = closure(tab_ref, c_ref[z, :, ch], p)
-            root = root * mask_ref[:, ch]
+        for ch in chunks(cols):
+            p = p_in[z, :, ch]
+            values = params(tab_ref, c_in[z, :, ch])
+            for i, v in enumerate(values):
+                given[i, z, :, ch] = v
+            content, capacity, root = closure(values, p)
             h_ref[z + 1, :, ch] = root
             q_ref[z + 1, :, ch] = root * p
             n_ref[z, :, ch] = capacity * p
@@ -103,22 +133,96 @@
 
     lax.fori_loop(0, layers, first, 0)
 
-    def sums(z, h, q):
-        mid, over, under = h[z + 1], h[z], h[z + 2]
-        weights = lateral(mid) + over + under
-        flows = lateral(q[z + 1]) + q[z] + q[z + 2] + GRAVITY_STEP * (over - under)
-        return mid, weights, flows
+    gap = jnp.zeros((1, span), f32)
+    p = jnp.concatenate([got[0:2], sent[4:5], gap, sent[1:2], got[4:6], gap], axis=0)
+    kind = jnp.concatenate([got[2:4], sent[6:7], gap, sent[3:4], got[6:8], gap], axis=0).astype(jnp.int32)
+    sub = lax.broadcasted_iota(jnp.int32, (SUBS, span), 0)
+    lane = lax.broadcasted_iota(jnp.int32, (SUBS, span), 1)
+    row = lane % rows
+    row_ok = jnp.where(row < 2, ok[0], jnp.where(row < own + 2, 1, jnp.where(row < own + 4, ok[1], 0)))
+    col_ok = jnp.where(sub < 2, ok[2], jnp.where((sub == 2) | (sub == 4), 1, jnp.where((sub == 5) | (sub == 6), ok[3], 0)))
+    mask = (row_ok * col_ok).astype(f32)
+    values = [params(tab_ref, kind[:, ch]) for ch in chunks(span)]
+    content, capacity, root = wide([closure(v, p[:, ch]) for v, ch in zip(values, chunks(span))])
+    h, q = root * mask, root * mask * p
+
+    def over(x):
+        return jnp.where(lane < rows, 0.0, pltpu.roll(x, rows, 1))
+
+    def under(x):
+        return jnp.where(lane >= span - rows, 0.0, pltpu.roll(x, span - rows, 1))
+
+    weights = lateral(h) + over(h) + under(h)
+    flows = lateral(q) + over(q) + under(q) + GRAVITY_STEP * (over(h) - under(h))
+    p1 = (capacity * p + h * flows) / (capacity + h * weights)
+    root = wide([closure(v, p1[:, ch]) for v, ch in zip(values, chunks(span))])[2] * mask
+    turn[...] = jnp.zeros_like(turn)
+    for i, x in enumerate((h, q, root, root * p1)):
+        turn[i * SUBS : (i + 1) * SUBS, :] = x
+    corner[...] = turn[...].T.reshape(layers, rows, LANES)
+
+    zsub = lax.broadcasted_iota(jnp.int32, (layers, cols), 0)
+    zlane = lax.broadcasted_iota(jnp.int32, (layers, LANES), 1)
+
+    def sides(x, edge, at, lanes):
+        left, right = pltpu.roll(x, 1, 1), pltpu.roll(x, cols - 1, 1)
+        a = jnp.where(lanes == 0, pltpu.roll(edge, LANES - at, 1), left[:, :LANES])
+        b = jnp.where(lanes == LANES - 1, pltpu.roll(edge, LANES - 1 - (at + 4), 1), right[:, cols - LANES :])
+        return jnp.concatenate([a, left[:, LANES:]], axis=1) + jnp.concatenate([right[:, : cols - LANES], b], axis=1)
+
+    for side, (halo, close, far, edge_row, valid) in enumerate(((up_in, 1, 0, 1, ok[0]), (down_in, 0, 1, own + 2, ok[1]))):
+        inside = valid.astype(f32)
+        ours = 0 if side == 0 else own - 1
+        values, states, beyond = [], [], []
+        for ch in chunks(cols):
+            p = halo[0, close, :, ch]
+            v = params(tab_ref, halo[1, close, :, ch].astype(jnp.int32))
+            content, capacity, root = closure(v, p)
+            root = root * inside
+            values.append(v)
+            states.append((p, capacity, root, root * p))
+            p = halo[0, far, :, ch]
+            root = closure(params(tab_ref, halo[1, far, :, ch].astype(jnp.int32)), p)[2] * inside
+            beyond.append((root, root * p))
+        p, capacity, h, q = wide(states)
+        far_h, far_q = wide(beyond)
+        near[side, 0] = h
+        near[side, 1] = q
+        edge = corner[:, edge_row, :]
+        top_h = jnp.where(zsub == 0, 0.0, pltpu.roll(h, 1, 0))
+        low_h = jnp.where(zsub == layers - 1, 0.0, pltpu.roll(h, layers - 1, 0))
+        top_q = jnp.where(zsub == 0, 0.0, pltpu.roll(q, 1, 0))
+        low_q = jnp.where(zsub == layers - 1, 0.0, pltpu.roll(q, layers - 1, 0))
+        weights = far_h + h_ref[1 : layers + 1, ours, :] + sides(h, edge, 1, zlane) + top_h + low_h
+        flows = far_q + q_ref[1 : layers + 1, ours, :] + sides(q, edge, 1 + SUBS, zlane) + top_q + low_q + GRAVITY_STEP * (top_h - low_h)
+        p1 = (capacity * p + h * flows) / (capacity + h * weights)
+        for v, ch in zip(values, chunks(cols)):
+            root = closure(v, p1[:, ch])[2] * inside
+            near2[side, 0, :, ch] = root
+            near2[side, 1, :, ch] = root * p1[:, ch]
+
+    tsub = lax.broadcasted_iota(jnp.int32, (own, cols), 0)
+    tlane = lax.broadcasted_iota(jnp.int32, (own, LANES), 1)
+
+    def around(z, h, q, rim, at):
+        edge = corner[z, 2 : 2 + own, :]
+        out = []
+        for i, x in enumerate((h[z + 1], q[z + 1])):
+            above = jnp.where(tsub == 0, rim[0, i, pl.ds(z, 1), :], pltpu.roll(x, 1, 0))
+            below = jnp.where(tsub == own - 1, rim[1, i, pl.ds(z, 1), :], pltpu.roll(x, own - 1, 0))
+            out.append(above + below + sides(x, edge, at + i * SUBS, tlane))
+        weights, flows = out
+        low = h[z + 2]
+        return weights + low, flows + q[z + 2] - GRAVITY_STEP * low
 
     def second(z, carry):
-        mid, weights, flows = sums(z, h_ref, q_ref)
-        top = n_ref[z] + mid * flows
-        if gain is not None:
-            top = top + jnp.where(z == 0, 1.0, 0.0) * gain
-        q2_ref[z + 1] = top / (d_ref[z] + mid * weights)
-        for ch in chunks(width):
-            p = q2_ref[z + 1, :, ch]
-            content, capacity, root = closure(tab_ref, c_ref[z, :, ch], p)
-            root = root * mask_ref[:, ch]
+        mid, top = h_ref[z + 1], h_ref[z]
+        weights, flows = around(z, h_ref, q_ref, near, 1)
+        flows = flows + q_ref[z] + GRAVITY_STEP * top
+        p1 = (n_ref[z] + mid * flows) / (d_ref[z] + mid * (weights + top))
+        for ch in chunks(cols):
+            p = p1[:, ch]
+            content, capacity, root = closure([given[i, z, :, ch] for i in range(5)], p)
             h2_ref[z + 1, :, ch] = root
             q2_ref[z + 1, :, ch] = root * p
             n2_ref[z, :, ch] = capacity * p - (content - k_ref[z, :, ch])
@@ -128,124 +232,83 @@
     lax.fori_loop(0, layers, second, 0)
 
     def third(z, carry):
-        mid, weights, flows = sums(z, h2_ref, q2_ref)
-        top = n2_ref[z] + mid * flows
-        if gain is not None:
-            top = top + jnp.where(z == 0, 1.0, 0.0) * gain
-        out(z, top / (d2_ref[z] + mid * weights))
+        mid, top = h2_ref[z + 1], h2_ref[z]
+        weights, flows = around(z, h2_ref, q2_ref, near2, 1 + 2 * SUBS)
+        flows = flows + q2_ref[z] + GRAVITY_STEP * top
+        out_ref[z] = (n2_ref[z] + mid * flows) / (d2_ref[z] + mid * (weights + top))
         return carry
 
-    return third
-
-
-def soil_scratch(layers, rows, width):
-    tall = pltpu.VMEM((layers + 2, rows, width), jnp.float32)
-    flat = pltpu.VMEM((layers, rows, width), jnp.float32)
-    return [tall, tall, flat, flat, tall, tall, flat, flat, flat]
-
-
-def soil_pack_kernel(p_ref, c_ref, next_ref, prev_ref):
-    layers, own, _ = p_ref.shape
-    for z in range(layers):
-        next_ref[0, z] = p_ref[z, own - 2 :, :]
-        next_ref[1, z] = c_ref[z, own - 2 :, :].astype(jnp.float32)
-        prev_ref[0, z] = p_ref[z, :2, :]
-        prev_ref[1, z] = c_ref[z, :2, :].astype(jnp.float32)
-
-
-def soil_pack(pressure, soil_class):
-    layers, _, cols = pressure.shape
-    shape = jax.ShapeDtypeStruct((2, layers, 2, cols), jnp.float32)
-    return pl.pallas_call(soil_pack_kernel, out_shape=(shape, shape), name="soil_pack")(pressure, soil_class)
-
-
-def soil_edge_kernel(p_first, c_first, p_last, c_last, up_first, up_last, down_first, down_last, out_ref, box):
-    layers, own, _ = p_first.shape
-    rows = box.shape[1]
-    out = []
-    for side in ((p_last, c_last, up_last, down_last), (p_first, c_first, up_first, down_first)):
-        for f in range(2):
-            for z in range(layers):
-                box[z, :own] = side[f][z].astype(jnp.float32)
-                box[z, own : own + 2] = side[3][f, z]
-                box[z, own + 2 : rows - 2] = jnp.zeros((rows - own - 4, LANES), jnp.float32)
-                box[z, rows - 2 :] = side[2][f, z]
-            turned = box[...].reshape(layers * rows, LANES).T
-            out.append(turned[LANES - 2 :] if len(out) < 2 else turned[:2])
-    out_ref[...] = jnp.concatenate(out, axis=0)
-
-
-def soil_edge(pressure, soil_class, up, down):
-    layers, own, cols = pressure.shape
-    rows = own + SUBS
-    last = cols // LANES - 1
-    tile = [pl.BlockSpec((layers, own, LANES), lambda _, i=i: (0, 0, i)) for i in (0, 0, last, last)]
-    halo = [pl.BlockSpec((2, layers, 2, LANES), lambda _, i=i: (0, 0, 0, i)) for i in (0, last, 0, last)]
-    return pl.pallas_call(
-        soil_edge_kernel,
-        out_shape=jax.ShapeDtypeStruct((8, layers * rows), jnp.float32),
-        grid=(1,),
-        in_specs=tile + halo,
-        scratch_shapes=[pltpu.VMEM((layers, rows, LANES), jnp.float32)],
-        name="soil_edge",
-    )(pressure, soil_class, pressure, soil_class, up, up, down, down)
-
-
-def soil_kernel(flags_ref, tab_ref, p_in, c_in, up_in, down_in, edge_in, out_ref, pe_out, ce_out, pe, ce, mask_ref, turn, *s):
-    layers, own, cols = p_in.shape
-    _, rows, width = pe.shape
-    pad = jnp.zeros((rows - own, cols), jnp.float32)
-    turn[...] = jnp.zeros_like(turn)
-    for f, dst in enumerate((pe, ce)):
-        turn[LANES - 2 :, :] = edge_in[2 * f : 2 * f + 2, :]
-        turn[:2, :] = edge_in[4 + 2 * f : 6 + 2 * f, :]
-        dst[:, :, cols:] = turn[...].T.reshape(layers, rows, LANES).astype(dst.dtype)
-
-    def build(z, carry):
-        for f, (src, dst) in enumerate(((p_in, pe), (c_in, ce))):
-            kind = dst.dtype
-            dst[z, own:, :cols] = pad.astype(kind)
+    lax.fori_loop(2, layers, third, 0)
+
+    weights, flows = around(1, h2_ref, q2_ref, near2, 1 + 2 * SUBS)
+    for i, x in enumerate((h2_ref[2], q2_ref[2], n2_ref[1], d2_ref[1], weights, flows)):
+        next_out[i] = x
+    for f, (src, dst, halo_at) in enumerate(((p_in, pe, 0), (c_in, ce, 2))):
+        turn[...] = jnp.zeros_like(turn)
+        turn[LANES - 2 :, :] = got[halo_at : halo_at + 2]
+        turn[:2, :] = got[halo_at + 4 : halo_at + 6]
+        block = turn[:, :LANES].T
+        for z in range(2):
+            dst[z, own:, :cols] = jnp.zeros((SUBS, cols), dst.dtype)
             dst[z, :own, :cols] = src[z]
-            dst[z, own : own + 2, :cols] = down_in[f, z].astype(kind)
-            dst[z, rows - 2 :, :cols] = up_in[f, z].astype(kind)
-        return carry
-
-    lax.fori_loop(0, layers, build, 0)
-    mask_ref[...] = soil_mask(flags_ref, rows, width, own, cols)
-
-    def out(z, p):
-        out_ref[z] = p[:own, :cols]
-
-    third = soil_sweeps(layers, pe, ce, tab_ref, mask_ref, s, None, out)
-    lax.fori_loop(0, layers, third, 0)
-    pe_out[...] = pe[:TOP_LAYERS]
-    ce_out[...] = ce[:TOP_LAYERS]
-
-
-def soil_interior(flags, tables, pressure, soil_class, up, down, edge):
+            dst[z, :, cols:] = jnp.zeros((rows, LANES), dst.dtype)
+            dst[z, : own + 2, cols:] = block[z * rows + 2 : z * rows + own + 4].astype(dst.dtype)
+            dst[z, rows - 2 :, cols:] = block[z * rows : z * rows + 2].astype(dst.dtype)
+            for r in range(2):
+                dst[z, own + r : own + r + 1, :cols] = down_in[f, r, z : z + 1, :].astype(dst.dtype)
+                dst[z, rows - 2 + r : rows - 1 + r, :cols] = up_in[f, r, z : z + 1, :].astype(dst.dtype)
+    width = cols + LANES
+    mask = soil_mask(flags_ref, rows, width, own, cols)
+    states = []
+    for z in range(2):
+        content, capacity, root = wide([closure(params(tab_ref, ce[z, :, ch]), pe[z, :, ch]) for ch in chunks(width)])
+        states.append((content, capacity, root * mask))
+    content, capacity, h = states[0]
+    low = states[1][2]
+    weights = lateral(h) + low
+    flows = lateral(h * pe[0]) + low * pe[1] - GRAVITY_STEP * low
+    weight = capacity + h * weights
+    top_out[0] = (capacity * pe[0] + h * flows) / weight
+    top_out[1] = 1.0 / weight
+    top_out[2] = content
+    class_out[...] = ce[0]
+
+
+def soil_interior(flags, tables, pressure, soil_class, up, down, got, sent):
     layers, own, cols = pressure.shape
     rows, width = own + SUBS, cols + LANES
+    f32 = jnp.float32
+    span = layers * rows
+    tall = pltpu.VMEM((layers + 2, own, cols), f32)
+    flat = pltpu.VMEM((layers, own, cols), f32)
+    edge = pl.BlockSpec((SUBS, span), lambda _: (0, 0))
+    vmem = pl.BlockSpec(memory_space=pltpu.VMEM)
     return pl.pallas_call(
         soil_kernel,
         out_shape=(
-            jax.ShapeDtypeStruct(pressure.shape, jnp.float32),
-            jax.ShapeDtypeStruct((TOP_LAYERS, rows, width), jnp.float32),
-            jax.ShapeDtypeStruct((TOP_LAYERS, rows, width), jnp.int32),
+            jax.ShapeDtypeStruct(pressure.shape, f32),
+            jax.ShapeDtypeStruct((3, rows, width), f32),
+            jax.ShapeDtypeStruct((rows, width), jnp.int32),
+            jax.ShapeDtypeStruct((6, own, cols), f32),
         ),
-        in_specs=[pl.BlockSpec(memory_space=pltpu.SMEM)] + [pl.BlockSpec(memory_space=pltpu.VMEM)] * 6,
-        out_specs=[pl.BlockSpec(memory_space=pltpu.VMEM)] * 3,
-        scratch_shapes=[
-            pltpu.VMEM((layers, rows, width), jnp.float32),
-            pltpu.VMEM((layers, rows, width), jnp.int32),
-            pltpu.VMEM((rows, width), jnp.float32),
-            pltpu.VMEM((LANES, layers * rows), jnp.float32),
-        ]
-        + soil_scratch(layers, rows, width),
+        grid=(1,),
+        in_specs=[pl.BlockSpec(memory_space=pltpu.SMEM)] + [vmem] * 5 + [edge, edge],
+        out_specs=[vmem] * 4,
+        scratch_shapes=[tall, tall, flat, flat, flat, tall, tall, flat, flat]
+        + [
+            pltpu.VMEM((5, layers, own, cols), f32),
+            pltpu.VMEM((layers, rows, LANES), f32),
+            pltpu.VMEM((LANES, span), f32),
+            pltpu.VMEM((2, 2, layers, cols), f32),
+            pltpu.VMEM((2, 2, layers, cols), f32),
+            pltpu.VMEM((2, rows, width), f32),
+            pltpu.VMEM((2, rows, width), jnp.int32),
+        ],
         name="soil_interior",
-    )(flags, tables, pressure, soil_class, up, down, edge)
-
-
-def surface_pack_kernel(p_ref, c_ref, depth, level, rough, rain, land, channel, main_ref, next_ref, prev_ref):
+    )(flags, tables, pressure, soil_class, up, down, got, sent)
+
+
+def surface_rows(p_ref, c_ref, depth, level, rough, rain, land, channel, main_ref, next_ref, prev_ref):
     height, width = depth.shape
     _, own, cols = p_ref.shape
     fields = (
@@ -272,26 +335,25 @@
 EDGE_ROWS = 16
 
 
-def surface_pack(pressure, soil_class, depth, level, rough, rain, land, channel):
-    _, own, cols = pressure.shape
-    height = depth.shape[0]
-    top = pl.BlockSpec((1, own, cols), lambda _: (0, 0, 0))
-    strip = EDGE_ROWS + 4 * cols // LANES
+def pack(pressure, soil_class, *ground):
+    layers, own, cols = pressure.shape
     f32 = jnp.float32
-    return pl.pallas_call(
-        surface_pack_kernel,
-        out_shape=(
-            jax.ShapeDtypeStruct((5 * height + 2 * own * cols // LANES, LANES), f32),
-            jax.ShapeDtypeStruct((strip, LANES), f32),
-            jax.ShapeDtypeStruct((strip, LANES), f32),
-        ),
-        grid=(1,),
-        in_specs=[top, top] + [pl.BlockSpec(memory_space=pltpu.VMEM)] * 6,
-        name="surface_pack",
-    )(pressure, soil_class, depth, level, rough, rain, land, channel)
-
-
-def surface_edge_kernel(main_ref, above_ref, below_ref, out_ref, box, *, height, own, cols):
+    edge = jax.ShapeDtypeStruct((2, 2, layers, cols), f32)
+    out = [edge, edge]
+    if ground:
+        height = ground[0].shape[0]
+        strip = jax.ShapeDtypeStruct((EDGE_ROWS + 4 * cols // LANES, LANES), f32)
+        out = [jax.ShapeDtypeStruct((5 * height + 2 * own * cols // LANES, LANES), f32), strip, strip] + out
+
+    def body(p_ref, c_ref, *refs):
+        if ground:
+            surface_rows(p_ref, c_ref, *refs[:-2])
+        soil_rows(p_ref, c_ref, *refs[-2:])
+
+    return pl.pallas_call(body, out_shape=out, name="pack")(pressure, soil_class, *ground)
+
+
+def surface_columns(main_ref, above_ref, below_ref, box, height, own, cols):
     n = cols // LANES
     tall = height + SUBS
     box[...] = jnp.zeros_like(box)
@@ -310,23 +372,40 @@
         box[at + tall - 3 : at + tall, :] = above_ref[3 * f : 3 * f + 3, :]
     turned = box[...].T
     edges = jnp.concatenate([turned[LANES - 3 :], turned[:3], jnp.zeros((2, turned.shape[1]), jnp.float32)], axis=0)
-    for j, ch in enumerate(chunks(turned.shape[1])):
-        out_ref[j * SUBS : (j + 1) * SUBS, :] = edges[:, ch]
-
-
-def surface_edge(main, above, below, height, own, cols):
-    wide = LANES + 5 * (height + SUBS)
-    wide += -wide % LANES
+    return edges
+
+
+def columns(pressure, soil_class, up, down, surface):
+    layers, own, cols = pressure.shape
+    rows = own + SUBS
+    last = cols // LANES - 1
+    tile = [pl.BlockSpec((layers, own, LANES), lambda _, i=i: (0, 0, i)) for i in (0, 0, last, last)]
+    halo = [pl.BlockSpec((2, 2, layers, LANES), lambda _, i=i: (0, 0, 0, i)) for i in (0, last, 0, last)]
+    span = layers * rows
+    scratch = [pltpu.VMEM((layers, rows, LANES), jnp.float32)]
+    width = span
+    if surface:
+        height = (surface[0].shape[0] - 2 * own * cols // LANES) // 5
+        tall = LANES + 5 * (height + SUBS)
+        tall += -tall % LANES
+        width += tall
+        scratch.append(pltpu.VMEM((tall, LANES), jnp.float32))
 
     def body(*refs):
-        surface_edge_kernel(*refs, height=height, own=own, cols=cols)
+        n = 8 + len(surface)
+        out_ref = refs[n]
+        out_ref[:, :span] = soil_columns(*refs[:8], refs[n + 1])
+        if surface:
+            out_ref[:, span:] = surface_columns(*refs[8:n], refs[n + 2], height, own, cols)
 
     return pl.pallas_call(
         body,
-        out_shape=jax.ShapeDtypeStruct((wide // LANES * SUBS, LANES), jnp.float32),
-        scratch_shapes=[pltpu.VMEM((wide, LANES), jnp.float32)],
-        name="surface_edge",
-    )(main, above, below)
+        out_shape=jax.ShapeDtypeStruct((SUBS, width), jnp.float32),
+        grid=(1,),
+        in_specs=tile + halo + [pl.BlockSpec(memory_space=pltpu.VMEM)] * len(surface),
+        scratch_shapes=scratch,
+        name="columns",
+    )(pressure, soil_class, pressure, soil_class, up, up, down, down, *surface)
 
 
 def assemble(spot_ref, mains, strips, surf_ref, tops_ref, turn, own, height, count):
@@ -395,8 +474,8 @@
 
 
 def last_kernel(
-    spot_ref, flags_ref, tab_ref, surf_ref, tops_ref, pe, ce, head_out, water_ref,
-    ex_ref, w_ref, mask_ref, new_ref, sem, *s, own,
+    spot_ref, flags_ref, tab_ref, surf_ref, tops_ref, top_ref, class_ref, next_ref, head_out, water_ref,
+    ex_ref, w_ref, new_ref, sem, own,
 ):
     _, rows, width = surf_ref.shape
     block_rows, block_cols = rows - SUBS, width - LANES
@@ -420,7 +499,7 @@
     gates = [convey * across(convey), convey * along(convey)]
     parts = []
     for ch in chunks(width):
-        _, _, root = closure(tab_ref, tops_ref[1, :, ch].astype(jnp.int32), top[:, ch])
+        _, _, root = closure(params(tab_ref, tops_ref[1, :, ch].astype(jnp.int32)), top[:, ch])
         parts.append(0.25 * root * root)
     leak = leak * jnp.concatenate(parts, axis=1)
     water = surf_ref[0]
@@ -450,35 +529,43 @@
     sub = lax.broadcasted_iota(jnp.int32, (SUBS, width), 0)
     rim = jnp.where(sub == SUBS - 1, ex_ref[pl.ds(before, SUBS), :], jnp.where(sub == 0, ex_ref[pl.ds(after, SUBS), :], 0.0))
     gain = jnp.concatenate([ex_ref[pl.ds(first, own), :], rim], axis=0)
-    mask_ref[...] = soil_mask(flags_ref, own + SUBS, width, own, block_cols)
-
-    def out(z, p):
-        new_ref[z] = p[:own, :block_cols]
-
-    third = soil_sweeps(TOP_LAYERS, pe, ce, tab_ref, mask_ref, s, gain, out)
-    lax.fori_loop(0, TOP_LAYERS - 2, third, 0)
-    copy = pltpu.make_async_copy(new_ref, head_out.at[: TOP_LAYERS - 2], sem)
+    mask = soil_mask(flags_ref, own + SUBS, width, own, block_cols)
+    p = top_ref[0] + gain * top_ref[1]
+    content, capacity, root = wide([closure(params(tab_ref, class_ref[:, ch]), p[:, ch]) for ch in chunks(width)])
+    h = root * mask
+    q = h * p
+    low, low_q, low_n, low_d, weights, flows = (next_ref[i] for i in range(6))
+
+    def tile(x):
+        return x[:own, :block_cols]
+
+    top_n = tile(capacity * p - (content - top_ref[2]) + gain + h * lateral(q)) + tile(h) * (low_q - GRAVITY_STEP * low)
+    new_ref[0] = top_n / (tile(capacity + h * lateral(h)) + tile(h) * low)
+    low_n = low_n + low * (flows + tile(q) + GRAVITY_STEP * tile(h))
+    new_ref[1] = low_n / (low_d + low * (weights + tile(h)))
+    copy = pltpu.make_async_copy(new_ref, head_out.at[:TOP_LAYERS], sem)
     copy.start()
     copy.wait()
 
 
-def finish(spot, flags, tables, fields, pe, ce, head, block, count):
+def finish(spot, flags, tables, fields, tops, head, block, count):
     own = head.shape[1]
     whole = count == 0
     rows, width = block[0] + SUBS, block[1] + LANES
     n = len(fields)
 
     def body(spot_ref, flags_ref, tab_ref, *refs):
-        given, (pe_ref, ce_ref, _, head_out, water_ref), (box, turn), rest = refs[:n], refs[n : n + 5], refs[n + 5 : n + 7], refs[n + 7 :]
+        given, known, (head_out, water_ref), (box, turn), rest = refs[:n], refs[n : n + 3], refs[n + 4 : n + 6], refs[n + 6 : n + 8], refs[n + 8 :]
         if whole:
             surf, tops = given
         else:
             surf, tops = box
-            assemble(spot_ref, given[:count], given[count:], surf, tops, turn, own, block[0], count)
-        last_kernel(spot_ref, flags_ref, tab_ref, surf, tops, pe_ref, ce_ref, head_out, water_ref, *rest, own=own)
+            cut = given[0].shape[0] - 2 * (EDGE_ROWS + 4 * block[1] // LANES) - turn.shape[1] // LANES * SUBS
+            assemble(spot_ref, [x.at[:cut] for x in given], [x.at[cut:] for x in given], surf, tops, turn, own, block[0], count)
+        last_kernel(spot_ref, flags_ref, tab_ref, surf, tops, *known, head_out, water_ref, *rest, own=own)
 
     def scratch_body(*refs):
-        cut = 3 + n + 5
+        cut = 3 + n + 6
         body(*refs[:cut], refs[cut : cut + 2], refs[cut + 2], *refs[cut + 3 :])
 
     tall = LANES + 5 * (block[0] + SUBS)
@@ -493,7 +580,7 @@
             jax.ShapeDtypeStruct(head.shape, jnp.float32),
             jax.ShapeDtypeStruct(water, jnp.float32),
         ),
-        in_specs=[smem, smem] + [vmem] * (n + 3) + [pl.BlockSpec(memory_space=pl.ANY)],
+        in_specs=[smem, smem] + [vmem] * (n + 4) + [pl.BlockSpec(memory_space=pl.ANY)],
         out_specs=[pl.BlockSpec(memory_space=pl.ANY), vmem],
         scratch_shapes=[
             pltpu.VMEM(small if whole else (5, rows, width), jnp.float32),
@@ -501,14 +588,12 @@
             pltpu.VMEM((SUBS, LANES) if whole else (LANES, tall), jnp.float32),
             pltpu.VMEM((rows, width), jnp.float32),
             pltpu.VMEM((rows, width), jnp.float32),
-            pltpu.VMEM((own + SUBS, width), jnp.float32),
-            pltpu.VMEM((TOP_LAYERS - 2, own, block[1]), jnp.float32),
+            pltpu.VMEM((TOP_LAYERS, own, block[1]), jnp.float32),
             pltpu.SemaphoreType.DMA,
-        ]
-        + soil_scratch(TOP_LAYERS, own + SUBS, width),
-        input_output_aliases={n + 5: 0},
+        ],
+        input_output_aliases={n + 6: 0},
         name="surface_and_top",
-    )(spot, flags, tables, *fields, pe, ce, head)
+    )(spot, flags, tables, *fields, *tops, head)
 
 
 def lane_rows(size):
@@ -600,19 +685,6 @@
     )
 
 
-def block_parts(pressure, soil_class, depth, elevation, roughness, rain, land_mask, channel_mask):
-    ny = lax.axis_size("gy")
-    _, own, cols = pressure.shape
-    main, after, before = surface_pack(pressure, soil_class, depth, elevation, roughness, rain, land_mask, channel_mask)
-    above = shift(after, "grp", 1)
-    below = shift(before, "grp", -1)
-    mains = [main] + [shift(main, "gy", step) for step in range(1, ny)]
-    edge = surface_edge(main, above, below, depth.shape[0], own, cols)
-    edge = gx_trade(edge, lax.broadcasted_iota(jnp.int32, edge.shape, 0) % SUBS < 3)
-    strip = jnp.concatenate([above, below, edge], axis=0)
-    return mains + [strip] + [shift(strip, "gy", step) for step in range(1, ny)]
-
-
 def local(
     pressure, soil_class, capacity_range, inverse_entry, shape_index, conductivity,
     depth, elevation, roughness, rain, land_mask, channel_mask,
@@ -630,17 +702,27 @@
 
     even = scols == LANES and own == SUBS
     if even:
-        fields = block_parts(pressure, soil_class, *ground)
+        main, strip_after, strip_before, after, before = pack(pressure, soil_class, *ground)
+        above = shift(strip_after, "grp", 1)
+        below = shift(strip_before, "grp", -1)
+        surface = (main, above, below)
+    else:
+        after, before = pack(pressure, soil_class)
+        surface = ()
+    up = shift(after, ("grp", "gy"), 1)
+    down = shift(before, ("grp", "gy"), -1)
+    sent = columns(pressure, soil_class, up, down, surface)
+    span = pressure.shape[0] * (own + SUBS)
+    half = jnp.where(lax.broadcasted_iota(jnp.int32, sent.shape, 1) < span, 4, 3)
+    got = gx_trade(sent, lax.broadcasted_iota(jnp.int32, sent.shape, 0) < half)
+    if even:
+        strip = jnp.concatenate([above, below] + [got[:, ch] for ch in chunks(sent.shape[1])[span // LANES :]], axis=0)
+        strip = jnp.concatenate([main, strip], axis=0)
+        fields = [strip] + [shift(strip, "gy", step) for step in range(1, ny)]
     else:
         fields = block_general(pressure, soil_class, *ground)
-
-    after, before = soil_pack(pressure, soil_class)
-    up = shift(after, ("grp", "gy"), 1)
-    down = shift(before, ("grp", "gy"), -1)
-    edge = soil_edge(pressure, soil_class, up, down)
-    edge = gx_trade(edge, lax.broadcasted_iota(jnp.int32, edge.shape, 0) < 4)
-    head, pe, ce = soil_interior(flags, tables, pressure, soil_class, up, down, edge)
-    head, water = finish(spot, flags, tables, fields, pe, ce, head, (srows, cols), ny if even else 0)
+    head, *tops = soil_interior(flags, tables, pressure, soil_class, up, down, got, sent)
+    head, water = finish(spot, flags, tables, fields, tops, head, (srows, cols), ny if even else 0)
     if not even:
         water = lax.dynamic_slice_in_dim(water, iy * scols, scols, axis=1)
     return head, water

time: 60.1 us -> 48 us (0.80)
  Pallas kernels: 30.3 us -> 20.1 us
  starting transfers between devices: 20.4 us -> 13.7 us
  waiting for transfers between devices: 2.78 us -> 6.9 us
  local copies, waits for them, and re-layouts: 4.7 us -> 5.61 us
    ppermute x12 -> x8, starting transfers between devices: 20.4 us -> 13.7 us  [shift(): return lax.ppermute(x, axis, [(i, (i + step) % size) for i in range(size)])]
    pallas_call x1, Pallas kernels: 17.1 us -> 11.8 us  [soil_interior(): pl.pallas_call(soil_kernel, out_shape=(jax.ShapeDtypeStruct(pressure.shap...]
    ppermute x12 -> x8, waiting for transfers between devices: 2.78 us -> 6.9 us  [shift(): return lax.ppermute(x, axis, [(i, (i + step) % size) for i in range(size)])]
    pallas_call x4 -> x2, Pallas kernels: 7.04 us -> 4.27 us  [the longest x1 2.27 us: columns(): pl.pallas_call(body, out_shape=jax.ShapeDtypeStruct((SUBS, width), jnp.fl...]
    pallas_call x1, Pallas kernels: 6.21 us -> 4.01 us  [finish(): pl.pallas_call(scratch_body, out_shape=(jax.ShapeDtypeStruct(head.shape,...]
    unnamed x38 -> x31, local copies, waits for them, and re-layouts: 3.4 us -> 4.32 us
  transfers between devices with their start and end apart: 12 -> 8, of which waited for: 2 -> 4; matrix products, arithmetic and copies ran while one was open for 4% -> 7% of each run, Pallas kernels for 38% -> 25%
where the time goes in v3:
time: 48 us; the launch traced here: 47.7 us
  Pallas kernels  20.1 us (42%)
  starting transfers between devices  13.7 us (29%)
  waiting for transfers between devices  6.9 us (14%)
  local copies, waits for them, and re-layouts  5.61 us (12%)
  between operations  0.8 us (2%)
  other arithmetic  0.62 us (1%)
    ppermute x8, starting transfers between devices, shift(): return lax.ppermute(x, axis, [(i, (i + step) % size) for i in range(size)])  13.7 us
    pallas_call x1, Pallas kernels, soil_interior(): pl.pallas_call(soil_kernel, out_shape=(jax.ShapeDtypeStruct(pressure.shap...  11.8 us
    ppermute x8, waiting for transfers between devices, shift(): return lax.ppermute(x, axis, [(i, (i + step) % size) for i in range(size)])  6.9 us
    unnamed x31, local copies, waits for them, and re-layouts  4.32 us
    pallas_call x1, Pallas kernels, finish(): pl.pallas_call(scratch_body, out_shape=(jax.ShapeDtypeStruct(head.shape,...  4.01 us
    pallas_call x1, Pallas kernels, columns(): pl.pallas_call(body, out_shape=jax.ShapeDtypeStruct((SUBS, width), jnp.fl...  2.27 us
    pallas_call x1, Pallas kernels, pack(): pl.pallas_call(body, out_shape=out, name='pack')  2 us
  transfers between devices with their start and end apart: 8, of which 4 were waited for; matrix products, arithmetic and copies ran while one was open for 7% of the time, Pallas kernels for 25%

profile of v3, /device:TPU:0, one launch (start us, length us, event | category | flops | bytes accessed | tf_op | source)
XLA Modules:
  0.0 47.7 jit_solution(1077641938065221287)
XLA Ops:
  0.6 2.0 %pack.1 = (f32[224,128]{1,0:T(8,128)}, f32[32,128]{1,0:T(8,128)}, f32[32,128]{1,0:T(8,128)}, f32[2,2,24,512]{3,2,1,0:T(8,128)}, f32[2,2,24,512]{3,2,1,0:T(8,128)}) custom-call(f32[24,8,512]{2,1,0:T(8,128)} %p_in.1, s32[24,8,512]{2,1,0:T(8,128)} %c_in.1, f32[32,128]{1,0:T(8,128)} %refs_0_.2, f32[32,128]{1,0:T(8,128)} %refs_1_.2, f32[32,128]{1,0:T(8,128)} %refs_2_.2, ...), custom_call_target="tpu_custom_call" | custom-call | tf_op jit(solution)/shard_map/pack/pallas_call | solution.py:353
  2.6 3.1 %collective-permute-start.2 = (f32[2,2,24,512]{3,2,1,0:T(8,128)}, f32[2,2,24,512]{3,2,1,0:T(8,128)S(1)}, u32[]{:S(2)}, u32[]{:S(2)}) collective-permute-start(f32[2,2,24,512]{3,2,1,0:T(8,128)} %get-tuple-element.14), channel_id=1, source_target_pairs={{0,1},{1,2},{2,3},{3,8},{8,9},{9,10},{10,11},{11,16},{16,17},{17,1... | collective-permute-start | bytes 589832 | tf_op jit(solution)/shard_map/ppermute | solution.py:23
  5.7 2.4 %collective-permute-start.3 = (f32[2,2,24,512]{3,2,1,0:T(8,128)}, f32[2,2,24,512]{3,2,1,0:T(8,128)S(1)}, u32[]{:S(2)}, u32[]{:S(2)}) collective-permute-start(f32[2,2,24,512]{3,2,1,0:T(8,128)} %get-tuple-element.15), channel_id=1, source_target_pairs={{0,27},{1,0},{2,1},{3,2},{8,3},{9,8},{10,9},{11,10},{16,11},{17,16... | collective-permute-start | bytes 589832 | tf_op jit(solution)/shard_map/ppermute | solution.py:23
  8.1 0.0 collective-permute-start
  8.1 1.7 %collective-permute-start.1 = (f32[32,128]{1,0:T(8,128)}, f32[32,128]{1,0:T(8,128)S(1)}, u32[]{:S(2)}, u32[]{:S(2)}) collective-permute-start(f32[32,128]{1,0:T(8,128)} %get-tuple-element.13), channel_id=1, source_target_pairs={{0,24},{8,0},{16,8},{24,16},{1,25},{9,1},{17,9},{25,17},{2,26},{10... | collective-permute-start | bytes 49160 | tf_op jit(solution)/shard_map/ppermute | solution.py:23
  9.9 0.9 %constant_dynamic-update-slice_fusion.5 = f32[312,128]{1,0:T(8,128)S(1)} fusion(f32[224,128]{1,0:T(8,128)} %get-tuple-element.11.refs_8_), kind=kLoop, calls=%fused_computation.5 | loop fusion | bytes 229376
  10.8 0.9 %collective-permute-done.refs_9_ = f32[32,128]{1,0:T(8,128)S(1)} collective-permute-done((f32[32,128]{1,0:T(8,128)}, f32[32,128]{1,0:T(8,128)S(1)}, u32[]{:S(2)}, u32[]{:S(2)}) %collective-permute-start) | collective-permute-done | bytes 16416 | tf_op jit(solution)/shard_map/ppermute | solution.py:23
  11.7 0.6 %copy-done.7 = f32[32,128]{1,0:T(8,128)} copy-done((f32[32,128]{1,0:T(8,128)}, f32[32,128]{1,0:T(8,128)S(1)}, u32[]{:S(2)}) %copy-start.7) | copy-done | bytes 16408
  12.2 0.0 collective-permute-done.1.refs_10_
  12.2 0.7 %collective-permute-done.2.refs_4_.refs_5_.up_in = f32[2,2,24,512]{3,2,1,0:T(8,128)S(1)} collective-permute-done((f32[2,2,24,512]{3,2,1,0:T(8,128)}, f32[2,2,24,512]{3,2,1,0:T(8,128)S(1)}, u32[]{:S(2)}, u32[]{:S(2)}) %collective-permute-start.2) | collective-permute-done | bytes 196640 | tf_op jit(solution)/shard_map/ppermute | solution.py:23
  13.0 3.5 %collective-permute-done.3.refs_6_.refs_7_.down_in = f32[2,2,24,512]{3,2,1,0:T(8,128)S(1)} collective-permute-done((f32[2,2,24,512]{3,2,1,0:T(8,128)}, f32[2,2,24,512]{3,2,1,0:T(8,128)S(1)}, u32[]{:S(2)}, u32[]{:S(2)}) %collective-permute-start.3) | collective-permute-done | bytes 196640 | tf_op jit(solution)/shard_map/ppermute | solution.py:23
  16.5 0.7 %copy-done.1 = f32[2,2,24,512]{3,2,1,0:T(8,128)} copy-done((f32[2,2,24,512]{3,2,1,0:T(8,128)}, f32[2,2,24,512]{3,2,1,0:T(8,128)S(1)}, u32[]{:S(2)}) %copy-start.1) | copy-done | bytes 196632
  17.1 2.3 %columns.1.sent = f32[8,768]{1,0:T(8,128)} custom-call(f32[24,8,512]{2,1,0:T(8,128)} %p_in.1, s32[24,8,512]{2,1,0:T(8,128)} %c_in.1, f32[24,8,512]{2,1,0:T(8,128)} %p_in.1, s32[24,8,512]{2,1,0:T(8,128)} %c_in.1, f32[2,2,24,512]{3,2,1,0:T(8,128)} %copy-done, f32[2,2,24,512]{3,2,1,0:T(8,128)} %copy-done, f32[2,2,24,512]{3,2,1,0:T(8,128)} %copy-done.1, ...), custom_call_target="tpu_custom_call" | custom-call | tf_op jit(solution)/shard_map/columns/pallas_call | solution.py:401
  19.4 1.5 %collective-permute-start.4 = (f32[8,768]{1,0:T(8,128)}, f32[8,768]{1,0:T(8,128)S(1)}, u32[]{:S(2)}, u32[]{:S(2)}) collective-permute-start(f32[8,768]{1,0:T(8,128)} %columns.1.sent), channel_id=1, source_target_pairs={{0,4},{4,0},{1,5},{5,1},{2,6},{6,2},{3,7},{7,3},{8,12},{12,8},{9,1... | collective-permute-start | bytes 73736 | tf_op jit(solution)/shard_map/ppermute | solution.py:23
  20.9 0.7 %constant_dynamic-update-slice_fusion.3 = f32[312,128]{1,0:T(8,128)S(1)} fusion(f32[312,128]{1,0:T(8,128)S(1)} %constant_dynamic-update-slice_fusion.4, f32[32,128]{1,0:T(8,128)} %copy-done.6), kind=kLoop, calls=%fused_computation.3 | loop fusion | bytes 32768
  21.7 1.8 %collective-permute-done.4.got = f32[8,768]{1,0:T(8,128)S(1)} collective-permute-done((f32[8,768]{1,0:T(8,128)}, f32[8,768]{1,0:T(8,128)S(1)}, u32[]{:S(2)}, u32[]{:S(2)}) %collective-permute-start.4) | collective-permute-done | bytes 24608 | tf_op jit(solution)/shard_map/ppermute | solution.py:23
  23.5 1.6 %collective-permute-start.5 = (f32[312,128]{1,0:T(8,128)S(1)}, f32[312,128]{1,0:T(8,128)S(1)}, u32[]{:S(2)}, u32[]{:S(2)}) collective-permute-start(f32[312,128]{1,0:T(8,128)S(1)} %constant_dynamic-update-slice_fusion.refs_3_), channel_id=1, source_target_pairs={{0,1},{1,2},{2,3},{3,0},{4,5},{5,6},{6,7},{7,4},{8,9},{9,10},{10,1... | collective-permute-start | bytes 479240 | tf_op jit(solution)/shard_map/ppermute | solution.py:23
  25.1 2.0 %collective-permute-start.6 = (f32[312,128]{1,0:T(8,128)S(1)}, f32[312,128]{1,0:T(8,128)S(1)}, u32[]{:S(2)}, u32[]{:S(2)}) collective-permute-start(f32[312,128]{1,0:T(8,128)S(1)} %constant_dynamic-update-slice_fusion.refs_3_), channel_id=1, source_target_pairs={{0,2},{1,3},{2,0},{3,1},{4,6},{5,7},{6,4},{7,5},{8,10},{9,11},{10,... | collective-permute-start | bytes 479240 | tf_op jit(solution)/shard_map/ppermute | solution.py:23
  27.1 1.3 %collective-permute-start.7 = (f32[312,128]{1,0:T(8,128)S(1)}, f32[312,128]{1,0:T(8,128)S(1)}, u32[]{:S(2)}, u32[]{:S(2)}) collective-permute-start(f32[312,128]{1,0:T(8,128)S(1)} %constant_dynamic-update-slice_fusion.refs_3_), channel_id=1, source_target_pairs={{0,3},{1,0},{2,1},{3,2},{4,7},{5,4},{6,5},{7,6},{8,11},{9,8},{10,9... | collective-permute-start | bytes 479240 | tf_op jit(solution)/shard_map/ppermute | solution.py:23
  28.5 0.0 copy-start.11
  28.5 0.6 %copy-done.11 = f32[12]{0:T(128)S(1)} copy-done((f32[12]{0:T(128)S(1)}, f32[12]{0:T(128)}, u32[]{:S(2)}) %copy-start.11) | copy-done | bytes 72
  29.2 0.6 %pad.4.tab_ref.refs_2_ = f32[8,128]{1,0:T(8,128)} pad(f32[5,12]{1,0:T(8,128)S(1)} %stack.87, f32[]{:T(128)} %constant.61.clone.1), padding=0_3x0_116 | pad | bytes 4340 | tf_op jit(solution)/shard_map/jit(_pad)/pad | solution.py:29
  29.8 0.7 %stack.76.refs_0_ = s32[8]{0:T(128)} concatenate(s32[1]{0:T(128)} %bitcast, s32[1]{0:T(128)} %bitcast.1, s32[1]{0:T(128)} %bitcast.2, s32[1]{0:T(128)} %bitcast.3, s32[1]{0:T(128)} %bitcast.4, s32[1]{0:T(128)} %bitcast.5, s32[1]{0:T(128)} %bitcast.6, s32[1]{0:T(128)} %bitcast.7), dimensions={0} | concatenate | bytes 64 | tf_op jit(solution)/shard_map/stack | solution.py:701
  30.5 0.6 %add_convert_fusion.flags_ref.refs_1_ = s32[4]{0:T(128)} fusion(pred[1]{0:T(512)(128)(4,1)} %bitcast.11, pred[1]{0:T(512)(128)(4,1)} %bitcast.10, pred[1]{0:T(512)(128)(4,1)} %bitcast.9, pred[1]{0:T(512)(128)(4,1)} %bitcast.8), kind=kLoop, calls=%fused_computation.6 | loop fusion | flops 16 | bytes 20 | tf_op jit(solution)/shard_map/convert_element_type | solution.py:699
  31.1 11.8 %soil_interior.1 = (f32[24,8,512]{2,1,0:T(8,128)}, f32[3,16,640]{2,1,0:T(8,128)}, s32[16,640]{1,0:T(8,128)}, f32[6,8,512]{2,1,0:T(8,128)}) custom-call(s32[4]{0:T(128)} %add_convert_fusion.flags_ref.refs_1_, f32[8,128]{1,0:T(8,128)} %pad.4.tab_ref.refs_2_, f32[24,8,512]{2,1,0:T(8,128)} %p_in.1, s32[24,8,512]{2,1,0:T(8,128)} %c_in.1, ...), custom_call_target="tpu_custom_call" | custom-call | tf_op jit(solution)/shard_map/soil_interior/pallas_call | solution.py:286
  42.9 0.0 collective-permute-done.5.refs_4_
  42.9 0.0 collective-permute-done.6.refs_5_
  43.0 0.0 collective-permute-done.7.refs_6_
  43.0 0.6 %copy-done.3 = f32[312,128]{1,0:T(8,128)} copy-done((f32[312,128]{1,0:T(8,128)}, f32[312,128]{1,0:T(8,128)S(1)}, u32[]{:S(2)}) %copy-start.3) | copy-done | bytes 159768
  43.6 0.1 copy-done.4
  43.7 0.1 copy-done.5
  43.7 4.0 %surface_and_top.1 = (f32[24,8,512]{2,1,0:T(8,128)}, f32[32,128]{1,0:T(8,128)}) custom-call(s32[8]{0:T(128)} %stack.76.refs_0_, s32[4]{0:T(128)} %add_convert_fusion.flags_ref.refs_1_, f32[8,128]{1,0:T(8,128)} %pad.4.tab_ref.refs_2_, f32[312,128]{1,0:T(8,128)} %copy-done.2, f32[312,128]{1,0:T(8,128)} %copy-done.3, ...), custom_call_target="tpu_custom_call", output_to_operand_aliasing={{0}: (10, {})} | custom-call | tf_op jit(solution)/shard_map/surface_and_top/pallas_call | solution.py:577
  (26 shorter events, 0.1 us)
Async XLA Ops:
  2.6 10.4 %collective-permute-start.2 = (f32[2,2,24,512]{3,2,1,0:T(8,128)}, f32[2,2,24,512]{3,2,1,0:T(8,128)S(1)}, u32[]{:S(2)}, u32[]{:S(2)}) collective-permute-start(f32[2,2,24,512]{3,2,1,0:T(8,128)} %get-tuple-element.14), channel_id=1, source_target_pairs={{0,1},{1,2},{2,3},{3,8},{8,9},{9,10},{10,11},{11,16},{16,17},{17,1... | collective-permute-start | bytes 589832 | tf_op jit(solution)/shard_map/ppermute | solution.py:23
  5.7 10.8 %collective-permute-start.3 = (f32[2,2,24,512]{3,2,1,0:T(8,128)}, f32[2,2,24,512]{3,2,1,0:T(8,128)S(1)}, u32[]{:S(2)}, u32[]{:S(2)}) collective-permute-start(f32[2,2,24,512]{3,2,1,0:T(8,128)} %get-tuple-element.15), channel_id=1, source_target_pairs={{0,27},{1,0},{2,1},{3,2},{8,3},{9,8},{10,9},{11,10},{16,11},{17,16... | collective-permute-start | bytes 589832 | tf_op jit(solution)/shard_map/ppermute | solution.py:23
  8.1 1.8 %copy-start.9 = (f32[12]{0:T(128)S(1)}, f32[12]{0:T(128)}, u32[]{:S(2)}) copy-start(f32[12]{0:T(128)} %param.17) | copy-start | bytes 148
  8.1 1.8 %copy-start.10 = (f32[12]{0:T(128)S(1)}, f32[12]{0:T(128)}, u32[]{:S(2)}) copy-start(f32[12]{0:T(128)} %param.15) | copy-start | bytes 148
  8.1 3.5 %collective-permute-start = (f32[32,128]{1,0:T(8,128)}, f32[32,128]{1,0:T(8,128)S(1)}, u32[]{:S(2)}, u32[]{:S(2)}) collective-permute-start(f32[32,128]{1,0:T(8,128)} %get-tuple-element.12), channel_id=1, source_target_pairs={{0,8},{8,16},{16,24},{24,0},{1,9},{9,17},{17,25},{25,1},{2,10},{10... | collective-permute-start | bytes 49160 | tf_op jit(solution)/shard_map/ppermute | solution.py:23
  8.1 4.1 %collective-permute-start.1 = (f32[32,128]{1,0:T(8,128)}, f32[32,128]{1,0:T(8,128)S(1)}, u32[]{:S(2)}, u32[]{:S(2)}) collective-permute-start(f32[32,128]{1,0:T(8,128)} %get-tuple-element.13), channel_id=1, source_target_pairs={{0,24},{8,0},{16,8},{24,16},{1,25},{9,1},{17,9},{25,17},{2,26},{10... | collective-permute-start | bytes 49160 | tf_op jit(solution)/shard_map/ppermute | solution.py:23
  11.6 0.6 %copy-start.7 = (f32[32,128]{1,0:T(8,128)}, f32[32,128]{1,0:T(8,128)S(1)}, u32[]{:S(2)}) copy-start(f32[32,128]{1,0:T(8,128)S(1)} %collective-permute-done.refs_9_) | copy-start | bytes 49156
  12.2 4.2 %copy-start.6 = (f32[32,128]{1,0:T(8,128)}, f32[32,128]{1,0:T(8,128)S(1)}, u32[]{:S(2)}) copy-start(f32[32,128]{1,0:T(8,128)S(1)} %collective-permute-done.1.refs_10_) | copy-start | bytes 49156
  13.0 3.5 %copy-start = (f32[2,2,24,512]{3,2,1,0:T(8,128)}, f32[2,2,24,512]{3,2,1,0:T(8,128)S(1)}, u32[]{:S(2)}) copy-start(f32[2,2,24,512]{3,2,1,0:T(8,128)S(1)} %collective-permute-done.2.refs_4_.refs_5_.up_in) | copy-start | bytes 589828
  16.5 0.7 %copy-start.1 = (f32[2,2,24,512]{3,2,1,0:T(8,128)}, f32[2,2,24,512]{3,2,1,0:T(8,128)S(1)}, u32[]{:S(2)}) copy-start(f32[2,2,24,512]{3,2,1,0:T(8,128)S(1)} %collective-permute-done.3.refs_6_.refs_7_.down_in) | copy-start | bytes 589828
  19.4 4.0 %collective-permute-start.4 = (f32[8,768]{1,0:T(8,128)}, f32[8,768]{1,0:T(8,128)S(1)}, u32[]{:S(2)}, u32[]{:S(2)}) collective-permute-start(f32[8,768]{1,0:T(8,128)} %columns.1.sent), channel_id=1, source_target_pairs={{0,4},{4,0},{1,5},{5,1},{2,6},{6,2},{3,7},{7,3},{8,12},{12,8},{9,1... | collective-permute-start | bytes 73736 | tf_op jit(solution)/shard_map/ppermute | solution.py:23
  23.5 5.0 %copy-start.8 = (f32[8,768]{1,0:T(8,128)}, f32[8,768]{1,0:T(8,128)S(1)}, u32[]{:S(2)}) copy-start(f32[8,768]{1,0:T(8,128)S(1)} %collective-permute-done.4.got) | copy-start | bytes 73732
  23.5 5.0 %copy-start.12 = (f32[12]{0:T(128)S(1)}, f32[12]{0:T(128)}, u32[]{:S(2)}) copy-start(f32[12]{0:T(128)} %param.16) | copy-start | bytes 148
  23.5 19.4 %copy-start.2 = (f32[312,128]{1,0:T(8,128)}, f32[312,128]{1,0:T(8,128)S(1)}, u32[]{:S(2)}) copy-start(f32[312,128]{1,0:T(8,128)S(1)} %constant_dynamic-update-slice_fusion.refs_3_) | copy-start | bytes 479236
  23.5 19.4 %collective-permute-start.5 = (f32[312,128]{1,0:T(8,128)S(1)}, f32[312,128]{1,0:T(8,128)S(1)}, u32[]{:S(2)}, u32[]{:S(2)}) collective-permute-start(f32[312,128]{1,0:T(8,128)S(1)} %constant_dynamic-update-slice_fusion.refs_3_), channel_id=1, source_target_pairs={{0,1},{1,2},{2,3},{3,0},{4,5},{5,6},{6,7},{7,4},{8,9},{9,10},{10,1... | collective-permute-start | bytes 479240 | tf_op jit(solution)/shard_map/ppermute | solution.py:23
  25.1 17.8 %collective-permute-start.6 = (f32[312,128]{1,0:T(8,128)S(1)}, f32[312,128]{1,0:T(8,128)S(1)}, u32[]{:S(2)}, u32[]{:S(2)}) collective-permute-start(f32[312,128]{1,0:T(8,128)S(1)} %constant_dynamic-update-slice_fusion.refs_3_), channel_id=1, source_target_pairs={{0,2},{1,3},{2,0},{3,1},{4,6},{5,7},{6,4},{7,5},{8,10},{9,11},{10,... | collective-permute-start | bytes 479240 | tf_op jit(solution)/shard_map/ppermute | solution.py:23
  27.1 15.9 %collective-permute-start.7 = (f32[312,128]{1,0:T(8,128)S(1)}, f32[312,128]{1,0:T(8,128)S(1)}, u32[]{:S(2)}, u32[]{:S(2)}) collective-permute-start(f32[312,128]{1,0:T(8,128)S(1)} %constant_dynamic-update-slice_fusion.refs_3_), channel_id=1, source_target_pairs={{0,3},{1,0},{2,1},{3,2},{4,7},{5,4},{6,5},{7,6},{8,11},{9,8},{10,9... | collective-permute-start | bytes 479240 | tf_op jit(solution)/shard_map/ppermute | solution.py:23
  28.5 0.7 %copy-start.11 = (f32[12]{0:T(128)S(1)}, f32[12]{0:T(128)}, u32[]{:S(2)}) copy-start(f32[12]{0:T(128)} %param.14) | copy-start | bytes 148
  42.9 0.7 %copy-start.3 = (f32[312,128]{1,0:T(8,128)}, f32[312,128]{1,0:T(8,128)S(1)}, u32[]{:S(2)}) copy-start(f32[312,128]{1,0:T(8,128)S(1)} %collective-permute-done.5.refs_4_) | copy-start | bytes 479236
  43.0 0.7 %copy-start.4 = (f32[312,128]{1,0:T(8,128)}, f32[312,128]{1,0:T(8,128)S(1)}, u32[]{:S(2)}) copy-start(f32[312,128]{1,0:T(8,128)S(1)} %collective-permute-done.6.refs_5_) | copy-start | bytes 479236
  43.0 0.7 %copy-start.5 = (f32[312,128]{1,0:T(8,128)}, f32[312,128]{1,0:T(8,128)S(1)}, u32[]{:S(2)}) copy-start(f32[312,128]{1,0:T(8,128)S(1)} %collective-permute-done.7.refs_6_) | copy-start | bytes 479236

commit v4 on v3

--- a/solution.py
+++ b/solution.py
@@ -15,6 +15,7 @@
 
 LANES = 128
 SUBS = 8
+UNROLL = 4
 TOP_LAYERS = 2
 
 
@@ -23,10 +24,26 @@
     return lax.ppermute(x, axis, [(i, (i + step) % size) for i in range(size)])
 
 
-def class_tables(capacity_range, inverse_entry, shape_index, conductivity):
-    pore = 1.0 - 1.0 / shape_index
-    rows = [-inverse_entry, 1.0 / (1.0 - pore), pore, capacity_range, 2.0 * jnp.sqrt(conductivity)]
-    return jnp.pad(jnp.stack(rows), ((0, SUBS - len(rows)), (0, LANES - shape_index.shape[0])))
+def class_tables(refs):
+    lane = lax.broadcasted_iota(jnp.int32, (1, LANES), 1)
+    spread = []
+    for ref in refs:
+        row = jnp.ones((1, LANES), jnp.float32)
+        for k in range(ref.shape[0]):
+            row = jnp.where(lane == k, ref[k], row)
+        spread.append(row)
+    span, entry, shape, ks = spread
+    pore = 1.0 - 1.0 / shape
+    rows = [-entry, 1.0 / (1.0 - pore), pore, span, 2.0 * jnp.sqrt(ks)]
+    return jnp.concatenate(rows + [jnp.zeros((SUBS - len(rows), LANES), jnp.float32)], axis=0)
+
+
+def place():
+    tile = lax.axis_index("grp") * lax.axis_size("gy") + lax.axis_index("gy")
+    tiles = lax.axis_size("grp") * lax.axis_size("gy")
+    column, columns = lax.axis_index("gx"), lax.axis_size("gx")
+    tests = (tile > 0, tile < tiles - 1, column > 0, column < columns - 1)
+    return [jnp.where(t, 1, 0) for t in tests]
 
 
 def params(tab_ref, idx):
@@ -68,51 +85,54 @@
     )
 
 
-def soil_mask(flags_ref, rows, width, own_rows, own_cols):
+def soil_mask(ok, rows, width, own_rows, own_cols):
     r = lax.broadcasted_iota(jnp.int32, (rows, width), 0)
     c = lax.broadcasted_iota(jnp.int32, (rows, width), 1)
-    above = jnp.where(r >= rows - 2, flags_ref[0], 0)
-    below = jnp.where((r >= own_rows) & (r < own_rows + 2), flags_ref[1], 0)
-    left = jnp.where(c >= width - 2, flags_ref[2], 0)
-    right = jnp.where((c >= own_cols) & (c < own_cols + 2), flags_ref[3], 0)
+    above = jnp.where(r >= rows - 2, ok[0], 0)
+    below = jnp.where((r >= own_rows) & (r < own_rows + 2), ok[1], 0)
+    left = jnp.where(c >= width - 2, ok[2], 0)
+    right = jnp.where((c >= own_cols) & (c < own_cols + 2), ok[3], 0)
     in_rows = jnp.where(r < own_rows, 1, above + below)
     in_cols = jnp.where(c < own_cols, 1, left + right)
     return (in_rows * in_cols).astype(jnp.float32)
 
 
-def soil_rows(p_ref, c_ref, next_ref, prev_ref):
-    _, own, _ = p_ref.shape
+def soil_rows(p_ref, c_ref, next_ref, prev_ref, next_end, prev_end):
+    layers, own, cols = p_ref.shape
+    start = lax.broadcasted_iota(jnp.int32, (layers, LANES), 1) < LANES // 2
     for f, x in enumerate((p_ref, c_ref)):
         for r in range(2):
             next_ref[f, r] = x[:, own - 2 + r, :].astype(jnp.float32)
             prev_ref[f, r] = x[:, r, :].astype(jnp.float32)
-
-
-def soil_columns(p_first, c_first, p_last, c_last, up_first, up_last, down_first, down_last, box):
+        next_end[f] = jnp.where(start, next_ref[f, 1, :, :LANES], next_ref[f, 1, :, cols - LANES :])
+        prev_end[f] = jnp.where(start, prev_ref[f, 0, :, :LANES], prev_ref[f, 0, :, cols - LANES :])
+
+
+def soil_columns(p_first, c_first, p_last, c_last, up_end, down_end, box):
     layers, own, _ = p_first.shape
     rows = box.shape[1]
     out = []
-    for side in ((p_last, c_last, up_last, down_last), (p_first, c_first, up_first, down_first)):
+    for side in ((p_last, c_last), (p_first, c_first)):
         for f in range(2):
             box[:, 2 : 2 + own, :] = side[f][...].astype(jnp.float32)
-            box[:, own + 4 :, :] = jnp.zeros((layers, rows - own - 4, LANES), jnp.float32)
-            for r in range(2):
-                box[:, r, :] = side[2][f, r]
-                box[:, own + 2 + r, :] = side[3][f, r]
+            box[:, 0, :] = jnp.zeros((layers, LANES), jnp.float32)
+            box[:, 1, :] = up_end[f]
+            box[:, own + 2, :] = down_end[f]
+            box[:, own + 3 :, :] = jnp.zeros((layers, rows - own - 3, LANES), jnp.float32)
             turned = box[...].reshape(layers * rows, LANES).T
             out.append(turned[LANES - 2 :] if len(out) < 2 else turned[:2])
     return jnp.concatenate(out, axis=0)
 
 
 def soil_kernel(
-    flags_ref, tab_ref, p_in, c_in, up_in, down_in, got, sent, out_ref, top_out, class_out, next_out,
+    tab_ref, p_in, c_in, up_in, down_in, got, sent, out_ref, top_out, class_out, next_out,
     h_ref, q_ref, n_ref, d_ref, k_ref, h2_ref, q2_ref, n2_ref, d2_ref, given, corner, turn, near, near2, pe, ce,
 ):
     layers, own, cols = p_in.shape
     rows = own + SUBS
     span = layers * rows
     f32 = jnp.float32
-    ok = [flags_ref[i] for i in range(4)]
+    ok = place()
     for ref in (h_ref, q_ref, h2_ref, q2_ref):
         ref[0] = jnp.zeros((own, cols), f32)
         ref[layers + 1] = jnp.zeros((own, cols), f32)
@@ -131,7 +151,7 @@
             k_ref[z, :, ch] = content
         return carry
 
-    lax.fori_loop(0, layers, first, 0)
+    lax.fori_loop(0, layers, first, 0, unroll=UNROLL)
 
     gap = jnp.zeros((1, span), f32)
     p = jnp.concatenate([got[0:2], sent[4:5], gap, sent[1:2], got[4:6], gap], axis=0)
@@ -229,7 +249,7 @@
             d2_ref[z, :, ch] = capacity
         return carry
 
-    lax.fori_loop(0, layers, second, 0)
+    lax.fori_loop(0, layers, second, 0, unroll=UNROLL)
 
     def third(z, carry):
         mid, top = h2_ref[z + 1], h2_ref[z]
@@ -238,7 +258,7 @@
         out_ref[z] = (n2_ref[z] + mid * flows) / (d2_ref[z] + mid * (weights + top))
         return carry
 
-    lax.fori_loop(2, layers, third, 0)
+    lax.fori_loop(0, layers, third, 0, unroll=UNROLL)
 
     weights, flows = around(1, h2_ref, q2_ref, near2, 1 + 2 * SUBS)
     for i, x in enumerate((h2_ref[2], q2_ref[2], n2_ref[1], d2_ref[1], weights, flows)):
@@ -258,7 +278,7 @@
                 dst[z, own + r : own + r + 1, :cols] = down_in[f, r, z : z + 1, :].astype(dst.dtype)
                 dst[z, rows - 2 + r : rows - 1 + r, :cols] = up_in[f, r, z : z + 1, :].astype(dst.dtype)
     width = cols + LANES
-    mask = soil_mask(flags_ref, rows, width, own, cols)
+    mask = soil_mask(ok, rows, width, own, cols)
     states = []
     for z in range(2):
         content, capacity, root = wide([closure(params(tab_ref, ce[z, :, ch]), pe[z, :, ch]) for ch in chunks(width)])
@@ -274,7 +294,7 @@
     class_out[...] = ce[0]
 
 
-def soil_interior(flags, tables, pressure, soil_class, up, down, got, sent):
+def soil_interior(tables, pressure, soil_class, up, down, got, sent):
     layers, own, cols = pressure.shape
     rows, width = own + SUBS, cols + LANES
     f32 = jnp.float32
@@ -292,7 +312,7 @@
             jax.ShapeDtypeStruct((6, own, cols), f32),
         ),
         grid=(1,),
-        in_specs=[pl.BlockSpec(memory_space=pltpu.SMEM)] + [vmem] * 5 + [edge, edge],
+        in_specs=[vmem] * 5 + [edge, edge],
         out_specs=[vmem] * 4,
         scratch_shapes=[tall, tall, flat, flat, flat, tall, tall, flat, flat]
         + [
@@ -305,7 +325,7 @@
             pltpu.VMEM((2, rows, width), jnp.int32),
         ],
         name="soil_interior",
-    )(flags, tables, pressure, soil_class, up, down, got, sent)
+    )(tables, pressure, soil_class, up, down, got, sent)
 
 
 def surface_rows(p_ref, c_ref, depth, level, rough, rain, land, channel, main_ref, next_ref, prev_ref):
@@ -335,22 +355,32 @@
 EDGE_ROWS = 16
 
 
-def pack(pressure, soil_class, *ground):
+def pack(pressure, soil_class, classes, ground):
     layers, own, cols = pressure.shape
     f32 = jnp.float32
     edge = jax.ShapeDtypeStruct((2, 2, layers, cols), f32)
-    out = [edge, edge]
+    end = jax.ShapeDtypeStruct((2, layers, LANES), f32)
+    out = [edge, edge, end, end]
     if ground:
         height = ground[0].shape[0]
         strip = jax.ShapeDtypeStruct((EDGE_ROWS + 4 * cols // LANES, LANES), f32)
         out = [jax.ShapeDtypeStruct((5 * height + 2 * own * cols // LANES, LANES), f32), strip, strip] + out
 
-    def body(p_ref, c_ref, *refs):
+    def body(*refs):
+        tables, rest = refs[: len(classes)], refs[len(classes) :]
         if ground:
-            surface_rows(p_ref, c_ref, *refs[:-2])
-        soil_rows(p_ref, c_ref, *refs[-2:])
-
-    return pl.pallas_call(body, out_shape=out, name="pack")(pressure, soil_class, *ground)
+            surface_rows(*rest[: 2 + len(ground)], *rest[3 + len(ground) : 6 + len(ground)])
+        soil_rows(*rest[:2], *rest[-4:])
+        rest[2 + len(ground)][...] = class_tables(tables)
+
+    vmem = pl.BlockSpec(memory_space=pltpu.VMEM)
+    smem = pl.BlockSpec(memory_space=pltpu.SMEM)
+    return pl.pallas_call(
+        body,
+        out_shape=[jax.ShapeDtypeStruct((SUBS, LANES), f32)] + out,
+        in_specs=[smem] * len(classes) + [vmem] * (2 + len(ground)),
+        name="pack",
+    )(*classes, pressure, soil_class, *ground)
 
 
 def surface_columns(main_ref, above_ref, below_ref, box, height, own, cols):
@@ -375,12 +405,11 @@
     return edges
 
 
-def columns(pressure, soil_class, up, down, surface):
+def columns(pressure, soil_class, up_end, down_end, surface):
     layers, own, cols = pressure.shape
     rows = own + SUBS
     last = cols // LANES - 1
     tile = [pl.BlockSpec((layers, own, LANES), lambda _, i=i: (0, 0, i)) for i in (0, 0, last, last)]
-    halo = [pl.BlockSpec((2, 2, layers, LANES), lambda _, i=i: (0, 0, 0, i)) for i in (0, last, 0, last)]
     span = layers * rows
     scratch = [pltpu.VMEM((layers, rows, LANES), jnp.float32)]
     width = span
@@ -392,23 +421,23 @@
         scratch.append(pltpu.VMEM((tall, LANES), jnp.float32))
 
     def body(*refs):
-        n = 8 + len(surface)
+        n = 6 + len(surface)
         out_ref = refs[n]
-        out_ref[:, :span] = soil_columns(*refs[:8], refs[n + 1])
+        out_ref[:, :span] = soil_columns(*refs[:6], refs[n + 1])
         if surface:
-            out_ref[:, span:] = surface_columns(*refs[8:n], refs[n + 2], height, own, cols)
+            out_ref[:, span:] = surface_columns(*refs[6:n], refs[n + 2], height, own, cols)
 
     return pl.pallas_call(
         body,
         out_shape=jax.ShapeDtypeStruct((SUBS, width), jnp.float32),
         grid=(1,),
-        in_specs=tile + halo + [pl.BlockSpec(memory_space=pltpu.VMEM)] * len(surface),
+        in_specs=tile + [pl.BlockSpec(memory_space=pltpu.VMEM)] * (2 + len(surface)),
         scratch_shapes=scratch,
         name="columns",
-    )(pressure, soil_class, pressure, soil_class, up, up, down, down, *surface)
-
-
-def assemble(spot_ref, mains, strips, surf_ref, tops_ref, turn, own, height, count):
+    )(pressure, soil_class, pressure, soil_class, up_end, down_end, *surface)
+
+
+def assemble(mains, strips, surf_ref, tops_ref, turn, own, height, count):
     _, rows, width = surf_ref.shape
     cols = width - LANES
     n = cols // LANES
@@ -420,7 +449,7 @@
     turn[...] = jnp.zeros_like(turn)
     for s in range(count):
         main, extra = mains[s], strips[s]
-        who = spot_ref[4 + s]
+        who = (lax.axis_index("gy") - s) % count
         at = pl.multiple_of(who * LANES, LANES)
         first = pl.multiple_of(who * own, own)
         above, below = 0, strip
@@ -474,15 +503,18 @@
 
 
 def last_kernel(
-    spot_ref, flags_ref, tab_ref, surf_ref, tops_ref, top_ref, class_ref, next_ref, head_out, water_ref,
+    tab_ref, surf_ref, tops_ref, top_ref, class_ref, next_ref, head_out, water_ref,
     ex_ref, w_ref, new_ref, sem, own,
 ):
     _, rows, width = surf_ref.shape
     block_rows, block_cols = rows - SUBS, width - LANES
     r = lax.broadcasted_iota(jnp.int32, (rows, width), 0)
     c = lax.broadcasted_iota(jnp.int32, (rows, width), 1)
-    row_ok = jnp.where(r < block_rows, 1, jnp.where(r >= rows - 3, spot_ref[2], jnp.where(r < block_rows + 3, spot_ref[3], 0)))
-    col_ok = jnp.where(c < block_cols, 1, jnp.where(c >= width - 3, flags_ref[2], jnp.where(c < block_cols + 3, flags_ref[3], 0)))
+    ok = place()
+    group, groups, line = lax.axis_index("grp"), lax.axis_size("grp"), lax.axis_index("gy")
+    more = [jnp.where(t, 1, 0) for t in (group > 0, group < groups - 1)]
+    row_ok = jnp.where(r < block_rows, 1, jnp.where(r >= rows - 3, more[0], jnp.where(r < block_rows + 3, more[1], 0)))
+    col_ok = jnp.where(c < block_cols, 1, jnp.where(c >= width - 3, ok[2], jnp.where(c < block_cols + 3, ok[3], 0)))
     inside = (row_ok * col_ok).astype(jnp.float32)
     level = surf_ref[1]
     convey = jnp.sqrt(surf_ref[2]) * inside
@@ -521,15 +553,15 @@
     if water_ref.shape[1] % LANES:
         water_ref[...] = w_ref[:block_rows, :block_cols]
     else:
-        mine = pl.multiple_of(spot_ref[4] * water_ref.shape[1], LANES)
+        mine = pl.multiple_of(line * water_ref.shape[1], LANES)
         water_ref[...] = w_ref[:block_rows, pl.ds(mine, water_ref.shape[1])]
-    first = pl.multiple_of(spot_ref[0], SUBS)
-    after = pl.multiple_of(spot_ref[0] + own, SUBS)
-    before = pl.multiple_of(spot_ref[1], SUBS)
+    first = pl.multiple_of(line * own, SUBS)
+    after = pl.multiple_of(line * own + own, SUBS)
+    before = pl.multiple_of(jnp.where(line > 0, line * own - SUBS, block_rows), SUBS)
     sub = lax.broadcasted_iota(jnp.int32, (SUBS, width), 0)
     rim = jnp.where(sub == SUBS - 1, ex_ref[pl.ds(before, SUBS), :], jnp.where(sub == 0, ex_ref[pl.ds(after, SUBS), :], 0.0))
     gain = jnp.concatenate([ex_ref[pl.ds(first, own), :], rim], axis=0)
-    mask = soil_mask(flags_ref, own + SUBS, width, own, block_cols)
+    mask = soil_mask(ok, own + SUBS, width, own, block_cols)
     p = top_ref[0] + gain * top_ref[1]
     content, capacity, root = wide([closure(params(tab_ref, class_ref[:, ch]), p[:, ch]) for ch in chunks(width)])
     h = root * mask
@@ -548,31 +580,30 @@
     copy.wait()
 
 
-def finish(spot, flags, tables, fields, tops, head, block, count):
+def finish(tables, fields, tops, head, block, count):
     own = head.shape[1]
     whole = count == 0
     rows, width = block[0] + SUBS, block[1] + LANES
     n = len(fields)
 
-    def body(spot_ref, flags_ref, tab_ref, *refs):
+    def body(tab_ref, *refs):
         given, known, (head_out, water_ref), (box, turn), rest = refs[:n], refs[n : n + 3], refs[n + 4 : n + 6], refs[n + 6 : n + 8], refs[n + 8 :]
         if whole:
             surf, tops = given
         else:
             surf, tops = box
             cut = given[0].shape[0] - 2 * (EDGE_ROWS + 4 * block[1] // LANES) - turn.shape[1] // LANES * SUBS
-            assemble(spot_ref, [x.at[:cut] for x in given], [x.at[cut:] for x in given], surf, tops, turn, own, block[0], count)
-        last_kernel(spot_ref, flags_ref, tab_ref, surf, tops, *known, head_out, water_ref, *rest, own=own)
+            assemble([x.at[:cut] for x in given], [x.at[cut:] for x in given], surf, tops, turn, own, block[0], count)
+        last_kernel(tab_ref, surf, tops, *known, head_out, water_ref, *rest, own=own)
 
     def scratch_body(*refs):
-        cut = 3 + n + 6
+        cut = 1 + n + 6
         body(*refs[:cut], refs[cut : cut + 2], refs[cut + 2], *refs[cut + 3 :])
 
     tall = LANES + 5 * (block[0] + SUBS)
     tall += -tall % LANES
     small = (1, SUBS, LANES)
     vmem = pl.BlockSpec(memory_space=pltpu.VMEM)
-    smem = pl.BlockSpec(memory_space=pltpu.SMEM)
     water = block if whole else (block[0], LANES)
     return pl.pallas_call(
         scratch_body,
@@ -580,7 +611,7 @@
             jax.ShapeDtypeStruct(head.shape, jnp.float32),
             jax.ShapeDtypeStruct(water, jnp.float32),
         ),
-        in_specs=[smem, smem] + [vmem] * (n + 4) + [pl.BlockSpec(memory_space=pl.ANY)],
+        in_specs=[vmem] * (n + 4) + [pl.BlockSpec(memory_space=pl.ANY)],
         out_specs=[pl.BlockSpec(memory_space=pl.ANY), vmem],
         scratch_shapes=[
             pltpu.VMEM(small if whole else (5, rows, width), jnp.float32),
@@ -591,9 +622,9 @@
             pltpu.VMEM((TOP_LAYERS, own, block[1]), jnp.float32),
             pltpu.SemaphoreType.DMA,
         ],
-        input_output_aliases={n + 6: 0},
+        input_output_aliases={n + 4: 0},
         name="surface_and_top",
-    )(spot, flags, tables, *fields, *tops, head)
+    )(tables, *fields, *tops, head)
 
 
 def lane_rows(size):
@@ -689,29 +720,24 @@
     pressure, soil_class, capacity_range, inverse_entry, shape_index, conductivity,
     depth, elevation, roughness, rain, land_mask, channel_mask,
 ):
-    ng, nx, ny = (lax.axis_size(a) for a in ("grp", "gx", "gy"))
-    ig, ix, iy = (lax.axis_index(a) for a in ("grp", "gx", "gy"))
+    ny, iy = lax.axis_size("gy"), lax.axis_index("gy")
     _, own, cols = pressure.shape
     srows, scols = depth.shape
     ground = (depth, elevation, roughness, rain, land_mask, channel_mask)
-    tables = class_tables(capacity_range, inverse_entry, shape_index, conductivity)
-    tile = ig * ny + iy
-    flags = jnp.stack([tile > 0, tile < ng * ny - 1, ix > 0, ix < nx - 1]).astype(jnp.int32)
-    spot = [iy * own, jnp.where(iy > 0, iy * own - SUBS, srows), (ig > 0).astype(jnp.int32), (ig < ng - 1).astype(jnp.int32)]
-    spot = jnp.stack(spot + [(iy - step) % ny for step in range(ny)])
-
+    classes = (capacity_range, inverse_entry, shape_index, conductivity)
     even = scols == LANES and own == SUBS
+    tables, *packed = pack(pressure, soil_class, classes, ground if even else ())
+    after, before, after_end, before_end = packed[-4:]
+    surface = ()
     if even:
-        main, strip_after, strip_before, after, before = pack(pressure, soil_class, *ground)
+        main, strip_after, strip_before = packed[:3]
         above = shift(strip_after, "grp", 1)
         below = shift(strip_before, "grp", -1)
         surface = (main, above, below)
-    else:
-        after, before = pack(pressure, soil_class)
-        surface = ()
-    up = shift(after, ("grp", "gy"), 1)
-    down = shift(before, ("grp", "gy"), -1)
-    sent = columns(pressure, soil_class, up, down, surface)
+    rows = ("grp", "gy")
+    sent = columns(pressure, soil_class, shift(after_end, rows, 1), shift(before_end, rows, -1), surface)
+    up = shift(after, rows, 1)
+    down = shift(before, rows, -1)
     span = pressure.shape[0] * (own + SUBS)
     half = jnp.where(lax.broadcasted_iota(jnp.int32, sent.shape, 1) < span, 4, 3)
     got = gx_trade(sent, lax.broadcasted_iota(jnp.int32, sent.shape, 0) < half)
@@ -721,8 +747,8 @@
         fields = [strip] + [shift(strip, "gy", step) for step in range(1, ny)]
     else:
         fields = block_general(pressure, soil_class, *ground)
-    head, *tops = soil_interior(flags, tables, pressure, soil_class, up, down, got, sent)
-    head, water = finish(spot, flags, tables, fields, tops, head, (srows, cols), ny if even else 0)
+    head, *tops = soil_interior(tables, pressure, soil_class, up, down, got, sent)
+    head, water = finish(tables, fields, tops, head, (srows, cols), ny if even else 0)
     if not even:
         water = lax.dynamic_slice_in_dim(water, iy * scols, scols, axis=1)
     return head, water

time: 48 us -> 40.7 us (0.85)
  waiting for transfers between devices: 6.9 us -> 2.24 us
  Pallas kernels: 20.1 us -> 15.5 us
  starting transfers between devices: 13.7 us -> 17.6 us
  local copies, waits for them, and re-layouts: 5.61 us -> 4.34 us
  other arithmetic: 0.62 us -> 0 us
    ppermute x8 -> x10, waiting for transfers between devices: 6.9 us -> 2.24 us  [shift(): return lax.ppermute(x, axis, [(i, (i + step) % size) for i in range(size)])]
    pallas_call x1, Pallas kernels: 11.8 us -> 7.29 us  [soil_interior(): pl.pallas_call(soil_kernel, out_shape=(jax.ShapeDtypeStruct(pressure.shap...]
    ppermute x8 -> x10, starting transfers between devices: 13.7 us -> 17.6 us  [shift(): return lax.ppermute(x, axis, [(i, (i + step) % size) for i in range(size)])]
    another operation x2 -> x0, local copies, waits for them, and re-layouts: 0.69 us -> none  [the longest x1 0.67 us: local(): spot = jnp.stack(spot + [(iy - step) % ny for step in range(ny)])]
    convert_element_type x1 -> x0, other arithmetic: 0.61 us -> none  [local(): jnp.stack([tile > 0, tile < ng * ny - 1, ix > 0, ix < nx - 1])]
    pad x1 -> x0, local copies, waits for them, and re-layouts: 0.6 us -> none  [class_tables(): jnp.pad(jnp.stack(rows), ((0, SUBS - len(rows)), (0, LANES - shape_index....]
    unnamed x31 -> x29, local copies, waits for them, and re-layouts: 4.32 us -> 4.34 us
  transfers between devices with their start and end apart: 8 -> 10, of which waited for: 4 -> 2; matrix products, arithmetic and copies ran while one was open for 7% -> 4% of each run, Pallas kernels for 25% -> 23%
where the time goes in v4:
time: 40.7 us; the launch traced here: 40.4 us
  starting transfers between devices  17.6 us (43%)
  Pallas kernels  15.5 us (38%)
  local copies, waits for them, and re-layouts  4.34 us (11%)
  waiting for transfers between devices  2.24 us (6%)
  between operations  0.78 us (2%)
    ppermute x10, starting transfers between devices, shift(): return lax.ppermute(x, axis, [(i, (i + step) % size) for i in range(size)])  17.6 us
    pallas_call x1, Pallas kernels, soil_interior(): pl.pallas_call(soil_kernel, out_shape=(jax.ShapeDtypeStruct(pressure.shap...  7.29 us
    unnamed x29, local copies, waits for them, and re-layouts  4.34 us
    pallas_call x1, Pallas kernels, finish(): pl.pallas_call(scratch_body, out_shape=(jax.ShapeDtypeStruct(head.shape,...  4 us
    ppermute x10, waiting for transfers between devices, shift(): return lax.ppermute(x, axis, [(i, (i + step) % size) for i in range(size)])  2.24 us
    pallas_call x1, Pallas kernels, columns(): pl.pallas_call(body, out_shape=jax.ShapeDtypeStruct((SUBS, width), jnp.fl...  2.19 us
    pallas_call x1, Pallas kernels, pack(): pl.pallas_call(body, out_shape=[jax.ShapeDtypeStruct((SUBS, LANES), f32)]...  2 us
  transfers between devices with their start and end apart: 10, of which 2 were waited for; matrix products, arithmetic and copies ran while one was open for 4% of the time, Pallas kernels for 23%

profile of v4, /device:TPU:0, one launch (start us, length us, event | category | flops | bytes accessed | tf_op | source)
XLA Modules:
  0.0 40.4 jit_solution(12510056594502700040)
XLA Ops:
  0.6 2.0 %pack.1 = (f32[8,128]{1,0:T(8,128)}, f32[224,128]{1,0:T(8,128)}, f32[32,128]{1,0:T(8,128)}, f32[32,128]{1,0:T(8,128)}, f32[2,2,24,512]{3,2,1,0:T(8,128)}, /*inde...) custom-call(f32[12]{0:T(128)} %refs_0_.2, f32[12]{0:T(128)} %refs_1_.2, f32[12]{0:T(128)} %refs_2_.2, ...), custom_call_target="tpu_custom_call" | custom-call | tf_op jit(solution)/shard_map/pack/pallas_call | solution.py:378
  2.6 0.5 %collective-permute-start = (f32[32,128]{1,0:T(8,128)}, f32[32,128]{1,0:T(8,128)S(1)}, u32[]{:S(2)}, u32[]{:S(2)}) collective-permute-start(f32[32,128]{1,0:T(8,128)} %get-tuple-element.16), channel_id=1, source_target_pairs={{0,8},{8,16},{16,24},{24,0},{1,9},{9,17},{17,25},{25,1},{2,10},{10... | collective-permute-start | bytes 49160 | tf_op jit(solution)/shard_map/ppermute | solution.py:24
  3.2 2.0 %collective-permute-start.1 = (f32[32,128]{1,0:T(8,128)}, f32[32,128]{1,0:T(8,128)S(1)}, u32[]{:S(2)}, u32[]{:S(2)}) collective-permute-start(f32[32,128]{1,0:T(8,128)} %get-tuple-element.17), channel_id=1, source_target_pairs={{0,24},{8,0},{16,8},{24,16},{1,25},{9,1},{17,9},{25,17},{2,26},{10... | collective-permute-start | bytes 49160 | tf_op jit(solution)/shard_map/ppermute | solution.py:24
  5.2 2.3 %collective-permute-start.2 = (f32[2,24,128]{2,1,0:T(8,128)}, f32[2,24,128]{2,1,0:T(8,128)S(1)}, u32[]{:S(2)}, u32[]{:S(2)}) collective-permute-start(f32[2,24,128]{2,1,0:T(8,128)} %get-tuple-element.18), channel_id=1, source_target_pairs={{0,1},{1,2},{2,3},{3,8},{8,9},{9,10},{10,11},{11,16},{16,17},{17,1... | collective-permute-start | bytes 73736 | tf_op jit(solution)/shard_map/ppermute | solution.py:24
  7.5 2.1 %collective-permute-start.3 = (f32[2,24,128]{2,1,0:T(8,128)}, f32[2,24,128]{2,1,0:T(8,128)S(1)}, u32[]{:S(2)}, u32[]{:S(2)}) collective-permute-start(f32[2,24,128]{2,1,0:T(8,128)} %get-tuple-element.19), channel_id=1, source_target_pairs={{0,27},{1,0},{2,1},{3,2},{8,3},{9,8},{10,9},{11,10},{16,11},{17,16... | collective-permute-start | bytes 73736 | tf_op jit(solution)/shard_map/ppermute | solution.py:24
  9.6 0.0 collective-permute-start.8
  9.6 0.9 %constant_dynamic-update-slice_fusion.5 = f32[312,128]{1,0:T(8,128)S(1)} fusion(f32[224,128]{1,0:T(8,128)} %get-tuple-element.15.refs_6_), kind=kLoop, calls=%fused_computation.5 | loop fusion | bytes 229376
  10.5 0.0 collective-permute-done.refs_7_
  10.5 4.5 %collective-permute-start.9 = (f32[2,2,24,512]{3,2,1,0:T(8,128)S(1)}, f32[2,2,24,512]{3,2,1,0:T(8,128)S(1)}, u32[]{:S(2)}, u32[]{:S(2)}) collective-permute-start(f32[2,2,24,512]{3,2,1,0:T(8,128)S(1)} %copy-done.11), channel_id=1, source_target_pairs={{0,27},{1,0},{2,1},{3,2},{8,3},{9,8},{10,9},{11,10},{16,11},{17,16... | collective-permute-start | bytes 589832 | tf_op jit(solution)/shard_map/ppermute | solution.py:24
  15.0 0.0 collective-permute-done.1.refs_8_
  15.1 0.0 copy-start.6
  15.1 0.0 collective-permute-done.2.refs_4_
  15.1 0.0 collective-permute-done.3.refs_5_
  15.1 0.6 %copy-done.6 = f32[32,128]{1,0:T(8,128)} copy-done((f32[32,128]{1,0:T(8,128)}, f32[32,128]{1,0:T(8,128)S(1)}, u32[]{:S(2)}) %copy-start.6) | copy-done | bytes 16408
  15.7 0.0 copy-done.9
  15.7 0.6 %copy-done.10 = f32[2,24,128]{2,1,0:T(8,128)} copy-done((f32[2,24,128]{2,1,0:T(8,128)}, f32[2,24,128]{2,1,0:T(8,128)S(1)}, u32[]{:S(2)}) %copy-start.10) | copy-done | bytes 24600
  16.3 2.2 %columns.1.sent = f32[8,768]{1,0:T(8,128)} custom-call(f32[24,8,512]{2,1,0:T(8,128)} %p_in.1, s32[24,8,512]{2,1,0:T(8,128)} %c_in.1, f32[24,8,512]{2,1,0:T(8,128)} %p_in.1, s32[24,8,512]{2,1,0:T(8,128)} %c_in.1, f32[2,24,128]{2,1,0:T(8,128)} %copy-done.9, f32[2,24,128]{2,1,0:T(8,128)} %copy-done.10, f32[224,128]{1,0:T(8,128)} %get-tuple-element.15.refs_6_, ...), custom_call_target="tpu_custom_call" | custom-call | tf_op jit(solution)/shard_map/columns/pallas_call | solution.py:430
  18.5 2.3 %collective-permute-start.4 = (f32[8,768]{1,0:T(8,128)}, f32[8,768]{1,0:T(8,128)S(1)}, u32[]{:S(2)}, u32[]{:S(2)}) collective-permute-start(f32[8,768]{1,0:T(8,128)} %columns.1.sent), channel_id=1, source_target_pairs={{0,4},{4,0},{1,5},{5,1},{2,6},{6,2},{3,7},{7,3},{8,12},{12,8},{9,1... | collective-permute-start | bytes 73736 | tf_op jit(solution)/shard_map/ppermute | solution.py:24
  20.8 0.7 %constant_dynamic-update-slice_fusion.3 = f32[312,128]{1,0:T(8,128)S(1)} fusion(f32[312,128]{1,0:T(8,128)S(1)} %constant_dynamic-update-slice_fusion.4, f32[32,128]{1,0:T(8,128)} %copy-done.6), kind=kLoop, calls=%fused_computation.3 | loop fusion | bytes 32768
  21.5 1.3 %collective-permute-done.4.got = f32[8,768]{1,0:T(8,128)S(1)} collective-permute-done((f32[8,768]{1,0:T(8,128)}, f32[8,768]{1,0:T(8,128)S(1)}, u32[]{:S(2)}, u32[]{:S(2)}) %collective-permute-start.4) | collective-permute-done | bytes 24608 | tf_op jit(solution)/shard_map/ppermute | solution.py:24
  22.8 0.1 collective-permute-start.5
  22.9 0.1 collective-permute-start.6
  22.9 3.7 %collective-permute-start.7 = (f32[312,128]{1,0:T(8,128)S(1)}, f32[312,128]{1,0:T(8,128)S(1)}, u32[]{:S(2)}, u32[]{:S(2)}) collective-permute-start(f32[312,128]{1,0:T(8,128)S(1)} %constant_dynamic-update-slice_fusion.refs_1_), channel_id=1, source_target_pairs={{0,3},{1,0},{2,1},{3,2},{4,7},{5,4},{6,5},{7,6},{8,11},{9,8},{10,9... | collective-permute-start | bytes 479240 | tf_op jit(solution)/shard_map/ppermute | solution.py:24
  26.7 0.0 collective-permute-done.8.up_in
  26.7 0.0 collective-permute-done.9.down_in
  26.7 0.6 %copy-done.1 = f32[2,2,24,512]{3,2,1,0:T(8,128)} copy-done((f32[2,2,24,512]{3,2,1,0:T(8,128)}, f32[2,2,24,512]{3,2,1,0:T(8,128)S(1)}, u32[]{:S(2)}) %copy-start.1) | copy-done | bytes 196632
  27.4 0.1 copy-done.2
  27.4 7.3 %soil_interior.1 = (f32[24,8,512]{2,1,0:T(8,128)}, f32[3,16,640]{2,1,0:T(8,128)}, s32[16,640]{1,0:T(8,128)}, f32[6,8,512]{2,1,0:T(8,128)}) custom-call(f32[8,128]{1,0:T(8,128)} %get-tuple-element.14.tab_ref.refs_0_, f32[24,8,512]{2,1,0:T(8,128)} %p_in.1, s32[24,8,512]{2,1,0:T(8,128)} %c_in.1, f32[2,2,24,512]{3,2,1,0:T(8,128)} %copy-done.1, ...), custom_call_target="tpu_custom_call" | custom-call | tf_op jit(solution)/shard_map/soil_interior/pallas_call | solution.py:306
  34.8 0.9 %collective-permute-done.6.refs_3_ = f32[312,128]{1,0:T(8,128)S(1)} collective-permute-done((f32[312,128]{1,0:T(8,128)S(1)}, f32[312,128]{1,0:T(8,128)S(1)}, u32[]{:S(2)}, u32[]{:S(2)}) %collective-permute-start.6) | collective-permute-done | bytes 159776 | tf_op jit(solution)/shard_map/ppermute | solution.py:24
  35.7 0.6 %copy-done.4 = f32[312,128]{1,0:T(8,128)} copy-done((f32[312,128]{1,0:T(8,128)}, f32[312,128]{1,0:T(8,128)S(1)}, u32[]{:S(2)}) %copy-start.4) | copy-done | bytes 159768
  36.3 0.1 copy-done.5
  36.4 4.0 %surface_and_top.1 = (f32[24,8,512]{2,1,0:T(8,128)}, f32[32,128]{1,0:T(8,128)}) custom-call(f32[8,128]{1,0:T(8,128)} %get-tuple-element.14.tab_ref.refs_0_, f32[312,128]{1,0:T(8,128)} %copy-done, f32[312,128]{1,0:T(8,128)} %copy-done.3, f32[312,128]{1,0:T(8,128)} %copy-done.4, f32[312,128]{1,0:T(8,128)} %copy-done.5, ...), custom_call_target="tpu_custom_call", output_to_operand_aliasing={{0}: (8, {})} | custom-call | tf_op jit(solution)/shard_map/surface_and_top/pallas_call | solution.py:608
  (22 shorter events, 0.0 us)
Async XLA Ops:
  2.6 7.9 %copy-start.11 = (f32[2,2,24,512]{3,2,1,0:T(8,128)S(1)}, f32[2,2,24,512]{3,2,1,0:T(8,128)}, u32[]{:S(2)}) copy-start(f32[2,2,24,512]{3,2,1,0:T(8,128)} %get-tuple-element.21) | copy-start | bytes 589828
  2.6 7.9 %collective-permute-start = (f32[32,128]{1,0:T(8,128)}, f32[32,128]{1,0:T(8,128)S(1)}, u32[]{:S(2)}, u32[]{:S(2)}) collective-permute-start(f32[32,128]{1,0:T(8,128)} %get-tuple-element.16), channel_id=1, source_target_pairs={{0,8},{8,16},{16,24},{24,0},{1,9},{9,17},{17,25},{25,1},{2,10},{10... | collective-permute-start | bytes 49160 | tf_op jit(solution)/shard_map/ppermute | solution.py:24
  3.2 11.9 %collective-permute-start.1 = (f32[32,128]{1,0:T(8,128)}, f32[32,128]{1,0:T(8,128)S(1)}, u32[]{:S(2)}, u32[]{:S(2)}) collective-permute-start(f32[32,128]{1,0:T(8,128)} %get-tuple-element.17), channel_id=1, source_target_pairs={{0,24},{8,0},{16,8},{24,16},{1,25},{9,1},{17,9},{25,17},{2,26},{10... | collective-permute-start | bytes 49160 | tf_op jit(solution)/shard_map/ppermute | solution.py:24
  5.2 9.9 %collective-permute-start.2 = (f32[2,24,128]{2,1,0:T(8,128)}, f32[2,24,128]{2,1,0:T(8,128)S(1)}, u32[]{:S(2)}, u32[]{:S(2)}) collective-permute-start(f32[2,24,128]{2,1,0:T(8,128)} %get-tuple-element.18), channel_id=1, source_target_pairs={{0,1},{1,2},{2,3},{3,8},{8,9},{9,10},{10,11},{11,16},{16,17},{17,1... | collective-permute-start | bytes 73736 | tf_op jit(solution)/shard_map/ppermute | solution.py:24
  7.5 7.6 %collective-permute-start.3 = (f32[2,24,128]{2,1,0:T(8,128)}, f32[2,24,128]{2,1,0:T(8,128)S(1)}, u32[]{:S(2)}, u32[]{:S(2)}) collective-permute-start(f32[2,24,128]{2,1,0:T(8,128)} %get-tuple-element.19), channel_id=1, source_target_pairs={{0,27},{1,0},{2,1},{3,2},{8,3},{9,8},{10,9},{11,10},{16,11},{17,16... | collective-permute-start | bytes 73736 | tf_op jit(solution)/shard_map/ppermute | solution.py:24
  9.6 17.1 %collective-permute-start.8 = (f32[2,2,24,512]{3,2,1,0:T(8,128)}, f32[2,2,24,512]{3,2,1,0:T(8,128)S(1)}, u32[]{:S(2)}, u32[]{:S(2)}) collective-permute-start(f32[2,2,24,512]{3,2,1,0:T(8,128)} %get-tuple-element.20), channel_id=1, source_target_pairs={{0,1},{1,2},{2,3},{3,8},{8,9},{9,10},{10,11},{11,16},{16,17},{17,1... | collective-permute-start | bytes 589832 | tf_op jit(solution)/shard_map/ppermute | solution.py:24
  10.5 4.5 %copy-start.7 = (f32[32,128]{1,0:T(8,128)}, f32[32,128]{1,0:T(8,128)S(1)}, u32[]{:S(2)}) copy-start(f32[32,128]{1,0:T(8,128)S(1)} %collective-permute-done.refs_7_) | copy-start | bytes 49156
  10.5 16.1 %collective-permute-start.9 = (f32[2,2,24,512]{3,2,1,0:T(8,128)S(1)}, f32[2,2,24,512]{3,2,1,0:T(8,128)S(1)}, u32[]{:S(2)}, u32[]{:S(2)}) collective-permute-start(f32[2,2,24,512]{3,2,1,0:T(8,128)S(1)} %copy-done.11), channel_id=1, source_target_pairs={{0,27},{1,0},{2,1},{3,2},{8,3},{9,8},{10,9},{11,10},{16,11},{17,16... | collective-permute-start | bytes 589832 | tf_op jit(solution)/shard_map/ppermute | solution.py:24
  15.1 0.6 %copy-start.6 = (f32[32,128]{1,0:T(8,128)}, f32[32,128]{1,0:T(8,128)S(1)}, u32[]{:S(2)}) copy-start(f32[32,128]{1,0:T(8,128)S(1)} %collective-permute-done.1.refs_8_) | copy-start | bytes 49156
  15.1 0.6 %copy-start.9 = (f32[2,24,128]{2,1,0:T(8,128)}, f32[2,24,128]{2,1,0:T(8,128)S(1)}, u32[]{:S(2)}) copy-start(f32[2,24,128]{2,1,0:T(8,128)S(1)} %collective-permute-done.2.refs_4_) | copy-start | bytes 73732
  15.7 0.6 %copy-start.10 = (f32[2,24,128]{2,1,0:T(8,128)}, f32[2,24,128]{2,1,0:T(8,128)S(1)}, u32[]{:S(2)}) copy-start(f32[2,24,128]{2,1,0:T(8,128)S(1)} %collective-permute-done.3.refs_5_) | copy-start | bytes 73732
  18.5 4.3 %collective-permute-start.4 = (f32[8,768]{1,0:T(8,128)}, f32[8,768]{1,0:T(8,128)S(1)}, u32[]{:S(2)}, u32[]{:S(2)}) collective-permute-start(f32[8,768]{1,0:T(8,128)} %columns.1.sent), channel_id=1, source_target_pairs={{0,4},{4,0},{1,5},{5,1},{2,6},{6,2},{3,7},{7,3},{8,12},{12,8},{9,1... | collective-permute-start | bytes 73736 | tf_op jit(solution)/shard_map/ppermute | solution.py:24
  22.8 3.9 %copy-start.8 = (f32[8,768]{1,0:T(8,128)}, f32[8,768]{1,0:T(8,128)S(1)}, u32[]{:S(2)}) copy-start(f32[8,768]{1,0:T(8,128)S(1)} %collective-permute-done.4.got) | copy-start | bytes 73732
  22.8 12.0 %copy-start = (f32[312,128]{1,0:T(8,128)}, f32[312,128]{1,0:T(8,128)S(1)}, u32[]{:S(2)}) copy-start(f32[312,128]{1,0:T(8,128)S(1)} %constant_dynamic-update-slice_fusion.refs_1_) | copy-start | bytes 479236
  22.8 11.9 %collective-permute-start.5 = (f32[312,128]{1,0:T(8,128)S(1)}, f32[312,128]{1,0:T(8,128)S(1)}, u32[]{:S(2)}, u32[]{:S(2)}) collective-permute-start(f32[312,128]{1,0:T(8,128)S(1)} %constant_dynamic-update-slice_fusion.refs_1_), channel_id=1, source_target_pairs={{0,1},{1,2},{2,3},{3,0},{4,5},{5,6},{6,7},{7,4},{8,9},{9,10},{10,1... | collective-permute-start | bytes 479240 | tf_op jit(solution)/shard_map/ppermute | solution.py:24
  22.9 12.8 %collective-permute-start.6 = (f32[312,128]{1,0:T(8,128)S(1)}, f32[312,128]{1,0:T(8,128)S(1)}, u32[]{:S(2)}, u32[]{:S(2)}) collective-permute-start(f32[312,128]{1,0:T(8,128)S(1)} %constant_dynamic-update-slice_fusion.refs_1_), channel_id=1, source_target_pairs={{0,2},{1,3},{2,0},{3,1},{4,6},{5,7},{6,4},{7,5},{8,10},{9,11},{10,... | collective-permute-start | bytes 479240 | tf_op jit(solution)/shard_map/ppermute | solution.py:24
  22.9 12.7 %collective-permute-start.7 = (f32[312,128]{1,0:T(8,128)S(1)}, f32[312,128]{1,0:T(8,128)S(1)}, u32[]{:S(2)}, u32[]{:S(2)}) collective-permute-start(f32[312,128]{1,0:T(8,128)S(1)} %constant_dynamic-update-slice_fusion.refs_1_), channel_id=1, source_target_pairs={{0,3},{1,0},{2,1},{3,2},{4,7},{5,4},{6,5},{7,6},{8,11},{9,8},{10,9... | collective-permute-start | bytes 479240 | tf_op jit(solution)/shard_map/ppermute | solution.py:24
  26.7 0.7 %copy-start.1 = (f32[2,2,24,512]{3,2,1,0:T(8,128)}, f32[2,2,24,512]{3,2,1,0:T(8,128)S(1)}, u32[]{:S(2)}) copy-start(f32[2,2,24,512]{3,2,1,0:T(8,128)S(1)} %collective-permute-done.8.up_in) | copy-start | bytes 589828
  26.7 0.8 %copy-start.2 = (f32[2,2,24,512]{3,2,1,0:T(8,128)}, f32[2,2,24,512]{3,2,1,0:T(8,128)S(1)}, u32[]{:S(2)}) copy-start(f32[2,2,24,512]{3,2,1,0:T(8,128)S(1)} %collective-permute-done.9.down_in) | copy-start | bytes 589828
  34.7 0.9 %copy-start.3 = (f32[312,128]{1,0:T(8,128)}, f32[312,128]{1,0:T(8,128)S(1)}, u32[]{:S(2)}) copy-start(f32[312,128]{1,0:T(8,128)S(1)} %collective-permute-done.5.refs_2_) | copy-start | bytes 479236
  35.7 0.7 %copy-start.4 = (f32[312,128]{1,0:T(8,128)}, f32[312,128]{1,0:T(8,128)S(1)}, u32[]{:S(2)}) copy-start(f32[312,128]{1,0:T(8,128)S(1)} %collective-permute-done.6.refs_3_) | copy-start | bytes 479236
  35.7 0.7 %copy-start.5 = (f32[312,128]{1,0:T(8,128)}, f32[312,128]{1,0:T(8,128)S(1)}, u32[]{:S(2)}) copy-start(f32[312,128]{1,0:T(8,128)S(1)} %collective-permute-done.7.refs_4_) | copy-start | bytes 479236

commit v5 on v4

--- a/solution.py
+++ b/solution.py
@@ -4,6 +4,7 @@
 from jax.experimental import pallas as pl
 from jax.experimental.pallas import tpu as pltpu
 from jax.sharding import PartitionSpec as P
+
 
 PASSES = 3
 STORAGE = 0.01
@@ -15,13 +16,17 @@
 
 LANES = 128
 SUBS = 8
-UNROLL = 4
+UNROLL = 8
 TOP_LAYERS = 2
 
 
 def shift(x, axis, step):
     size = lax.axis_size(axis)
     return lax.ppermute(x, axis, [(i, (i + step) % size) for i in range(size)])
+
+
+def near(*arrays):
+    return [pltpu.with_memory_space_constraint(x, pltpu.VMEM) for x in arrays]
 
 
 def class_tables(refs):
@@ -125,19 +130,34 @@
 
 
 def soil_kernel(
-    tab_ref, p_in, c_in, up_in, down_in, got, sent, out_ref, top_out, class_out, next_out,
-    h_ref, q_ref, n_ref, d_ref, k_ref, h2_ref, q2_ref, n2_ref, d2_ref, given, corner, turn, near, near2, pe, ce,
+    tab_ref, p_far, c_far, up_in, down_in, got_in, sent_in, out_far, top_out, class_out, next_out,
+    p_in, c_in, out_ref, tile_sem, out_sem, h_ref, q_ref, n_ref, d_ref, k_ref, h2_ref, q2_ref, n2_ref, d2_ref, given, corner, turn, near, near2, pe, ce,
 ):
     layers, own, cols = p_in.shape
     rows = own + SUBS
     span = layers * rows
     f32 = jnp.float32
     ok = place()
+
+    def tile_copy(i, j):
+        part = pl.ds(j * UNROLL, UNROLL)
+        far, here = ((p_far, p_in), (c_far, c_in))[i]
+        return pltpu.make_async_copy(far.at[part], here.at[part], tile_sem.at[i, j])
+
+    def out_copy(j):
+        part = pl.ds(j * UNROLL, UNROLL)
+        return pltpu.make_async_copy(out_ref.at[part], out_far.at[part], out_sem.at[j])
+
+    got, sent = got_in[:, :span], sent_in[:, :span]
+    groups = layers // UNROLL
+    for j in range(groups):
+        tile_copy(0, j).start()
+        tile_copy(1, j).start()
     for ref in (h_ref, q_ref, h2_ref, q2_ref):
         ref[0] = jnp.zeros((own, cols), f32)
         ref[layers + 1] = jnp.zeros((own, cols), f32)
 
-    def first(z, carry):
+    def first(z):
         for ch in chunks(cols):
             p = p_in[z, :, ch]
             values = params(tab_ref, c_in[z, :, ch])
@@ -149,9 +169,15 @@
             n_ref[z, :, ch] = capacity * p
             d_ref[z, :, ch] = capacity
             k_ref[z, :, ch] = content
+
+    def first_group(j, carry):
+        tile_copy(0, j).wait()
+        tile_copy(1, j).wait()
+        for i in range(UNROLL):
+            first(j * UNROLL + i)
         return carry
 
-    lax.fori_loop(0, layers, first, 0, unroll=UNROLL)
+    lax.fori_loop(0, groups, first_group, 0)
 
     gap = jnp.zeros((1, span), f32)
     p = jnp.concatenate([got[0:2], sent[4:5], gap, sent[1:2], got[4:6], gap], axis=0)
@@ -251,14 +277,19 @@
 
     lax.fori_loop(0, layers, second, 0, unroll=UNROLL)
 
-    def third(z, carry):
+    def third(z):
         mid, top = h2_ref[z + 1], h2_ref[z]
         weights, flows = around(z, h2_ref, q2_ref, near2, 1 + 2 * SUBS)
         flows = flows + q2_ref[z] + GRAVITY_STEP * top
         out_ref[z] = (n2_ref[z] + mid * flows) / (d2_ref[z] + mid * (weights + top))
+
+    def third_group(j, carry):
+        for i in range(UNROLL):
+            third(j * UNROLL + i)
+        out_copy(j).start()
         return carry
 
-    lax.fori_loop(0, layers, third, 0, unroll=UNROLL)
+    lax.fori_loop(0, groups, third_group, 0)
 
     weights, flows = around(1, h2_ref, q2_ref, near2, 1 + 2 * SUBS)
     for i, x in enumerate((h2_ref[2], q2_ref[2], n2_ref[1], d2_ref[1], weights, flows)):
@@ -291,6 +322,10 @@
     top_out[0] = (capacity * pe[0] + h * flows) / weight
     top_out[1] = 1.0 / weight
     top_out[2] = content
+    top_out[3] = pe[0]
+    top_out[4] = h
+    for j in range(groups):
+        out_copy(j).wait()
     class_out[...] = ce[0]
 
 
@@ -301,20 +336,21 @@
     span = layers * rows
     tall = pltpu.VMEM((layers + 2, own, cols), f32)
     flat = pltpu.VMEM((layers, own, cols), f32)
-    edge = pl.BlockSpec((SUBS, span), lambda _: (0, 0))
     vmem = pl.BlockSpec(memory_space=pltpu.VMEM)
+    far = pl.BlockSpec(memory_space=pl.ANY)
     return pl.pallas_call(
         soil_kernel,
         out_shape=(
             jax.ShapeDtypeStruct(pressure.shape, f32),
-            jax.ShapeDtypeStruct((3, rows, width), f32),
-            jax.ShapeDtypeStruct((rows, width), jnp.int32),
-            jax.ShapeDtypeStruct((6, own, cols), f32),
+            pltpu.VMEM((5, rows, width), f32),
+            pltpu.VMEM((rows, width), jnp.int32),
+            pltpu.VMEM((6, own, cols), f32),
         ),
-        grid=(1,),
-        in_specs=[vmem] * 5 + [edge, edge],
-        out_specs=[vmem] * 4,
-        scratch_shapes=[tall, tall, flat, flat, flat, tall, tall, flat, flat]
+        in_specs=[vmem] + [far] * 2 + [vmem] * 4,
+        out_specs=[far] + [vmem] * 3,
+        scratch_shapes=[flat, pltpu.VMEM((layers, own, cols), jnp.int32), flat]
+        + [pltpu.SemaphoreType.DMA((2, layers // UNROLL)), pltpu.SemaphoreType.DMA((layers // UNROLL,))]
+        + [tall, tall, flat, flat, flat, tall, tall, flat, flat]
         + [
             pltpu.VMEM((5, layers, own, cols), f32),
             pltpu.VMEM((layers, rows, LANES), f32),
@@ -325,11 +361,11 @@
             pltpu.VMEM((2, rows, width), jnp.int32),
         ],
         name="soil_interior",
-    )(tables, pressure, soil_class, up, down, got, sent)
+    )(*near(tables), pressure, soil_class, *near(up, down, got, sent))
 
 
 def surface_rows(p_ref, c_ref, depth, level, rough, rain, land, channel, main_ref, next_ref, prev_ref):
-    height, width = depth.shape
+    height, _ = depth.shape
     _, own, cols = p_ref.shape
     fields = (
         depth[...],
@@ -358,13 +394,13 @@
 def pack(pressure, soil_class, classes, ground):
     layers, own, cols = pressure.shape
     f32 = jnp.float32
-    edge = jax.ShapeDtypeStruct((2, 2, layers, cols), f32)
-    end = jax.ShapeDtypeStruct((2, layers, LANES), f32)
+    edge = pltpu.VMEM((2, 2, layers, cols), f32)
+    end = pltpu.VMEM((2, layers, LANES), f32)
     out = [edge, edge, end, end]
     if ground:
         height = ground[0].shape[0]
-        strip = jax.ShapeDtypeStruct((EDGE_ROWS + 4 * cols // LANES, LANES), f32)
-        out = [jax.ShapeDtypeStruct((5 * height + 2 * own * cols // LANES, LANES), f32), strip, strip] + out
+        strip = pltpu.VMEM((EDGE_ROWS + 4 * cols // LANES, LANES), f32)
+        out = [pltpu.VMEM((5 * height + 2 * own * cols // LANES, LANES), f32), strip, strip] + out
 
     def body(*refs):
         tables, rest = refs[: len(classes)], refs[len(classes) :]
@@ -377,7 +413,7 @@
     smem = pl.BlockSpec(memory_space=pltpu.SMEM)
     return pl.pallas_call(
         body,
-        out_shape=[jax.ShapeDtypeStruct((SUBS, LANES), f32)] + out,
+        out_shape=[pltpu.VMEM((SUBS, LANES), f32)] + out,
         in_specs=[smem] * len(classes) + [vmem] * (2 + len(ground)),
         name="pack",
     )(*classes, pressure, soil_class, *ground)
@@ -408,8 +444,6 @@
 def columns(pressure, soil_class, up_end, down_end, surface):
     layers, own, cols = pressure.shape
     rows = own + SUBS
-    last = cols // LANES - 1
-    tile = [pl.BlockSpec((layers, own, LANES), lambda _, i=i: (0, 0, i)) for i in (0, 0, last, last)]
     span = layers * rows
     scratch = [pltpu.VMEM((layers, rows, LANES), jnp.float32)]
     width = span
@@ -420,211 +454,266 @@
         width += tall
         scratch.append(pltpu.VMEM((tall, LANES), jnp.float32))
 
+    n = 4 + len(surface)
+    kinds = (pressure.dtype, soil_class.dtype)
+
     def body(*refs):
-        n = 6 + len(surface)
-        out_ref = refs[n]
-        out_ref[:, :span] = soil_columns(*refs[:6], refs[n + 1])
+        out_ref, box, ends, sems = refs[n], refs[n + 1], refs[-5:-1], refs[-1]
+        copies = [
+            pltpu.make_async_copy(refs[i % 2].at[:, :, pl.ds(i // 2 * (cols - LANES), LANES)], ends[i], sems.at[i]) for i in range(4)
+        ]
+        for copy in copies:
+            copy.start()
         if surface:
-            out_ref[:, span:] = surface_columns(*refs[6:n], refs[n + 2], height, own, cols)
+            out_ref[:, span:] = surface_columns(*refs[4:n], refs[n + 2], height, own, cols)
+        for copy in copies:
+            copy.wait()
+        out_ref[:, :span] = soil_columns(*ends, *refs[2:4], box)
 
     return pl.pallas_call(
         body,
-        out_shape=jax.ShapeDtypeStruct((SUBS, width), jnp.float32),
-        grid=(1,),
-        in_specs=tile + [pl.BlockSpec(memory_space=pltpu.VMEM)] * (2 + len(surface)),
-        scratch_shapes=scratch,
+        out_shape=pltpu.VMEM((SUBS, width), jnp.float32),
+        in_specs=[pl.BlockSpec(memory_space=pl.ANY)] * 2 + [pl.BlockSpec(memory_space=pltpu.VMEM)] * (2 + len(surface)),
+        scratch_shapes=scratch + [pltpu.VMEM((layers, own, LANES), k) for k in kinds * 2] + [pltpu.SemaphoreType.DMA((4,))],
         name="columns",
-    )(pressure, soil_class, pressure, soil_class, up_end, down_end, *surface)
-
-
-def assemble(mains, strips, surf_ref, tops_ref, turn, own, height, count):
-    _, rows, width = surf_ref.shape
-    cols = width - LANES
-    n = cols // LANES
-    tall = height + SUBS
-    strip = EDGE_ROWS + 4 * n
+    )(pressure, soil_class, *near(up_end, down_end, *surface))
+
+
+def rim(at_end, at_start, lane, count):
+    return jnp.where(lane >= LANES - count, at_end, jnp.where(lane < count, at_start, 0.0))
+
+
+def ring(before, after, sub):
+    return jnp.where(sub >= SUBS - 3, before, jnp.where(sub < 3, after, 0.0))
+
+
+WINDOW = 136
+
+
+def windows_kernel(main, above, below, got, sent, *refs, span, height, own, count):
+    outs, (tall, wide_top, ends, turn) = refs[:count], refs[count:]
+    line = lax.axis_index("gy")
     lane = lax.broadcasted_iota(jnp.int32, (SUBS, LANES), 1)
-    surf_ref[...] = jnp.zeros_like(surf_ref)
-    tops_ref[...] = jnp.zeros_like(tops_ref)
+    sub = lax.broadcasted_iota(jnp.int32, (SUBS, LANES), 0)
+    tall[...] = jnp.zeros_like(tall)
+    ends[...] = jnp.zeros_like(ends)
     turn[...] = jnp.zeros_like(turn)
+    for f in range(5):
+        tall[f, SUBS : SUBS + height] = main[f * height : (f + 1) * height, :]
+        tall[f, SUBS - 3 : SUBS] = above[3 * f : 3 * f + 3, :]
+        tall[f, SUBS + height : SUBS + height + 3] = below[3 * f : 3 * f + 3, :]
+    turn[LANES - 3 :, :] = got[:3, span : span + LANES]
+    turn[:3, :] = got[3:6, span : span + LANES]
+    block = turn[...].T
+    last = line == count - 1
+    for f in range(2):
+        before, after = block[2 * f * SUBS :], block[2 * (2 + f) * SUBS :]
+        beside = rim(before[:SUBS], after[:SUBS], lane, 2)
+        beyond = rim(before[SUBS : 2 * SUBS], after[SUBS : 2 * SUBS], lane, 2)
+        beyond = jnp.where(last, beyond[2:4], beyond[:2])
+        for j in (0, count + 1):
+            wide_top[f, j] = beside
+            ends[j, 2 * f : 2 * f + 2] = beyond
+        for j in range(count):
+            src = 5 * height + (f * count + j) * own
+            wide_top[f, j + 1] = main[src : src + own, :]
+            at = EDGE_ROWS + 2 * (f * count + j)
+            ends[j + 1, 2 * f : 2 * f + 2] = jnp.where(last, above[at : at + 2, :], below[at : at + 2, :])
     for s in range(count):
-        main, extra = mains[s], strips[s]
-        who = (lax.axis_index("gy") - s) % count
+        who, out = (line + s) % count, outs[s]
+        for f in range(5):
+            first = pl.multiple_of(who * SUBS, SUBS)
+            out[2 * f * SUBS : (2 * f + 1) * SUBS, :] = tall[f, pl.ds(first + SUBS, SUBS), :]
+            out[(2 * f + 1) * SUBS : (2 * f + 2) * SUBS, :] = ring(
+                tall[f, pl.ds(first, SUBS), :], tall[f, pl.ds(first + 2 * SUBS, SUBS), :], sub
+            )
+        for f in range(2):
+            out[(10 + f) * SUBS : (11 + f) * SUBS, :] = wide_top[f, who + 1]
+            out[(12 + f) * SUBS : (13 + f) * SUBS, :] = rim(wide_top[f, who], wide_top[f, who + 2], lane, 2)
+        mid, side = ends[who + 1], rim(ends[who], ends[who + 2], lane, 2)
+        out[14 * SUBS : 14 * SUBS + 4, :] = mid[:4]
+        out[14 * SUBS + 4 : 15 * SUBS, :] = side[:4]
+        for j in range(2):
+            cut = slice(span + (j + 1) * LANES, span + (j + 2) * LANES)
+            at = (15 + j) * SUBS
+            out[at : at + 3, :] = jnp.where(last, got[:3, cut], sent[:3, cut])
+            out[at + 3 : at + 6, :] = jnp.where(line == 0, got[3:6, cut], sent[3:6, cut])
+            out[at + 6 : at + SUBS, :] = jnp.zeros((2, LANES), jnp.float32)
+
+
+def windows(main, above, below, got, sent, span, height, own, count):
+    def body(*refs):
+        windows_kernel(*refs, span=span, height=height, own=own, count=count)
+
+    return pl.pallas_call(
+        body,
+        out_shape=[pltpu.VMEM((WINDOW, LANES), jnp.float32)] * count,
+        scratch_shapes=[
+            pltpu.VMEM((5, height + 2 * SUBS, LANES), jnp.float32),
+            pltpu.VMEM((2, count + 2, own, LANES), jnp.float32),
+            pltpu.VMEM((count + 2, SUBS, LANES), jnp.float32),
+            pltpu.VMEM((LANES, LANES), jnp.float32),
+        ],
+        name="windows",
+    )(*near(main, above, below, got, sent))
+
+
+def assemble(main, above, below, sent, strip, tile, tops, turn, flat, own):
+    count = len(sent)
+    line = lax.axis_index("gy")
+    _, _, width = strip.shape
+    _, rows, _ = tile.shape
+    cols, height = width - LANES, rows - SUBS
+    sub = lax.broadcasted_iota(jnp.int32, (SUBS, LANES), 0)
+    turn[...] = jnp.zeros_like(turn)
+    tops[:, height:, :] = jnp.zeros((2, SUBS, 2 * LANES), jnp.float32)
+    for f in range(5):
+        tile[f, height:, :LANES] = jnp.zeros((SUBS, LANES), jnp.float32)
+        tile[f, :height, :LANES] = main[f * height : (f + 1) * height, :]
+        tile[f, height : height + 3, :LANES] = below[3 * f : 3 * f + 3, :]
+        tile[f, rows - 3 :, :LANES] = above[3 * f : 3 * f + 3, :]
+    for s in range(count):
+        part = sent[s]
+        who = (line - s) % count
         at = pl.multiple_of(who * LANES, LANES)
         first = pl.multiple_of(who * own, own)
-        above, below = 0, strip
         for f in range(5):
-            surf_ref[f, :height, pl.ds(at, LANES)] = main[f * height : (f + 1) * height, :]
-            surf_ref[f, height : height + 3, pl.ds(at, LANES)] = extra[below + 3 * f : below + 3 * f + 3, :]
-            surf_ref[f, rows - 3 :, pl.ds(at, LANES)] = extra[above + 3 * f : above + 3 * f + 3, :]
+            strip[f, :, pl.ds(at, LANES)] = part[2 * f * SUBS : (2 * f + 2) * SUBS, :]
         for f in range(2):
-            for j in range(n):
-                src = 5 * height + (f * n + j) * own
-                tops_ref[f, pl.ds(first, own), j * LANES : (j + 1) * LANES] = main[src : src + own, :]
-        turn[LANES - 3 :, :LANES] = extra[2 * strip : 2 * strip + 3, :]
-        turn[:3, :LANES] = extra[2 * strip + 3 : 2 * strip + 6, :]
-        block = turn[:, :LANES].T
-        for f in range(2):
-            after = block[2 * (2 + f) * SUBS :][: 2 * SUBS]
-            before = block[2 * f * SUBS :][: 2 * SUBS]
-            two = jnp.where(lane >= LANES - 2, before[:SUBS], jnp.where(lane < 2, after[:SUBS], 0.0))
-            more = jnp.where(lane >= LANES - 2, before[SUBS:], jnp.where(lane < 2, after[SUBS:], 0.0))
-            tops_ref[f, pl.ds(first, own), cols:] = two
-
-            @pl.when(who == 0)
-            def _(f=f, more=more, extra=extra):
-                tops_ref[f, height : height + 2, cols:] = more[:2]
-                for j in range(n):
-                    src = below + EDGE_ROWS + 2 * (f * n + j)
-                    tops_ref[f, height : height + 2, j * LANES : (j + 1) * LANES] = extra[src : src + 2, :]
-
-            @pl.when(who == count - 1)
-            def _(f=f, more=more, extra=extra):
-                tops_ref[f, rows - 2 :, cols:] = more[2:4]
-                for j in range(n):
-                    src = above + EDGE_ROWS + 2 * (f * n + j)
-                    tops_ref[f, rows - 2 :, j * LANES : (j + 1) * LANES] = extra[src : src + 2, :]
+            tops[f, pl.ds(first, own), :LANES] = part[(10 + f) * SUBS : (11 + f) * SUBS, :]
+            tops[f, pl.ds(first, own), LANES:] = part[(12 + f) * SUBS : (13 + f) * SUBS, :]
+
+        @pl.when(who == 0)
+        def _(part=part):
+            for f in range(2):
+                tops[f, height : height + 2, :LANES] = part[14 * SUBS + 2 * f : 14 * SUBS + 2 * f + 2, :]
+                tops[f, height : height + 2, LANES:] = part[14 * SUBS + 4 + 2 * f : 14 * SUBS + 6 + 2 * f, :]
+            for j in range(2):
+                turn[0, :3, j * LANES : (j + 1) * LANES] = part[(15 + j) * SUBS + 3 : (15 + j) * SUBS + 6, :]
 
         @pl.when(who == count - 1)
-        def _(extra=extra):
-            for j in range(1, turn.shape[1] // LANES):
-                src = 2 * strip + j * SUBS
-                turn[LANES - 3 :, j * LANES : (j + 1) * LANES] = extra[src : src + 3, :]
-
-        @pl.when(who == 0)
-        def _(extra=extra):
-            for j in range(1, turn.shape[1] // LANES):
-                src = 2 * strip + j * SUBS
-                turn[:3, j * LANES : (j + 1) * LANES] = extra[src + 3 : src + 6, :]
-
-    block = turn[:, LANES:].T
+        def _(part=part):
+            for f in range(2):
+                tops[f, rows - 2 :, :LANES] = part[14 * SUBS + 2 * f : 14 * SUBS + 2 * f + 2, :]
+                tops[f, rows - 2 :, LANES:] = part[14 * SUBS + 4 + 2 * f : 14 * SUBS + 6 + 2 * f, :]
+            for j in range(2):
+                turn[0, LANES - 3 :, j * LANES : (j + 1) * LANES] = part[(15 + j) * SUBS : (15 + j) * SUBS + 3, :]
+
+    for j in range(2):
+        cut = slice(j * LANES, (j + 1) * LANES)
+        turn[1, LANES - 3 :, cut] = sent[1 % count][(15 + j) * SUBS : (15 + j) * SUBS + 3, :]
+        turn[1, :3, cut] = sent[-1][(15 + j) * SUBS + 3 : (15 + j) * SUBS + 6, :]
+    beside = turn[1].T
+    flat[...] = turn[0].T
+    first = pl.multiple_of(line * own, SUBS)
+    before = pl.multiple_of(jnp.where(line > 0, line * own - SUBS, height), SUBS)
     for f in range(5):
-        surf_ref[f, :, cols:] = block[f * tall : (f + 1) * tall]
-
-
-def last_kernel(
-    tab_ref, surf_ref, tops_ref, top_ref, class_ref, next_ref, head_out, water_ref,
-    ex_ref, w_ref, new_ref, sem, own,
-):
-    _, rows, width = surf_ref.shape
-    block_rows, block_cols = rows - SUBS, width - LANES
+        tile[f, :, LANES:] = beside[f * rows : (f + 1) * rows]
+        strip[f, :own, cols:] = flat[pl.ds(first + f * rows, SUBS), :]
+        strip[f, own:, cols:] = ring(flat[pl.ds(before + f * rows, SUBS), :], flat[pl.ds(first + f * rows + SUBS, SUBS), :], sub)
+
+
+def flow(fields, top, conduct, row_flags, col_flags, own_rows, own_cols):
+    water, level, convey, land, rain = fields
+    rows, width = water.shape
     r = lax.broadcasted_iota(jnp.int32, (rows, width), 0)
     c = lax.broadcasted_iota(jnp.int32, (rows, width), 1)
-    ok = place()
-    group, groups, line = lax.axis_index("grp"), lax.axis_size("grp"), lax.axis_index("gy")
-    more = [jnp.where(t, 1, 0) for t in (group > 0, group < groups - 1)]
-    row_ok = jnp.where(r < block_rows, 1, jnp.where(r >= rows - 3, more[0], jnp.where(r < block_rows + 3, more[1], 0)))
-    col_ok = jnp.where(c < block_cols, 1, jnp.where(c >= width - 3, ok[2], jnp.where(c < block_cols + 3, ok[3], 0)))
-    inside = (row_ok * col_ok).astype(jnp.float32)
-    level = surf_ref[1]
-    convey = jnp.sqrt(surf_ref[2]) * inside
-    leak = surf_ref[3]
-    rain = surf_ref[4]
-    top = tops_ref[0]
-
-    def across(x):
-        return pltpu.roll(x, rows - 1, 0)
-
-    def along(x):
-        return pltpu.roll(x, width - 1, 1)
-
-    gates = [convey * across(convey), convey * along(convey)]
-    parts = []
-    for ch in chunks(width):
-        _, _, root = closure(params(tab_ref, tops_ref[1, :, ch].astype(jnp.int32)), top[:, ch])
-        parts.append(0.25 * root * root)
-    leak = leak * jnp.concatenate(parts, axis=1)
-    water = surf_ref[0]
+    row_ok = jnp.where(r < own_rows, 1, jnp.where(r >= rows - 3, row_flags[0], jnp.where(r < own_rows + 3, row_flags[1], 0)))
+    col_ok = jnp.where(c < own_cols, 1, jnp.where(c >= width - 3, col_flags[0], jnp.where(c < own_cols + 3, col_flags[1], 0)))
+    root = jnp.sqrt(convey) * (row_ok * col_ok).astype(jnp.float32)
+    leak = land * conduct
+    ahead = [lambda x: pltpu.roll(x, rows - 1, 0), lambda x: pltpu.roll(x, width - 1, 1)]
+    gates = [root * f(root) for f in ahead]
     exchange = jnp.zeros_like(water)
     for _ in range(PASSES):
         surface = level + water
         power = jnp.where(water > 0.0, jnp.exp2((5.0 / 3.0) * jnp.log2(jnp.maximum(water, 1e-30))), 0.0)
         outflow = jnp.zeros_like(water)
-        for axis, gate, beside in ((0, gates[0], across), (1, gates[1], along)):
-            slope = surface - beside(surface)
-            carried = jnp.where(slope >= 0.0, power, beside(power))
-            flux = gate * carried * slope * lax.rsqrt(jnp.maximum(jnp.abs(slope), SLOPE_FLOOR))
+        for axis in range(2):
+            slope = surface - ahead[axis](surface)
+            carried = jnp.where(slope >= 0.0, power, ahead[axis](power))
+            flux = gates[axis] * carried * slope * lax.rsqrt(jnp.maximum(jnp.abs(slope), SLOPE_FLOOR))
             outflow = outflow + flux - pltpu.roll(flux, 1, axis)
         rate = leak * (water - top)
         exchange = exchange + SURFACE_STEP * rate
         water = jnp.maximum(water + SURFACE_STEP * (rain - rate - outflow), 0.0)
-    ex_ref[...] = exchange
-    w_ref[...] = water
-    if water_ref.shape[1] % LANES:
-        water_ref[...] = w_ref[:block_rows, :block_cols]
-    else:
-        mine = pl.multiple_of(line * water_ref.shape[1], LANES)
-        water_ref[...] = w_ref[:block_rows, pl.ds(mine, water_ref.shape[1])]
-    first = pl.multiple_of(line * own, SUBS)
-    after = pl.multiple_of(line * own + own, SUBS)
-    before = pl.multiple_of(jnp.where(line > 0, line * own - SUBS, block_rows), SUBS)
-    sub = lax.broadcasted_iota(jnp.int32, (SUBS, width), 0)
-    rim = jnp.where(sub == SUBS - 1, ex_ref[pl.ds(before, SUBS), :], jnp.where(sub == 0, ex_ref[pl.ds(after, SUBS), :], 0.0))
-    gain = jnp.concatenate([ex_ref[pl.ds(first, own), :], rim], axis=0)
-    mask = soil_mask(ok, own + SUBS, width, own, block_cols)
+    return water, exchange
+
+
+def last_kernel(tab_ref, strip, tile, tops, top_ref, class_ref, next_ref, head_out, water_ref, new_ref, sem):
+    own = new_ref.shape[1]
+    _, rows, width = strip.shape
+    cols = width - LANES
+    height, across = water_ref.shape
+    ok = place()
+    group, groups = lax.axis_index("grp"), lax.axis_size("grp")
+    column = lax.axis_index("gx") * lax.axis_size("gy") + lax.axis_index("gy")
+    columns_all = lax.axis_size("gx") * lax.axis_size("gy")
+
+    def flags(*tests):
+        return [jnp.where(t, 1, 0) for t in tests]
+
+    root = top_ref[4]
+    _, gain = flow([strip[f] for f in range(5)], top_ref[3], 0.25 * root * root, ok[:2], ok[2:], own, cols)
+    mask = soil_mask(ok, rows, width, own, cols)
     p = top_ref[0] + gain * top_ref[1]
     content, capacity, root = wide([closure(params(tab_ref, class_ref[:, ch]), p[:, ch]) for ch in chunks(width)])
     h = root * mask
     q = h * p
     low, low_q, low_n, low_d, weights, flows = (next_ref[i] for i in range(6))
 
-    def tile(x):
-        return x[:own, :block_cols]
-
-    top_n = tile(capacity * p - (content - top_ref[2]) + gain + h * lateral(q)) + tile(h) * (low_q - GRAVITY_STEP * low)
-    new_ref[0] = top_n / (tile(capacity + h * lateral(h)) + tile(h) * low)
-    low_n = low_n + low * (flows + tile(q) + GRAVITY_STEP * tile(h))
-    new_ref[1] = low_n / (low_d + low * (weights + tile(h)))
+    def inner(x):
+        return x[:own, :cols]
+
+    top_n = inner(capacity * p - (content - top_ref[2]) + gain + h * lateral(q)) + inner(h) * (low_q - GRAVITY_STEP * low)
+    new_ref[0] = top_n / (inner(capacity + h * lateral(h)) + inner(h) * low)
+    low_n = low_n + low * (flows + inner(q) + GRAVITY_STEP * inner(h))
+    new_ref[1] = low_n / (low_d + low * (weights + inner(h)))
     copy = pltpu.make_async_copy(new_ref, head_out.at[:TOP_LAYERS], sem)
     copy.start()
+    roots = [closure(params(tab_ref, tops[1, :, ch].astype(jnp.int32)), tops[0, :, ch])[2] for ch in chunks(tile.shape[2])]
+    root = jnp.concatenate(roots, axis=1)
+    water, _ = flow(
+        [tile[f] for f in range(5)], tops[0], 0.25 * root * root,
+        flags(group > 0, group < groups - 1), flags(column > 0, column < columns_all - 1), height, across,
+    )
+    water_ref[...] = water[:height, :across]
     copy.wait()
 
 
-def finish(tables, fields, tops, head, block, count):
-    own = head.shape[1]
+def finish(tables, fields, tops, head, water, count):
+    _, own, cols = head.shape
+    height, across = water
     whole = count == 0
-    rows, width = block[0] + SUBS, block[1] + LANES
+    rows, width, high, broad = own + SUBS, cols + LANES, height + SUBS, across + LANES
     n = len(fields)
 
-    def body(tab_ref, *refs):
-        given, known, (head_out, water_ref), (box, turn), rest = refs[:n], refs[n : n + 3], refs[n + 4 : n + 6], refs[n + 6 : n + 8], refs[n + 8 :]
+    def body(*refs):
+        tab_ref, given, known, (head_out, water_ref) = refs[0], refs[1 : 1 + n], refs[1 + n : 4 + n], refs[5 + n : 7 + n]
+        rest = refs[7 + n :]
         if whole:
-            surf, tops = given
+            strip, tile, above = given
         else:
-            surf, tops = box
-            cut = given[0].shape[0] - 2 * (EDGE_ROWS + 4 * block[1] // LANES) - turn.shape[1] // LANES * SUBS
-            assemble([x.at[:cut] for x in given], [x.at[cut:] for x in given], surf, tops, turn, own, block[0], count)
-        last_kernel(tab_ref, surf, tops, *known, head_out, water_ref, *rest, own=own)
-
-    def scratch_body(*refs):
-        cut = 1 + n + 6
-        body(*refs[:cut], refs[cut : cut + 2], refs[cut + 2], *refs[cut + 3 :])
-
-    tall = LANES + 5 * (block[0] + SUBS)
-    tall += -tall % LANES
-    small = (1, SUBS, LANES)
+            strip, tile, above = rest[2:5]
+            assemble(*given[:3], given[3:], strip, tile, above, *rest[5:], own)
+        last_kernel(tab_ref, strip, tile, above, *known, head_out, water_ref, *rest[:2])
+
     vmem = pl.BlockSpec(memory_space=pltpu.VMEM)
-    water = block if whole else (block[0], LANES)
+    scratch = [pltpu.VMEM((TOP_LAYERS, own, cols), jnp.float32), pltpu.SemaphoreType.DMA]
+    if not whole:
+        scratch += [
+            pltpu.VMEM(shape, jnp.float32)
+            for shape in ((5, rows, width), (5, high, broad), (2, high, broad), (2, LANES, 2 * LANES), (2 * LANES, LANES))
+        ]
     return pl.pallas_call(
-        scratch_body,
-        out_shape=(
-            jax.ShapeDtypeStruct(head.shape, jnp.float32),
-            jax.ShapeDtypeStruct(water, jnp.float32),
-        ),
+        body,
+        out_shape=(jax.ShapeDtypeStruct(head.shape, jnp.float32), jax.ShapeDtypeStruct(water, jnp.float32)),
         in_specs=[vmem] * (n + 4) + [pl.BlockSpec(memory_space=pl.ANY)],
         out_specs=[pl.BlockSpec(memory_space=pl.ANY), vmem],
-        scratch_shapes=[
-            pltpu.VMEM(small if whole else (5, rows, width), jnp.float32),
-            pltpu.VMEM(small if whole else (2, rows, width), jnp.float32),
-            pltpu.VMEM((SUBS, LANES) if whole else (LANES, tall), jnp.float32),
-            pltpu.VMEM((rows, width), jnp.float32),
-            pltpu.VMEM((rows, width), jnp.float32),
-            pltpu.VMEM((TOP_LAYERS, own, block[1]), jnp.float32),
-            pltpu.SemaphoreType.DMA,
-        ],
+        scratch_shapes=scratch,
         input_output_aliases={n + 4: 0},
         name="surface_and_top",
-    )(tables, *fields, *tops, head)
+    )(*near(tables, *fields, *tops), head)
 
 
 def lane_rows(size):
@@ -711,17 +800,26 @@
         high = t[-1, :, :, own + 2 :].transpose(0, 2, 1)
         return jnp.concatenate([mid, low, jnp.zeros((2, 4, 2), jnp.float32), high], axis=1)
 
-    return blocks, jnp.concatenate(
+    top_blocks = jnp.concatenate(
         [f_tops, tops_edge(1), jnp.zeros((2, height, LANES - 4), jnp.float32), tops_edge(0)], axis=2
     )
+    line = lax.axis_index("gy")
+
+    def around(first, length, total, room):
+        spot = jnp.arange(room)
+        return (first + jnp.where(spot < length + 3, spot, spot - room)) % total
+
+    strip = jnp.take(blocks, around(line * own, own, height, own + SUBS), axis=1)
+    across = around(line * scols, scols, cols + LANES, -(-(scols + 6) // LANES) * LANES)
+    return strip, jnp.take(blocks, across, axis=2), jnp.take(top_blocks, across, axis=2)
 
 
 def local(
     pressure, soil_class, capacity_range, inverse_entry, shape_index, conductivity,
     depth, elevation, roughness, rain, land_mask, channel_mask,
 ):
-    ny, iy = lax.axis_size("gy"), lax.axis_index("gy")
-    _, own, cols = pressure.shape
+    ny = lax.axis_size("gy")
+    _, own, _ = pressure.shape
     srows, scols = depth.shape
     ground = (depth, elevation, roughness, rain, land_mask, channel_mask)
     classes = (capacity_range, inverse_entry, shape_index, conductivity)
@@ -735,28 +833,27 @@
         below = shift(strip_before, "grp", -1)
         surface = (main, above, below)
     rows = ("grp", "gy")
-    sent = columns(pressure, soil_class, shift(after_end, rows, 1), shift(before_end, rows, -1), surface)
+    up_end = shift(after_end, rows, 1)
+    down_end = shift(before_end, rows, -1)
+    sent = columns(pressure, soil_class, up_end, down_end, surface)
     up = shift(after, rows, 1)
     down = shift(before, rows, -1)
     span = pressure.shape[0] * (own + SUBS)
     half = jnp.where(lax.broadcasted_iota(jnp.int32, sent.shape, 1) < span, 4, 3)
     got = gx_trade(sent, lax.broadcasted_iota(jnp.int32, sent.shape, 0) < half)
     if even:
-        strip = jnp.concatenate([above, below] + [got[:, ch] for ch in chunks(sent.shape[1])[span // LANES :]], axis=0)
-        strip = jnp.concatenate([main, strip], axis=0)
-        fields = [strip] + [shift(strip, "gy", step) for step in range(1, ny)]
+        outs = windows(main, above, below, got, sent, span, srows, own, ny)
+        fields = [main, above, below, outs[0]] + [shift(outs[step], "gy", step) for step in range(1, ny)]
     else:
         fields = block_general(pressure, soil_class, *ground)
     head, *tops = soil_interior(tables, pressure, soil_class, up, down, got, sent)
-    head, water = finish(tables, fields, tops, head, (srows, cols), ny if even else 0)
-    if not even:
-        water = lax.dynamic_slice_in_dim(water, iy * scols, scols, axis=1)
-    return head, water
+    return finish(tables, fields, tops, head, (srows, scols), ny if even else 0)
 
 
 def solution(mesh):
     soil = P(None, ("grp", "gy"), "gx")
     ground = P("grp", ("gx", "gy"))
+
     return jax.shard_map(
         local,
         mesh=mesh,

time: 40.7 us -> 34.7 us (0.85)
  Pallas kernels: 15.5 us -> 10.7 us
  local copies, waits for them, and re-layouts: 4.34 us -> 0 us
  waiting for transfers between devices: 2.24 us -> 5.85 us
    unnamed x29 -> x0, local copies, waits for them, and re-layouts: 4.34 us -> none
    ppermute x10, waiting for transfers between devices: 2.24 us -> 5.85 us  [shift(): return lax.ppermute(x, axis, [(i, (i + step) % size) for i in range(size)])]
    pallas_call x3 -> x4, Pallas kernels: 8.18 us -> 4.98 us  [the longest x1 2.15 us: finish(): pl.pallas_call(body, out_shape=(jax.ShapeDtypeStruct(head.shape, jnp.floa...]
    pallas_call x1, Pallas kernels: 7.29 us -> 5.68 us  [soil_interior(): pl.pallas_call(soil_kernel, out_shape=(jax.ShapeDtypeStruct(pressure.shap...]
  transfers between devices with their start and end apart: 10 -> 10, of which waited for: 2 -> 3; matrix products, arithmetic and copies ran while one was open for 4% -> 0% of each run, Pallas kernels for 23% -> 21%
where the time goes in v5:
time: 34.7 us; the launch traced here: 34.5 us
  starting transfers between devices  17.3 us (50%)
  Pallas kernels  10.7 us (31%)
  waiting for transfers between devices  5.85 us (17%)
  between operations  0.7 us (2%)
    ppermute x10, starting transfers between devices, shift(): return lax.ppermute(x, axis, [(i, (i + step) % size) for i in range(size)])  17.3 us
    ppermute x10, waiting for transfers between devices, shift(): return lax.ppermute(x, axis, [(i, (i + step) % size) for i in range(size)])  5.85 us
    pallas_call x1, Pallas kernels, soil_interior(): pl.pallas_call(soil_kernel, out_shape=(jax.ShapeDtypeStruct(pressure.shap...  5.68 us
    pallas_call x1, Pallas kernels, finish(): pl.pallas_call(body, out_shape=(jax.ShapeDtypeStruct(head.shape, jnp.floa...  2.15 us
    pallas_call x1, Pallas kernels, columns(): pl.pallas_call(body, out_shape=pltpu.VMEM((SUBS, width), jnp.float32), in...  1.43 us
    pallas_call x1, Pallas kernels, pack(): pl.pallas_call(body, out_shape=[pltpu.VMEM((SUBS, LANES), f32)] + out, in...  1.29 us
  transfers between devices with their start and end apart: 10, of which 3 were waited for; matrix products, arithmetic and copies ran while one was open for 0% of the time, Pallas kernels for 21%

profile of v5, /device:TPU:0, one launch (start us, length us, event | category | flops | bytes accessed | tf_op | source)
XLA Modules:
  0.0 34.5 jit_solution(5716742695239501459)
XLA Ops:
  0.6 1.3 %pack.1 = (f32[8,128]{1,0:T(8,128)S(1)}, f32[224,128]{1,0:T(8,128)S(1)}, f32[32,128]{1,0:T(8,128)S(1)}, f32[32,128]{1,0:T(8,128)S(1)}, f32[2,2,24,512]{3,2,1,0:T...) custom-call(f32[12]{0:T(128)} %refs_0_.2, f32[12]{0:T(128)} %refs_1_.2, ...), custom_call_target="tpu_custom_call" | custom-call | tf_op jit(solution)/shard_map/pack/pallas_call | solution.py:414
  1.9 3.1 %collective-permute-start.8 = (f32[2,2,24,512]{3,2,1,0:T(8,128)S(1)}, f32[2,2,24,512]{3,2,1,0:T(8,128)S(1)}, u32[]{:S(2)}, u32[]{:S(2)}) collective-permute-start(f32[2,2,24,512]{3,2,1,0:T(8,128)S(1)} %get-tuple-element.28), channel_id=1, source_target_pairs={{0,1},{1,2},{2,3},{3,8},{8,9},{9,10},{10,11},{11,16},{16,17},{17,1... | collective-permute-start | bytes 589832 | tf_op jit(solution)/shard_map/ppermute | solution.py:25
  5.0 2.5 %collective-permute-start.9 = (f32[2,2,24,512]{3,2,1,0:T(8,128)S(1)}, f32[2,2,24,512]{3,2,1,0:T(8,128)S(1)}, u32[]{:S(2)}, u32[]{:S(2)}) collective-permute-start(f32[2,2,24,512]{3,2,1,0:T(8,128)S(1)} %get-tuple-element.29), channel_id=1, source_target_pairs={{0,27},{1,0},{2,1},{3,2},{8,3},{9,8},{10,9},{11,10},{16,11},{17,16... | collective-permute-start | bytes 589832 | tf_op jit(solution)/shard_map/ppermute | solution.py:25
  7.5 0.0 collective-permute-start
  7.5 0.0 collective-permute-start.2
  7.5 4.4 %collective-permute-start.3 = (f32[2,24,128]{2,1,0:T(8,128)S(1)}, f32[2,24,128]{2,1,0:T(8,128)S(1)}, u32[]{:S(2)}, u32[]{:S(2)}) collective-permute-start(f32[2,24,128]{2,1,0:T(8,128)S(1)} %get-tuple-element.23), channel_id=1, source_target_pairs={{0,27},{1,0},{2,1},{3,2},{8,3},{9,8},{10,9},{11,10},{16,11},{17,16... | collective-permute-start | bytes 73736 | tf_op jit(solution)/shard_map/ppermute | solution.py:25
  12.0 0.0 collective-permute-done.refs_5_.refs_1_.refs_2_
  12.0 0.8 %collective-permute-start.1 = (f32[32,128]{1,0:T(8,128)S(1)}, f32[32,128]{1,0:T(8,128)S(1)}, u32[]{:S(2)}, u32[]{:S(2)}) collective-permute-start(f32[32,128]{1,0:T(8,128)S(1)} %get-tuple-element.21), channel_id=1, source_target_pairs={{0,24},{8,0},{16,8},{24,16},{1,25},{9,1},{17,9},{25,17},{2,26},{10... | collective-permute-start | bytes 49160 | tf_op jit(solution)/shard_map/ppermute | solution.py:25
  12.8 1.4 %collective-permute-done.1.refs_6_.refs_2_.refs_3_ = f32[32,128]{1,0:T(8,128)S(1)} collective-permute-done((f32[32,128]{1,0:T(8,128)S(1)}, f32[32,128]{1,0:T(8,128)S(1)}, u32[]{:S(2)}, u32[]{:S(2)}) %collective-permute-start.1) | collective-permute-done | bytes 16416 | tf_op jit(solution)/shard_map/ppermute | solution.py:25
  14.2 2.6 %collective-permute-done.2.refs_2_ = f32[2,24,128]{2,1,0:T(8,128)S(1)} collective-permute-done((f32[2,24,128]{2,1,0:T(8,128)S(1)}, f32[2,24,128]{2,1,0:T(8,128)S(1)}, u32[]{:S(2)}, u32[]{:S(2)}) %collective-permute-start.2) | collective-permute-done | bytes 24608 | tf_op jit(solution)/shard_map/ppermute | solution.py:25
  16.8 0.0 collective-permute-done.3.refs_3_
  16.8 1.4 %columns.1.refs_4_.sent_in = f32[8,768]{1,0:T(8,128)S(1)} custom-call(f32[24,8,512]{2,1,0:T(8,128)} %p_far.1, s32[24,8,512]{2,1,0:T(8,128)} %c_far.1, f32[2,24,128]{2,1,0:T(8,128)S(1)} %collective-permute-done.2.refs_2_, f32[2,24,128]{2,1,0:T(8,128)S(1)} %collective-permute-done.3.refs_3_, f32[224,128]{1,0:T(8,128)S(1)} %get-tuple-element.19.refs_4_.refs_0_.refs_1_, ...), custom_call_target="tpu_custom_call" | custom-call | tf_op jit(solution)/shard_map/columns/pallas_call | solution.py:473
  18.3 2.5 %collective-permute-start.4 = (f32[8,768]{1,0:T(8,128)S(1)}, f32[8,768]{1,0:T(8,128)S(1)}, u32[]{:S(2)}, u32[]{:S(2)}) collective-permute-start(f32[8,768]{1,0:T(8,128)S(1)} %columns.1.refs_4_.sent_in), channel_id=1, source_target_pairs={{0,4},{4,0},{1,5},{5,1},{2,6},{6,2},{3,7},{7,3},{8,12},{12,8},{9,1... | collective-permute-start | bytes 73736 | tf_op jit(solution)/shard_map/ppermute | solution.py:25
  20.8 1.8 %collective-permute-done.4.refs_3_.got_in = f32[8,768]{1,0:T(8,128)S(1)} collective-permute-done((f32[8,768]{1,0:T(8,128)S(1)}, f32[8,768]{1,0:T(8,128)S(1)}, u32[]{:S(2)}, u32[]{:S(2)}) %collective-permute-start.4) | collective-permute-done | bytes 24608 | tf_op jit(solution)/shard_map/ppermute | solution.py:25
  22.6 0.1 windows.1
  22.7 0.8 %collective-permute-start.5 = (f32[136,128]{1,0:T(8,128)S(1)}, f32[136,128]{1,0:T(8,128)S(1)}, u32[]{:S(2)}, u32[]{:S(2)}) collective-permute-start(f32[136,128]{1,0:T(8,128)S(1)} %get-tuple-element.25), channel_id=1, source_target_pairs={{0,1},{1,2},{2,3},{3,0},{4,5},{5,6},{6,7},{7,4},{8,9},{9,10},{10,1... | collective-permute-start | bytes 208904 | tf_op jit(solution)/shard_map/ppermute | solution.py:25
  23.5 1.6 %collective-permute-start.6 = (f32[136,128]{1,0:T(8,128)S(1)}, f32[136,128]{1,0:T(8,128)S(1)}, u32[]{:S(2)}, u32[]{:S(2)}) collective-permute-start(f32[136,128]{1,0:T(8,128)S(1)} %get-tuple-element.26), channel_id=1, source_target_pairs={{0,2},{1,3},{2,0},{3,1},{4,6},{5,7},{6,4},{7,5},{8,10},{9,11},{10,... | collective-permute-start | bytes 208904 | tf_op jit(solution)/shard_map/ppermute | solution.py:25
  25.0 1.6 %collective-permute-start.7 = (f32[136,128]{1,0:T(8,128)S(1)}, f32[136,128]{1,0:T(8,128)S(1)}, u32[]{:S(2)}, u32[]{:S(2)}) collective-permute-start(f32[136,128]{1,0:T(8,128)S(1)} %get-tuple-element.27), channel_id=1, source_target_pairs={{0,3},{1,0},{2,1},{3,2},{4,7},{5,4},{6,5},{7,6},{8,11},{9,8},{10,9... | collective-permute-start | bytes 208904 | tf_op jit(solution)/shard_map/ppermute | solution.py:25
  26.6 0.0 collective-permute-done.8.up_in
  26.6 0.0 collective-permute-done.9.down_in
  26.6 5.7 %soil_interior.1 = (f32[24,8,512]{2,1,0:T(8,128)}, f32[5,16,640]{2,1,0:T(8,128)S(1)}, s32[16,640]{1,0:T(8,128)S(1)}, f32[6,8,512]{2,1,0:T(8,128)S(1)}) custom-call(f32[8,128]{1,0:T(8,128)S(1)} %get-tuple-element.18.tab_ref.refs_0_, f32[24,8,512]{2,1,0:T(8,128)} %p_far.1, s32[24,8,512]{2,1,0:T(8,128)} %c_far.1, ...), custom_call_target="tpu_custom_call" | custom-call | tf_op jit(solution)/shard_map/soil_interior/pallas_call | solution.py:341
  32.3 0.0 collective-permute-done.5.refs_5_
  32.3 0.0 collective-permute-done.6.refs_6_
  32.3 0.0 collective-permute-done.7.refs_7_
  32.3 2.2 %surface_and_top.1 = (f32[24,8,512]{2,1,0:T(8,128)}, f32[32,128]{1,0:T(8,128)}) custom-call(f32[8,128]{1,0:T(8,128)S(1)} %get-tuple-element.18.tab_ref.refs_0_, f32[224,128]{1,0:T(8,128)S(1)} %get-tuple-element.19.refs_4_.refs_0_.refs_1_, f32[32,128]{1,0:T(8,128)S(1)} %collective-permute-done.refs_5_.refs_1_.refs_2_, ...), custom_call_target="tpu_custom_call", output_to_operand_aliasing={{0}: (11, {})} | custom-call | tf_op jit(solution)/shard_map/surface_and_top/pallas_call | solution.py:708
Async XLA Ops:
  1.9 24.7 %collective-permute-start.8 = (f32[2,2,24,512]{3,2,1,0:T(8,128)S(1)}, f32[2,2,24,512]{3,2,1,0:T(8,128)S(1)}, u32[]{:S(2)}, u32[]{:S(2)}) collective-permute-start(f32[2,2,24,512]{3,2,1,0:T(8,128)S(1)} %get-tuple-element.28), channel_id=1, source_target_pairs={{0,1},{1,2},{2,3},{3,8},{8,9},{9,10},{10,11},{11,16},{16,17},{17,1... | collective-permute-start | bytes 589832 | tf_op jit(solution)/shard_map/ppermute | solution.py:25
  5.0 21.5 %collective-permute-start.9 = (f32[2,2,24,512]{3,2,1,0:T(8,128)S(1)}, f32[2,2,24,512]{3,2,1,0:T(8,128)S(1)}, u32[]{:S(2)}, u32[]{:S(2)}) collective-permute-start(f32[2,2,24,512]{3,2,1,0:T(8,128)S(1)} %get-tuple-element.29), channel_id=1, source_target_pairs={{0,27},{1,0},{2,1},{3,2},{8,3},{9,8},{10,9},{11,10},{16,11},{17,16... | collective-permute-start | bytes 589832 | tf_op jit(solution)/shard_map/ppermute | solution.py:25
  7.5 4.4 %collective-permute-start = (f32[32,128]{1,0:T(8,128)S(1)}, f32[32,128]{1,0:T(8,128)S(1)}, u32[]{:S(2)}, u32[]{:S(2)}) collective-permute-start(f32[32,128]{1,0:T(8,128)S(1)} %get-tuple-element.20), channel_id=1, source_target_pairs={{0,8},{8,16},{16,24},{24,0},{1,9},{9,17},{17,25},{25,1},{2,10},{10... | collective-permute-start | bytes 49160 | tf_op jit(solution)/shard_map/ppermute | solution.py:25
  7.5 9.3 %collective-permute-start.2 = (f32[2,24,128]{2,1,0:T(8,128)S(1)}, f32[2,24,128]{2,1,0:T(8,128)S(1)}, u32[]{:S(2)}, u32[]{:S(2)}) collective-permute-start(f32[2,24,128]{2,1,0:T(8,128)S(1)} %get-tuple-element.22), channel_id=1, source_target_pairs={{0,1},{1,2},{2,3},{3,8},{8,9},{9,10},{10,11},{11,16},{16,17},{17,1... | collective-permute-start | bytes 73736 | tf_op jit(solution)/shard_map/ppermute | solution.py:25
  7.5 9.3 %collective-permute-start.3 = (f32[2,24,128]{2,1,0:T(8,128)S(1)}, f32[2,24,128]{2,1,0:T(8,128)S(1)}, u32[]{:S(2)}, u32[]{:S(2)}) collective-permute-start(f32[2,24,128]{2,1,0:T(8,128)S(1)} %get-tuple-element.23), channel_id=1, source_target_pairs={{0,27},{1,0},{2,1},{3,2},{8,3},{9,8},{10,9},{11,10},{16,11},{17,16... | collective-permute-start | bytes 73736 | tf_op jit(solution)/shard_map/ppermute | solution.py:25
  12.0 2.3 %collective-permute-start.1 = (f32[32,128]{1,0:T(8,128)S(1)}, f32[32,128]{1,0:T(8,128)S(1)}, u32[]{:S(2)}, u32[]{:S(2)}) collective-permute-start(f32[32,128]{1,0:T(8,128)S(1)} %get-tuple-element.21), channel_id=1, source_target_pairs={{0,24},{8,0},{16,8},{24,16},{1,25},{9,1},{17,9},{25,17},{2,26},{10... | collective-permute-start | bytes 49160 | tf_op jit(solution)/shard_map/ppermute | solution.py:25
  18.3 4.3 %collective-permute-start.4 = (f32[8,768]{1,0:T(8,128)S(1)}, f32[8,768]{1,0:T(8,128)S(1)}, u32[]{:S(2)}, u32[]{:S(2)}) collective-permute-start(f32[8,768]{1,0:T(8,128)S(1)} %columns.1.refs_4_.sent_in), channel_id=1, source_target_pairs={{0,4},{4,0},{1,5},{5,1},{2,6},{6,2},{3,7},{7,3},{8,12},{12,8},{9,1... | collective-permute-start | bytes 73736 | tf_op jit(solution)/shard_map/ppermute | solution.py:25
  22.7 9.6 %collective-permute-start.5 = (f32[136,128]{1,0:T(8,128)S(1)}, f32[136,128]{1,0:T(8,128)S(1)}, u32[]{:S(2)}, u32[]{:S(2)}) collective-permute-start(f32[136,128]{1,0:T(8,128)S(1)} %get-tuple-element.25), channel_id=1, source_target_pairs={{0,1},{1,2},{2,3},{3,0},{4,5},{5,6},{6,7},{7,4},{8,9},{9,10},{10,1... | collective-permute-start | bytes 208904 | tf_op jit(solution)/shard_map/ppermute | solution.py:25
  23.5 8.8 %collective-permute-start.6 = (f32[136,128]{1,0:T(8,128)S(1)}, f32[136,128]{1,0:T(8,128)S(1)}, u32[]{:S(2)}, u32[]{:S(2)}) collective-permute-start(f32[136,128]{1,0:T(8,128)S(1)} %get-tuple-element.26), channel_id=1, source_target_pairs={{0,2},{1,3},{2,0},{3,1},{4,6},{5,7},{6,4},{7,5},{8,10},{9,11},{10,... | collective-permute-start | bytes 208904 | tf_op jit(solution)/shard_map/ppermute | solution.py:25
  25.0 7.3 %collective-permute-start.7 = (f32[136,128]{1,0:T(8,128)S(1)}, f32[136,128]{1,0:T(8,128)S(1)}, u32[]{:S(2)}, u32[]{:S(2)}) collective-permute-start(f32[136,128]{1,0:T(8,128)S(1)} %get-tuple-element.27), channel_id=1, source_target_pairs={{0,3},{1,0},{2,1},{3,2},{4,7},{5,4},{6,5},{7,6},{8,11},{9,8},{10,9... | collective-permute-start | bytes 208904 | tf_op jit(solution)/shard_map/ppermute | solution.py:25

commit v6 on v5

--- a/solution.py
+++ b/solution.py
@@ -102,10 +102,12 @@
     return (in_rows * in_cols).astype(jnp.float32)
 
 
-def soil_rows(p_ref, c_ref, next_ref, prev_ref, next_end, prev_end):
+def soil_rows(p_ref, c_ref, blocks, next_ref, prev_ref, next_end, prev_end):
     layers, own, cols = p_ref.shape
     start = lax.broadcasted_iota(jnp.int32, (layers, LANES), 1) < LANES // 2
     for f, x in enumerate((p_ref, c_ref)):
+        blocks[f] = x[:, :, :LANES].astype(jnp.float32)
+        blocks[2 + f] = x[:, :, cols - LANES :].astype(jnp.float32)
         for r in range(2):
             next_ref[f, r] = x[:, own - 2 + r, :].astype(jnp.float32)
             prev_ref[f, r] = x[:, r, :].astype(jnp.float32)
@@ -113,13 +115,13 @@
         prev_end[f] = jnp.where(start, prev_ref[f, 0, :, :LANES], prev_ref[f, 0, :, cols - LANES :])
 
 
-def soil_columns(p_first, c_first, p_last, c_last, up_end, down_end, box):
-    layers, own, _ = p_first.shape
+def soil_columns(blocks, up_end, down_end, box):
+    _, layers, own, _ = blocks.shape
     rows = box.shape[1]
     out = []
-    for side in ((p_last, c_last), (p_first, c_first)):
+    for side in (2, 0):
         for f in range(2):
-            box[:, 2 : 2 + own, :] = side[f][...].astype(jnp.float32)
+            box[:, 2 : 2 + own, :] = blocks[side + f]
             box[:, 0, :] = jnp.zeros((layers, LANES), jnp.float32)
             box[:, 1, :] = up_end[f]
             box[:, own + 2, :] = down_end[f]
@@ -156,6 +158,34 @@
     for ref in (h_ref, q_ref, h2_ref, q2_ref):
         ref[0] = jnp.zeros((own, cols), f32)
         ref[layers + 1] = jnp.zeros((own, cols), f32)
+
+    gap = jnp.zeros((1, span), f32)
+    p = jnp.concatenate([got[0:2], sent[4:5], gap, sent[1:2], got[4:6], gap], axis=0)
+    kind = jnp.concatenate([got[2:4], sent[6:7], gap, sent[3:4], got[6:8], gap], axis=0).astype(jnp.int32)
+    sub = lax.broadcasted_iota(jnp.int32, (SUBS, span), 0)
+    lane = lax.broadcasted_iota(jnp.int32, (SUBS, span), 1)
+    row = lane % rows
+    row_ok = jnp.where(row < 2, ok[0], jnp.where(row < own + 2, 1, jnp.where(row < own + 4, ok[1], 0)))
+    col_ok = jnp.where(sub < 2, ok[2], jnp.where((sub == 2) | (sub == 4), 1, jnp.where((sub == 5) | (sub == 6), ok[3], 0)))
+    mask = (row_ok * col_ok).astype(f32)
+    values = [params(tab_ref, kind[:, ch]) for ch in chunks(span)]
+    content, capacity, root = wide([closure(v, p[:, ch]) for v, ch in zip(values, chunks(span))])
+    h, q = root * mask, root * mask * p
+
+    def over(x):
+        return jnp.where(lane < rows, 0.0, pltpu.roll(x, rows, 1))
+
+    def under(x):
+        return jnp.where(lane >= span - rows, 0.0, pltpu.roll(x, span - rows, 1))
+
+    weights = lateral(h) + over(h) + under(h)
+    flows = lateral(q) + over(q) + under(q) + GRAVITY_STEP * (over(h) - under(h))
+    p1 = (capacity * p + h * flows) / (capacity + h * weights)
+    root = wide([closure(v, p1[:, ch]) for v, ch in zip(values, chunks(span))])[2] * mask
+    turn[...] = jnp.zeros_like(turn)
+    for i, x in enumerate((h, q, root, root * p1)):
+        turn[i * SUBS : (i + 1) * SUBS, :] = x
+    corner[...] = turn[...].T.reshape(layers, rows, LANES)
 
     def first(z):
         for ch in chunks(cols):
@@ -178,34 +208,6 @@
         return carry
 
     lax.fori_loop(0, groups, first_group, 0)
-
-    gap = jnp.zeros((1, span), f32)
-    p = jnp.concatenate([got[0:2], sent[4:5], gap, sent[1:2], got[4:6], gap], axis=0)
-    kind = jnp.concatenate([got[2:4], sent[6:7], gap, sent[3:4], got[6:8], gap], axis=0).astype(jnp.int32)
-    sub = lax.broadcasted_iota(jnp.int32, (SUBS, span), 0)
-    lane = lax.broadcasted_iota(jnp.int32, (SUBS, span), 1)
-    row = lane % rows
-    row_ok = jnp.where(row < 2, ok[0], jnp.where(row < own + 2, 1, jnp.where(row < own + 4, ok[1], 0)))
-    col_ok = jnp.where(sub < 2, ok[2], jnp.where((sub == 2) | (sub == 4), 1, jnp.where((sub == 5) | (sub == 6), ok[3], 0)))
-    mask = (row_ok * col_ok).astype(f32)
-    values = [params(tab_ref, kind[:, ch]) for ch in chunks(span)]
-    content, capacity, root = wide([closure(v, p[:, ch]) for v, ch in zip(values, chunks(span))])
-    h, q = root * mask, root * mask * p
-
-    def over(x):
-        return jnp.where(lane < rows, 0.0, pltpu.roll(x, rows, 1))
-
-    def under(x):
-        return jnp.where(lane >= span - rows, 0.0, pltpu.roll(x, span - rows, 1))
-
-    weights = lateral(h) + over(h) + under(h)
-    flows = lateral(q) + over(q) + under(q) + GRAVITY_STEP * (over(h) - under(h))
-    p1 = (capacity * p + h * flows) / (capacity + h * weights)
-    root = wide([closure(v, p1[:, ch]) for v, ch in zip(values, chunks(span))])[2] * mask
-    turn[...] = jnp.zeros_like(turn)
-    for i, x in enumerate((h, q, root, root * p1)):
-        turn[i * SUBS : (i + 1) * SUBS, :] = x
-    corner[...] = turn[...].T.reshape(layers, rows, LANES)
 
     zsub = lax.broadcasted_iota(jnp.int32, (layers, cols), 0)
     zlane = lax.broadcasted_iota(jnp.int32, (layers, LANES), 1)
@@ -396,7 +398,7 @@
     f32 = jnp.float32
     edge = pltpu.VMEM((2, 2, layers, cols), f32)
     end = pltpu.VMEM((2, layers, LANES), f32)
-    out = [edge, edge, end, end]
+    out = [pltpu.VMEM((4, layers, own, LANES), f32), edge, edge, end, end]
     if ground:
         height = ground[0].shape[0]
         strip = pltpu.VMEM((EDGE_ROWS + 4 * cols // LANES, LANES), f32)
@@ -406,7 +408,7 @@
         tables, rest = refs[: len(classes)], refs[len(classes) :]
         if ground:
             surface_rows(*rest[: 2 + len(ground)], *rest[3 + len(ground) : 6 + len(ground)])
-        soil_rows(*rest[:2], *rest[-4:])
+        soil_rows(*rest[:2], *rest[-5:])
         rest[2 + len(ground)][...] = class_tables(tables)
 
     vmem = pl.BlockSpec(memory_space=pltpu.VMEM)
@@ -441,8 +443,8 @@
     return edges
 
 
-def columns(pressure, soil_class, up_end, down_end, surface):
-    layers, own, cols = pressure.shape
+def columns(blocks, cols, up_end, down_end, surface):
+    _, layers, own, _ = blocks.shape
     rows = own + SUBS
     span = layers * rows
     scratch = [pltpu.VMEM((layers, rows, LANES), jnp.float32)]
@@ -454,29 +456,20 @@
         width += tall
         scratch.append(pltpu.VMEM((tall, LANES), jnp.float32))
 
-    n = 4 + len(surface)
-    kinds = (pressure.dtype, soil_class.dtype)
+    n = 3 + len(surface)
 
     def body(*refs):
-        out_ref, box, ends, sems = refs[n], refs[n + 1], refs[-5:-1], refs[-1]
-        copies = [
-            pltpu.make_async_copy(refs[i % 2].at[:, :, pl.ds(i // 2 * (cols - LANES), LANES)], ends[i], sems.at[i]) for i in range(4)
-        ]
-        for copy in copies:
-            copy.start()
+        out_ref, box = refs[n], refs[n + 1]
+        out_ref[:, :span] = soil_columns(*refs[:3], box)
         if surface:
-            out_ref[:, span:] = surface_columns(*refs[4:n], refs[n + 2], height, own, cols)
-        for copy in copies:
-            copy.wait()
-        out_ref[:, :span] = soil_columns(*ends, *refs[2:4], box)
+            out_ref[:, span:] = surface_columns(*refs[3:n], refs[n + 2], height, own, cols)
 
     return pl.pallas_call(
         body,
         out_shape=pltpu.VMEM((SUBS, width), jnp.float32),
-        in_specs=[pl.BlockSpec(memory_space=pl.ANY)] * 2 + [pl.BlockSpec(memory_space=pltpu.VMEM)] * (2 + len(surface)),
-        scratch_shapes=scratch + [pltpu.VMEM((layers, own, LANES), k) for k in kinds * 2] + [pltpu.SemaphoreType.DMA((4,))],
+        scratch_shapes=scratch,
         name="columns",
-    )(pressure, soil_class, *near(up_end, down_end, *surface))
+    )(*near(blocks, up_end, down_end, *surface))
 
 
 def rim(at_end, at_start, lane, count):
@@ -819,13 +812,13 @@
     depth, elevation, roughness, rain, land_mask, channel_mask,
 ):
     ny = lax.axis_size("gy")
-    _, own, _ = pressure.shape
+    _, own, cols = pressure.shape
     srows, scols = depth.shape
     ground = (depth, elevation, roughness, rain, land_mask, channel_mask)
     classes = (capacity_range, inverse_entry, shape_index, conductivity)
     even = scols == LANES and own == SUBS
     tables, *packed = pack(pressure, soil_class, classes, ground if even else ())
-    after, before, after_end, before_end = packed[-4:]
+    blocks, after, before, after_end, before_end = packed[-5:]
     surface = ()
     if even:
         main, strip_after, strip_before = packed[:3]
@@ -835,7 +828,7 @@
     rows = ("grp", "gy")
     up_end = shift(after_end, rows, 1)
     down_end = shift(before_end, rows, -1)
-    sent = columns(pressure, soil_class, up_end, down_end, surface)
+    sent = columns(blocks, cols, up_end, down_end, surface)
     up = shift(after, rows, 1)
     down = shift(before, rows, -1)
     span = pressure.shape[0] * (own + SUBS)

time: 34.7 us -> 33.6 us (0.968)
  Pallas kernels: 10.7 us -> 9.58 us
    pallas_call x1, Pallas kernels: 1.43 us -> 0.42 us  [columns(): pl.pallas_call(body, out_shape=pltpu.VMEM((SUBS, width), jnp.float32), sc...]
  transfers between devices with their start and end apart: 10 -> 10, of which waited for: 3 -> 3; matrix products, arithmetic and copies ran while one was open for 0% -> 0% of each run, Pallas kernels for 21% -> 18%
where the time goes in v6:
time: 33.6 us; the launch traced here: 33.4 us
  starting transfers between devices  17.3 us (51%)
  Pallas kernels  9.58 us (29%)
  waiting for transfers between devices  5.85 us (17%)
  between operations  0.7 us (2%)
    ppermute x10, starting transfers between devices, shift(): return lax.ppermute(x, axis, [(i, (i + step) % size) for i in range(size)])  17.3 us
    ppermute x10, waiting for transfers between devices, shift(): return lax.ppermute(x, axis, [(i, (i + step) % size) for i in range(size)])  5.85 us
    pallas_call x1, Pallas kernels, soil_interior(): pl.pallas_call(soil_kernel, out_shape=(jax.ShapeDtypeStruct(pressure.shap...  5.57 us
    pallas_call x1, Pallas kernels, finish(): pl.pallas_call(body, out_shape=(jax.ShapeDtypeStruct(head.shape, jnp.floa...  2.15 us
    pallas_call x1, Pallas kernels, pack(): pl.pallas_call(body, out_shape=[pltpu.VMEM((SUBS, LANES), f32)] + out, in...  1.34 us
  transfers between devices with their start and end apart: 10, of which 3 were waited for; matrix products, arithmetic and copies ran while one was open for 0% of the time, Pallas kernels for 18%

profile of v6, /device:TPU:0, one launch (start us, length us, event | category | flops | bytes accessed | tf_op | source)
XLA Modules:
  0.0 33.4 jit_solution(15026234621422805515)
XLA Ops:
  0.6 1.3 %pack.1 = (f32[8,128]{1,0:T(8,128)S(1)}, f32[224,128]{1,0:T(8,128)S(1)}, f32[32,128]{1,0:T(8,128)S(1)}, f32[32,128]{1,0:T(8,128)S(1)}, f32[4,24,8,128]{3,2,1,0:T...) custom-call(f32[12]{0:T(128)} %refs_0_.1, ...), custom_call_target="tpu_custom_call" | custom-call | tf_op jit(solution)/shard_map/pack/pallas_call | solution.py:416
  2.0 3.1 %collective-permute-start.8 = (f32[2,2,24,512]{3,2,1,0:T(8,128)S(1)}, f32[2,2,24,512]{3,2,1,0:T(8,128)S(1)}, u32[]{:S(2)}, u32[]{:S(2)}) collective-permute-start(f32[2,2,24,512]{3,2,1,0:T(8,128)S(1)} %get-tuple-element.30), channel_id=1, source_target_pairs={{0,1},{1,2},{2,3},{3,8},{8,9},{9,10},{10,11},{11,16},{16,17},{17,1... | collective-permute-start | bytes 589832 | tf_op jit(solution)/shard_map/ppermute | solution.py:25
  5.1 2.5 %collective-permute-start.9 = (f32[2,2,24,512]{3,2,1,0:T(8,128)S(1)}, f32[2,2,24,512]{3,2,1,0:T(8,128)S(1)}, u32[]{:S(2)}, u32[]{:S(2)}) collective-permute-start(f32[2,2,24,512]{3,2,1,0:T(8,128)S(1)} %get-tuple-element.31), channel_id=1, source_target_pairs={{0,27},{1,0},{2,1},{3,2},{8,3},{9,8},{10,9},{11,10},{16,11},{17,16... | collective-permute-start | bytes 589832 | tf_op jit(solution)/shard_map/ppermute | solution.py:25
  7.6 0.0 collective-permute-start
  7.6 0.0 collective-permute-start.2
  7.6 4.4 %collective-permute-start.3 = (f32[2,24,128]{2,1,0:T(8,128)S(1)}, f32[2,24,128]{2,1,0:T(8,128)S(1)}, u32[]{:S(2)}, u32[]{:S(2)}) collective-permute-start(f32[2,24,128]{2,1,0:T(8,128)S(1)} %get-tuple-element.25), channel_id=1, source_target_pairs={{0,27},{1,0},{2,1},{3,2},{8,3},{9,8},{10,9},{11,10},{16,11},{17,16... | collective-permute-start | bytes 73736 | tf_op jit(solution)/shard_map/ppermute | solution.py:25
  12.0 0.0 collective-permute-done.refs_4_.refs_1_.refs_2_
  12.0 0.8 %collective-permute-start.1 = (f32[32,128]{1,0:T(8,128)S(1)}, f32[32,128]{1,0:T(8,128)S(1)}, u32[]{:S(2)}, u32[]{:S(2)}) collective-permute-start(f32[32,128]{1,0:T(8,128)S(1)} %get-tuple-element.22), channel_id=1, source_target_pairs={{0,24},{8,0},{16,8},{24,16},{1,25},{9,1},{17,9},{25,17},{2,26},{10... | collective-permute-start | bytes 49160 | tf_op jit(solution)/shard_map/ppermute | solution.py:25
  12.8 1.4 %collective-permute-done.1.refs_5_.refs_2_.refs_3_ = f32[32,128]{1,0:T(8,128)S(1)} collective-permute-done((f32[32,128]{1,0:T(8,128)S(1)}, f32[32,128]{1,0:T(8,128)S(1)}, u32[]{:S(2)}, u32[]{:S(2)}) %collective-permute-start.1) | collective-permute-done | bytes 16416 | tf_op jit(solution)/shard_map/ppermute | solution.py:25
  14.3 2.6 %collective-permute-done.2.refs_1_ = f32[2,24,128]{2,1,0:T(8,128)S(1)} collective-permute-done((f32[2,24,128]{2,1,0:T(8,128)S(1)}, f32[2,24,128]{2,1,0:T(8,128)S(1)}, u32[]{:S(2)}, u32[]{:S(2)}) %collective-permute-start.2) | collective-permute-done | bytes 24608 | tf_op jit(solution)/shard_map/ppermute | solution.py:25
  16.9 0.0 collective-permute-done.3.refs_2_
  16.9 0.4 %columns.1.refs_4_.sent_in = f32[8,768]{1,0:T(8,128)S(1)} custom-call(f32[4,24,8,128]{3,2,1,0:T(8,128)S(1)} %get-tuple-element.23.refs_0_, f32[2,24,128]{2,1,0:T(8,128)S(1)} %collective-permute-done.2.refs_1_, f32[2,24,128]{2,1,0:T(8,128)S(1)} %collective-permute-done.3.refs_2_, f32[224,128]{1,0:T(8,128)S(1)} %get-tuple-element.20.refs_3_.refs_0_.refs_1_, ...), custom_call_target="tpu_custom_call" | custom-call | tf_op jit(solution)/shard_map/columns/pallas_call | solution.py:467
  17.3 2.5 %collective-permute-start.4 = (f32[8,768]{1,0:T(8,128)S(1)}, f32[8,768]{1,0:T(8,128)S(1)}, u32[]{:S(2)}, u32[]{:S(2)}) collective-permute-start(f32[8,768]{1,0:T(8,128)S(1)} %columns.1.refs_4_.sent_in), channel_id=1, source_target_pairs={{0,4},{4,0},{1,5},{5,1},{2,6},{6,2},{3,7},{7,3},{8,12},{12,8},{9,1... | collective-permute-start | bytes 73736 | tf_op jit(solution)/shard_map/ppermute | solution.py:25
  19.8 1.8 %collective-permute-done.4.refs_3_.got_in = f32[8,768]{1,0:T(8,128)S(1)} collective-permute-done((f32[8,768]{1,0:T(8,128)S(1)}, f32[8,768]{1,0:T(8,128)S(1)}, u32[]{:S(2)}, u32[]{:S(2)}) %collective-permute-start.4) | collective-permute-done | bytes 24608 | tf_op jit(solution)/shard_map/ppermute | solution.py:25
  21.6 0.1 windows.1
  21.7 0.8 %collective-permute-start.5 = (f32[136,128]{1,0:T(8,128)S(1)}, f32[136,128]{1,0:T(8,128)S(1)}, u32[]{:S(2)}, u32[]{:S(2)}) collective-permute-start(f32[136,128]{1,0:T(8,128)S(1)} %get-tuple-element.27), channel_id=1, source_target_pairs={{0,1},{1,2},{2,3},{3,0},{4,5},{5,6},{6,7},{7,4},{8,9},{9,10},{10,1... | collective-permute-start | bytes 208904 | tf_op jit(solution)/shard_map/ppermute | solution.py:25
  22.5 1.6 %collective-permute-start.6 = (f32[136,128]{1,0:T(8,128)S(1)}, f32[136,128]{1,0:T(8,128)S(1)}, u32[]{:S(2)}, u32[]{:S(2)}) collective-permute-start(f32[136,128]{1,0:T(8,128)S(1)} %get-tuple-element.28), channel_id=1, source_target_pairs={{0,2},{1,3},{2,0},{3,1},{4,6},{5,7},{6,4},{7,5},{8,10},{9,11},{10,... | collective-permute-start | bytes 208904 | tf_op jit(solution)/shard_map/ppermute | solution.py:25
  24.1 1.6 %collective-permute-start.7 = (f32[136,128]{1,0:T(8,128)S(1)}, f32[136,128]{1,0:T(8,128)S(1)}, u32[]{:S(2)}, u32[]{:S(2)}) collective-permute-start(f32[136,128]{1,0:T(8,128)S(1)} %get-tuple-element.29), channel_id=1, source_target_pairs={{0,3},{1,0},{2,1},{3,2},{4,7},{5,4},{6,5},{7,6},{8,11},{9,8},{10,9... | collective-permute-start | bytes 208904 | tf_op jit(solution)/shard_map/ppermute | solution.py:25
  25.6 0.0 collective-permute-done.8.up_in
  25.6 0.0 collective-permute-done.9.down_in
  25.6 5.6 %soil_interior.1 = (f32[24,8,512]{2,1,0:T(8,128)}, f32[5,16,640]{2,1,0:T(8,128)S(1)}, s32[16,640]{1,0:T(8,128)S(1)}, f32[6,8,512]{2,1,0:T(8,128)S(1)}) custom-call(f32[8,128]{1,0:T(8,128)S(1)} %get-tuple-element.19.tab_ref.refs_0_, f32[24,8,512]{2,1,0:T(8,128)} %p_far.1, s32[24,8,512]{2,1,0:T(8,128)} %c_far.1, ...), custom_call_target="tpu_custom_call" | custom-call | tf_op jit(solution)/shard_map/soil_interior/pallas_call | solution.py:343
  31.2 0.0 collective-permute-done.5.refs_5_
  31.2 0.0 collective-permute-done.6.refs_6_
  31.2 0.0 collective-permute-done.7.refs_7_
  31.2 2.2 %surface_and_top.1 = (f32[24,8,512]{2,1,0:T(8,128)}, f32[32,128]{1,0:T(8,128)}) custom-call(f32[8,128]{1,0:T(8,128)S(1)} %get-tuple-element.19.tab_ref.refs_0_, f32[224,128]{1,0:T(8,128)S(1)} %get-tuple-element.20.refs_3_.refs_0_.refs_1_, f32[32,128]{1,0:T(8,128)S(1)} %collective-permute-done.refs_4_.refs_1_.refs_2_, ...), custom_call_target="tpu_custom_call", output_to_operand_aliasing={{0}: (11, {})} | custom-call | tf_op jit(solution)/shard_map/surface_and_top/pallas_call | solution.py:701
Async XLA Ops:
  2.0 23.6 %collective-permute-start.8 = (f32[2,2,24,512]{3,2,1,0:T(8,128)S(1)}, f32[2,2,24,512]{3,2,1,0:T(8,128)S(1)}, u32[]{:S(2)}, u32[]{:S(2)}) collective-permute-start(f32[2,2,24,512]{3,2,1,0:T(8,128)S(1)} %get-tuple-element.30), channel_id=1, source_target_pairs={{0,1},{1,2},{2,3},{3,8},{8,9},{9,10},{10,11},{11,16},{16,17},{17,1... | collective-permute-start | bytes 589832 | tf_op jit(solution)/shard_map/ppermute | solution.py:25
  5.1 20.5 %collective-permute-start.9 = (f32[2,2,24,512]{3,2,1,0:T(8,128)S(1)}, f32[2,2,24,512]{3,2,1,0:T(8,128)S(1)}, u32[]{:S(2)}, u32[]{:S(2)}) collective-permute-start(f32[2,2,24,512]{3,2,1,0:T(8,128)S(1)} %get-tuple-element.31), channel_id=1, source_target_pairs={{0,27},{1,0},{2,1},{3,2},{8,3},{9,8},{10,9},{11,10},{16,11},{17,16... | collective-permute-start | bytes 589832 | tf_op jit(solution)/shard_map/ppermute | solution.py:25
  7.6 4.4 %collective-permute-start = (f32[32,128]{1,0:T(8,128)S(1)}, f32[32,128]{1,0:T(8,128)S(1)}, u32[]{:S(2)}, u32[]{:S(2)}) collective-permute-start(f32[32,128]{1,0:T(8,128)S(1)} %get-tuple-element.21), channel_id=1, source_target_pairs={{0,8},{8,16},{16,24},{24,0},{1,9},{9,17},{17,25},{25,1},{2,10},{10... | collective-permute-start | bytes 49160 | tf_op jit(solution)/shard_map/ppermute | solution.py:25
  7.6 9.3 %collective-permute-start.2 = (f32[2,24,128]{2,1,0:T(8,128)S(1)}, f32[2,24,128]{2,1,0:T(8,128)S(1)}, u32[]{:S(2)}, u32[]{:S(2)}) collective-permute-start(f32[2,24,128]{2,1,0:T(8,128)S(1)} %get-tuple-element.24), channel_id=1, source_target_pairs={{0,1},{1,2},{2,3},{3,8},{8,9},{9,10},{10,11},{11,16},{16,17},{17,1... | collective-permute-start | bytes 73736 | tf_op jit(solution)/shard_map/ppermute | solution.py:25
  7.6 9.3 %collective-permute-start.3 = (f32[2,24,128]{2,1,0:T(8,128)S(1)}, f32[2,24,128]{2,1,0:T(8,128)S(1)}, u32[]{:S(2)}, u32[]{:S(2)}) collective-permute-start(f32[2,24,128]{2,1,0:T(8,128)S(1)} %get-tuple-element.25), channel_id=1, source_target_pairs={{0,27},{1,0},{2,1},{3,2},{8,3},{9,8},{10,9},{11,10},{16,11},{17,16... | collective-permute-start | bytes 73736 | tf_op jit(solution)/shard_map/ppermute | solution.py:25
  12.0 2.3 %collective-permute-start.1 = (f32[32,128]{1,0:T(8,128)S(1)}, f32[32,128]{1,0:T(8,128)S(1)}, u32[]{:S(2)}, u32[]{:S(2)}) collective-permute-start(f32[32,128]{1,0:T(8,128)S(1)} %get-tuple-element.22), channel_id=1, source_target_pairs={{0,24},{8,0},{16,8},{24,16},{1,25},{9,1},{17,9},{25,17},{2,26},{10... | collective-permute-start | bytes 49160 | tf_op jit(solution)/shard_map/ppermute | solution.py:25
  17.3 4.3 %collective-permute-start.4 = (f32[8,768]{1,0:T(8,128)S(1)}, f32[8,768]{1,0:T(8,128)S(1)}, u32[]{:S(2)}, u32[]{:S(2)}) collective-permute-start(f32[8,768]{1,0:T(8,128)S(1)} %columns.1.refs_4_.sent_in), channel_id=1, source_target_pairs={{0,4},{4,0},{1,5},{5,1},{2,6},{6,2},{3,7},{7,3},{8,12},{12,8},{9,1... | collective-permute-start | bytes 73736 | tf_op jit(solution)/shard_map/ppermute | solution.py:25
  21.7 9.5 %collective-permute-start.5 = (f32[136,128]{1,0:T(8,128)S(1)}, f32[136,128]{1,0:T(8,128)S(1)}, u32[]{:S(2)}, u32[]{:S(2)}) collective-permute-start(f32[136,128]{1,0:T(8,128)S(1)} %get-tuple-element.27), channel_id=1, source_target_pairs={{0,1},{1,2},{2,3},{3,0},{4,5},{5,6},{6,7},{7,4},{8,9},{9,10},{10,1... | collective-permute-start | bytes 208904 | tf_op jit(solution)/shard_map/ppermute | solution.py:25
  22.5 8.7 %collective-permute-start.6 = (f32[136,128]{1,0:T(8,128)S(1)}, f32[136,128]{1,0:T(8,128)S(1)}, u32[]{:S(2)}, u32[]{:S(2)}) collective-permute-start(f32[136,128]{1,0:T(8,128)S(1)} %get-tuple-element.28), channel_id=1, source_target_pairs={{0,2},{1,3},{2,0},{3,1},{4,6},{5,7},{6,4},{7,5},{8,10},{9,11},{10,... | collective-permute-start | bytes 208904 | tf_op jit(solution)/shard_map/ppermute | solution.py:25
  24.1 7.2 %collective-permute-start.7 = (f32[136,128]{1,0:T(8,128)S(1)}, f32[136,128]{1,0:T(8,128)S(1)}, u32[]{:S(2)}, u32[]{:S(2)}) collective-permute-start(f32[136,128]{1,0:T(8,128)S(1)} %get-tuple-element.29), channel_id=1, source_target_pairs={{0,3},{1,0},{2,1},{3,2},{4,7},{5,4},{6,5},{7,6},{8,11},{9,8},{10,9... | collective-permute-start | bytes 208904 | tf_op jit(solution)/shard_map/ppermute | solution.py:25

commit v7 on v6

--- a/solution.py
+++ b/solution.py
@@ -16,7 +16,7 @@
 
 LANES = 128
 SUBS = 8
-UNROLL = 8
+UNROLL = 12
 TOP_LAYERS = 2
 
 
@@ -102,30 +102,25 @@
     return (in_rows * in_cols).astype(jnp.float32)
 
 
-def soil_rows(p_ref, c_ref, blocks, next_ref, prev_ref, next_end, prev_end):
+def soil_rows(p_ref, c_ref, next_ref, prev_ref):
+    _, own, cols = p_ref.shape
+    n = cols // LANES
+    for f, x in enumerate((p_ref, c_ref)):
+        for r in range(2):
+            last, first = x[:, own - 2 + r, :].astype(jnp.float32), x[:, r, :].astype(jnp.float32)
+            for j, ch in enumerate(chunks(cols)):
+                next_ref[f, r * n + j] = last[:, ch]
+                prev_ref[f, r * n + j] = first[:, ch]
+
+
+def soil_columns(p_ref, c_ref, box):
     layers, own, cols = p_ref.shape
-    start = lax.broadcasted_iota(jnp.int32, (layers, LANES), 1) < LANES // 2
-    for f, x in enumerate((p_ref, c_ref)):
-        blocks[f] = x[:, :, :LANES].astype(jnp.float32)
-        blocks[2 + f] = x[:, :, cols - LANES :].astype(jnp.float32)
-        for r in range(2):
-            next_ref[f, r] = x[:, own - 2 + r, :].astype(jnp.float32)
-            prev_ref[f, r] = x[:, r, :].astype(jnp.float32)
-        next_end[f] = jnp.where(start, next_ref[f, 1, :, :LANES], next_ref[f, 1, :, cols - LANES :])
-        prev_end[f] = jnp.where(start, prev_ref[f, 0, :, :LANES], prev_ref[f, 0, :, cols - LANES :])
-
-
-def soil_columns(blocks, up_end, down_end, box):
-    _, layers, own, _ = blocks.shape
     rows = box.shape[1]
+    box[...] = jnp.zeros_like(box)
     out = []
-    for side in (2, 0):
-        for f in range(2):
-            box[:, 2 : 2 + own, :] = blocks[side + f]
-            box[:, 0, :] = jnp.zeros((layers, LANES), jnp.float32)
-            box[:, 1, :] = up_end[f]
-            box[:, own + 2, :] = down_end[f]
-            box[:, own + 3 :, :] = jnp.zeros((layers, rows - own - 3, LANES), jnp.float32)
+    for ch in (chunks(cols)[-1], chunks(cols)[0]):
+        for x in (p_ref, c_ref):
+            box[:, 2 : 2 + own, :] = x[:, :, ch].astype(jnp.float32)
             turned = box[...].reshape(layers * rows, LANES).T
             out.append(turned[LANES - 2 :] if len(out) < 2 else turned[:2])
     return jnp.concatenate(out, axis=0)
@@ -161,13 +156,23 @@
 
     gap = jnp.zeros((1, span), f32)
     p = jnp.concatenate([got[0:2], sent[4:5], gap, sent[1:2], got[4:6], gap], axis=0)
-    kind = jnp.concatenate([got[2:4], sent[6:7], gap, sent[3:4], got[6:8], gap], axis=0).astype(jnp.int32)
+    kind = jnp.concatenate([got[2:4], sent[6:7], gap, sent[3:4], got[6:8], gap], axis=0)
     sub = lax.broadcasted_iota(jnp.int32, (SUBS, span), 0)
     lane = lax.broadcasted_iota(jnp.int32, (SUBS, span), 1)
     row = lane % rows
     row_ok = jnp.where(row < 2, ok[0], jnp.where(row < own + 2, 1, jnp.where(row < own + 4, ok[1], 0)))
     col_ok = jnp.where(sub < 2, ok[2], jnp.where((sub == 2) | (sub == 4), 1, jnp.where((sub == 5) | (sub == 6), ok[3], 0)))
     mask = (row_ok * col_ok).astype(f32)
+    n = cols // LANES
+    corner[...] = jnp.zeros_like(corner)
+    found = []
+    for f in range(2):
+        corner[:, 1, :] = up_in[f, 2 * n]
+        corner[:, own + 2, :] = down_in[f, 2 * n]
+        turned = corner[...].reshape(span, LANES).T
+        found.append(jnp.concatenate([gap, turned[LANES - 1 :], gap, gap, gap, turned[:1], gap, gap], axis=0))
+    p = p + found[0]
+    kind = (kind + found[1]).astype(jnp.int32)
     values = [params(tab_ref, kind[:, ch]) for ch in chunks(span)]
     content, capacity, root = wide([closure(v, p[:, ch]) for v, ch in zip(values, chunks(span))])
     h, q = root * mask, root * mask * p
@@ -222,15 +227,15 @@
         inside = valid.astype(f32)
         ours = 0 if side == 0 else own - 1
         values, states, beyond = [], [], []
-        for ch in chunks(cols):
-            p = halo[0, close, :, ch]
-            v = params(tab_ref, halo[1, close, :, ch].astype(jnp.int32))
+        for j in range(n):
+            p = halo[0, close * n + j]
+            v = params(tab_ref, halo[1, close * n + j].astype(jnp.int32))
             content, capacity, root = closure(v, p)
             root = root * inside
             values.append(v)
             states.append((p, capacity, root, root * p))
-            p = halo[0, far, :, ch]
-            root = closure(params(tab_ref, halo[1, far, :, ch].astype(jnp.int32)), p)[2] * inside
+            p = halo[0, far * n + j]
+            root = closure(params(tab_ref, halo[1, far * n + j].astype(jnp.int32)), p)[2] * inside
             beyond.append((root, root * p))
         p, capacity, h, q = wide(states)
         far_h, far_q = wide(beyond)
@@ -301,15 +306,20 @@
         turn[LANES - 2 :, :] = got[halo_at : halo_at + 2]
         turn[:2, :] = got[halo_at + 4 : halo_at + 6]
         block = turn[:, :LANES].T
+        zlane1 = lax.broadcasted_iota(jnp.int32, (1, LANES), 1)
         for z in range(2):
             dst[z, own:, :cols] = jnp.zeros((SUBS, cols), dst.dtype)
             dst[z, :own, :cols] = src[z]
             dst[z, :, cols:] = jnp.zeros((rows, LANES), dst.dtype)
             dst[z, : own + 2, cols:] = block[z * rows + 2 : z * rows + own + 4].astype(dst.dtype)
             dst[z, rows - 2 :, cols:] = block[z * rows : z * rows + 2].astype(dst.dtype)
+            for at, halo in ((own, down_in), (rows - 1, up_in)):
+                ends = halo[f, 2 * n, z : z + 1, :]
+                dst[z, at : at + 1, cols:] = jnp.where((zlane1 == 0) | (zlane1 == LANES - 1), ends, 0.0).astype(dst.dtype)
             for r in range(2):
-                dst[z, own + r : own + r + 1, :cols] = down_in[f, r, z : z + 1, :].astype(dst.dtype)
-                dst[z, rows - 2 + r : rows - 1 + r, :cols] = up_in[f, r, z : z + 1, :].astype(dst.dtype)
+                for j, ch in enumerate(chunks(cols)):
+                    dst[z, own + r : own + r + 1, ch] = down_in[f, r * n + j, z : z + 1, :].astype(dst.dtype)
+                    dst[z, rows - 2 + r : rows - 1 + r, ch] = up_in[f, r * n + j, z : z + 1, :].astype(dst.dtype)
     width = cols + LANES
     mask = soil_mask(ok, rows, width, own, cols)
     states = []
@@ -396,32 +406,98 @@
 def pack(pressure, soil_class, classes, ground):
     layers, own, cols = pressure.shape
     f32 = jnp.float32
-    edge = pltpu.VMEM((2, 2, layers, cols), f32)
-    end = pltpu.VMEM((2, layers, LANES), f32)
-    out = [pltpu.VMEM((4, layers, own, LANES), f32), edge, edge, end, end]
+    rows = own + SUBS
+    span = layers * rows
+    edge = pltpu.VMEM((2, 2 * cols // LANES, layers, LANES), f32)
+    scratch = [pltpu.VMEM((layers, rows, LANES), f32)]
+    width, more = span, []
     if ground:
         height = ground[0].shape[0]
         strip = pltpu.VMEM((EDGE_ROWS + 4 * cols // LANES, LANES), f32)
-        out = [pltpu.VMEM((5 * height + 2 * own * cols // LANES, LANES), f32), strip, strip] + out
+        more = [pltpu.VMEM((5 * height + 2 * own * cols // LANES, LANES), f32), strip, strip]
+        tall = LANES + 5 * (height + SUBS)
+        tall += -tall % LANES
+        width += tall
+        scratch.append(pltpu.VMEM((tall, LANES), f32))
+    out = [pltpu.VMEM((SUBS, LANES), f32), pltpu.VMEM((SUBS, width), f32), edge, edge] + more
+    given = 2 + len(ground)
 
     def body(*refs):
         tables, rest = refs[: len(classes)], refs[len(classes) :]
+        fields, outs, boxes = rest[:given], rest[given : given + len(out)], rest[given + len(out) :]
+        outs[1][:, :span] = soil_columns(*fields[:2], boxes[0])
         if ground:
-            surface_rows(*rest[: 2 + len(ground)], *rest[3 + len(ground) : 6 + len(ground)])
-        soil_rows(*rest[:2], *rest[-5:])
-        rest[2 + len(ground)][...] = class_tables(tables)
+            surface_rows(*fields, *outs[4:])
+            outs[1][:, span:] = surface_columns(outs[4], boxes[1], height, own, cols)
+        soil_rows(*fields[:2], *outs[2:4])
+        outs[0][...] = class_tables(tables)
 
     vmem = pl.BlockSpec(memory_space=pltpu.VMEM)
     smem = pl.BlockSpec(memory_space=pltpu.SMEM)
     return pl.pallas_call(
         body,
-        out_shape=[pltpu.VMEM((SUBS, LANES), f32)] + out,
-        in_specs=[smem] * len(classes) + [vmem] * (2 + len(ground)),
+        out_shape=out,
+        in_specs=[smem] * len(classes) + [vmem] * given,
+        scratch_shapes=scratch,
         name="pack",
     )(*classes, pressure, soil_class, *ground)
 
 
-def surface_columns(main_ref, above_ref, below_ref, box, height, own, cols):
+def corners_kernel(got, *refs, layers, own, cols, height):
+    n = cols // LANES
+    rows = own + SUBS
+    span = layers * rows
+    count = len(refs) // 2 - 1
+    given, outs, (turn, box) = refs[:count], refs[count : 2 * count], refs[2 * count :]
+    lane = lax.broadcasted_iota(jnp.int32, (layers, LANES), 1)
+    turn[...] = jnp.zeros_like(turn)
+    turn[:SUBS, :] = got[...]
+    turned = turn[...].T
+    box[...] = turned[:span].reshape(layers, rows, LANES)
+    for i, row in ((0, own + 1), (1, 2)):
+        x = box[:, row, :]
+        outs[i][:, : 2 * n] = given[i][...]
+        for f in range(2):
+            left, right = pltpu.roll(x, LANES - 2 - 2 * f, 1), pltpu.roll(x, LANES - 4 - 2 * f, 1)
+            outs[i][f, 2 * n] = jnp.where(lane == LANES - 1, left, jnp.where(lane == 0, right, 0.0))
+    if count == 2:
+        return
+    moved = pltpu.roll(turned[span:], LANES - 3, 1)
+    lane = lax.broadcasted_iota(jnp.int32, (3, LANES), 1)
+    tall = height + SUBS
+    for i in range(2):
+        out = outs[2 + i]
+        base = given[2 + i].shape[0]
+        out[:base, :] = given[2 + i][...]
+        out[base:, :] = jnp.zeros((out.shape[0] - base, LANES), jnp.float32)
+        for f in range(5):
+            at = LANES + f * tall + (height - 3 if i == 0 else 0)
+            out[base + 3 * f : base + 3 * f + 3, :] = jnp.where((lane < 3) | (lane >= LANES - 3), moved[at : at + 3], 0.0)
+        for f in range(2):
+            at = own - 2 if i == 0 else 0
+            left, right = moved[2 * f * SUBS + at :][:2], moved[2 * (2 + f) * SUBS + at :][:2]
+            out[base + 16 + 2 * f : base + 18 + 2 * f, :] = rim(left, right, lane[:2], 2)
+
+
+CORNERS = 24
+
+
+def corners(got, layers, own, cols, height, rows, strips):
+    f32 = jnp.float32
+
+    def body(*refs):
+        corners_kernel(*refs, layers=layers, own=own, cols=cols, height=height)
+
+    return pl.pallas_call(
+        body,
+        out_shape=[pltpu.VMEM((2, 2 * cols // LANES + 1, layers, LANES), f32)] * 2
+        + [pltpu.VMEM((x.shape[0] + CORNERS, LANES), f32) for x in strips],
+        scratch_shapes=[pltpu.VMEM((LANES, got.shape[1]), f32), pltpu.VMEM((layers, own + SUBS, LANES), f32)],
+        name="corners",
+    )(*near(got, *rows, *strips))
+
+
+def surface_columns(main_ref, box, height, own, cols):
     n = cols // LANES
     tall = height + SUBS
     box[...] = jnp.zeros_like(box)
@@ -429,49 +505,15 @@
         for f in range(2):
             at = (2 * side + f) * 2 * SUBS
             src = 5 * height + (f * n + j) * own
-            strip = EDGE_ROWS + 2 * (f * n + j)
             box[at : at + own, :] = main_ref[src : src + own, :]
-            box[at + own : at + own + 2, :] = below_ref[strip : strip + 2, :]
-            box[at + own + 2 : at + own + 4, :] = above_ref[strip : strip + 2, :]
     for f in range(5):
         at = LANES + f * tall
         box[at : at + height, :] = main_ref[f * height : (f + 1) * height, :]
-        box[at + height : at + height + 3, :] = below_ref[3 * f : 3 * f + 3, :]
-        box[at + tall - 3 : at + tall, :] = above_ref[3 * f : 3 * f + 3, :]
     turned = box[...].T
     edges = jnp.concatenate([turned[LANES - 3 :], turned[:3], jnp.zeros((2, turned.shape[1]), jnp.float32)], axis=0)
     return edges
 
 
-def columns(blocks, cols, up_end, down_end, surface):
-    _, layers, own, _ = blocks.shape
-    rows = own + SUBS
-    span = layers * rows
-    scratch = [pltpu.VMEM((layers, rows, LANES), jnp.float32)]
-    width = span
-    if surface:
-        height = (surface[0].shape[0] - 2 * own * cols // LANES) // 5
-        tall = LANES + 5 * (height + SUBS)
-        tall += -tall % LANES
-        width += tall
-        scratch.append(pltpu.VMEM((tall, LANES), jnp.float32))
-
-    n = 3 + len(surface)
-
-    def body(*refs):
-        out_ref, box = refs[n], refs[n + 1]
-        out_ref[:, :span] = soil_columns(*refs[:3], box)
-        if surface:
-            out_ref[:, span:] = surface_columns(*refs[3:n], refs[n + 2], height, own, cols)
-
-    return pl.pallas_call(
-        body,
-        out_shape=pltpu.VMEM((SUBS, width), jnp.float32),
-        scratch_shapes=scratch,
-        name="columns",
-    )(*near(blocks, up_end, down_end, *surface))
-
-
 def rim(at_end, at_start, lane, count):
     return jnp.where(lane >= LANES - count, at_end, jnp.where(lane < count, at_start, 0.0))
 
@@ -484,7 +526,7 @@
 
 
 def windows_kernel(main, above, below, got, sent, *refs, span, height, own, count):
-    outs, (tall, wide_top, ends, turn) = refs[:count], refs[count:]
+    outs, (tall, wide_top, ends, turn, flat) = refs[:count], refs[count:]
     line = lax.axis_index("gy")
     lane = lax.broadcasted_iota(jnp.int32, (SUBS, LANES), 1)
     sub = lax.broadcasted_iota(jnp.int32, (SUBS, LANES), 0)
@@ -501,9 +543,9 @@
     last = line == count - 1
     for f in range(2):
         before, after = block[2 * f * SUBS :], block[2 * (2 + f) * SUBS :]
+        spot = above.shape[0] - CORNERS + 16 + 2 * f
         beside = rim(before[:SUBS], after[:SUBS], lane, 2)
-        beyond = rim(before[SUBS : 2 * SUBS], after[SUBS : 2 * SUBS], lane, 2)
-        beyond = jnp.where(last, beyond[2:4], beyond[:2])
+        beyond = jnp.where(last, above[spot : spot + 2, :], below[spot : spot + 2, :])
         for j in (0, count + 1):
             wide_top[f, j] = beside
             ends[j, 2 * f : 2 * f + 2] = beyond
@@ -512,6 +554,17 @@
             wide_top[f, j + 1] = main[src : src + own, :]
             at = EDGE_ROWS + 2 * (f * count + j)
             ends[j + 1, 2 * f : 2 * f + 2] = jnp.where(last, above[at : at + 2, :], below[at : at + 2, :])
+    edges = []
+    for source, base in ((got, above.shape[0] - CORNERS), (sent, 0)):
+        flat[...] = jnp.zeros_like(flat)
+        for f in range(5):
+            at = f * (height + SUBS) + height
+            flat[at : at + 3, :] = below[base + 3 * f : base + 3 * f + 3, :]
+            flat[at + SUBS - 3 : at + SUBS, :] = above[base + 3 * f : base + 3 * f + 3, :]
+        turned = flat[...].T
+        edges.append((source[:3, span + LANES :] + turned[LANES - 3 :], source[3:6, span + LANES :] + turned[:3]))
+    before = jnp.where(last, edges[0][0], edges[1][0])
+    after = jnp.where(line == 0, edges[0][1], edges[1][1])
     for s in range(count):
         who, out = (line + s) % count, outs[s]
         for f in range(5):
@@ -527,10 +580,9 @@
         out[14 * SUBS : 14 * SUBS + 4, :] = mid[:4]
         out[14 * SUBS + 4 : 15 * SUBS, :] = side[:4]
         for j in range(2):
-            cut = slice(span + (j + 1) * LANES, span + (j + 2) * LANES)
             at = (15 + j) * SUBS
-            out[at : at + 3, :] = jnp.where(last, got[:3, cut], sent[:3, cut])
-            out[at + 3 : at + 6, :] = jnp.where(line == 0, got[3:6, cut], sent[3:6, cut])
+            out[at : at + 3, :] = before[:, j * LANES : (j + 1) * LANES]
+            out[at + 3 : at + 6, :] = after[:, j * LANES : (j + 1) * LANES]
             out[at + 6 : at + SUBS, :] = jnp.zeros((2, LANES), jnp.float32)
 
 
@@ -546,6 +598,7 @@
             pltpu.VMEM((2, count + 2, own, LANES), jnp.float32),
             pltpu.VMEM((count + 2, SUBS, LANES), jnp.float32),
             pltpu.VMEM((LANES, LANES), jnp.float32),
+            pltpu.VMEM((2 * LANES, LANES), jnp.float32),
         ],
         name="windows",
     )(*near(main, above, below, got, sent))
@@ -817,24 +870,18 @@
     ground = (depth, elevation, roughness, rain, land_mask, channel_mask)
     classes = (capacity_range, inverse_entry, shape_index, conductivity)
     even = scols == LANES and own == SUBS
-    tables, *packed = pack(pressure, soil_class, classes, ground if even else ())
-    blocks, after, before, after_end, before_end = packed[-5:]
-    surface = ()
-    if even:
-        main, strip_after, strip_before = packed[:3]
-        above = shift(strip_after, "grp", 1)
-        below = shift(strip_before, "grp", -1)
-        surface = (main, above, below)
-    rows = ("grp", "gy")
-    up_end = shift(after_end, rows, 1)
-    down_end = shift(before_end, rows, -1)
-    sent = columns(blocks, cols, up_end, down_end, surface)
-    up = shift(after, rows, 1)
-    down = shift(before, rows, -1)
+    tables, sent, *packed = pack(pressure, soil_class, classes, ground if even else ())
     span = pressure.shape[0] * (own + SUBS)
     half = jnp.where(lax.broadcasted_iota(jnp.int32, sent.shape, 1) < span, 4, 3)
     got = gx_trade(sent, lax.broadcasted_iota(jnp.int32, sent.shape, 0) < half)
+    after, before, *strips = corners(got, pressure.shape[0], own, cols, srows, packed[:2], packed[3:])
+    rows = ("grp", "gy")
+    up = shift(after, rows, 1)
+    down = shift(before, rows, -1)
     if even:
+        above = shift(strips[0], "grp", 1)
+        below = shift(strips[1], "grp", -1)
+        main = packed[2]
         outs = windows(main, above, below, got, sent, span, srows, own, ny)
         fields = [main, above, below, outs[0]] + [shift(outs[step], "gy", step) for step in range(1, ny)]
     else:

time: 33.6 us -> 28.5 us (0.85)
  the two profiles are of different devices: /device:TPU:0 before, /device:TPU:1 now
where the time goes in v7:
time: 28.5 us; the launch traced here: 28.3 us
  starting transfers between devices  13.1 us (46%)
  Pallas kernels  9.7 us (34%)
  waiting for transfers between devices  4.82 us (17%)
  between operations  0.7 us (2%)
    ppermute x8, starting transfers between devices, shift(): return lax.ppermute(x, axis, [(i, (i + step) % size) for i in range(size)])  13.1 us
    pallas_call x1, Pallas kernels, soil_interior(): pl.pallas_call(soil_kernel, out_shape=(jax.ShapeDtypeStruct(pressure.shap...  5.41 us
    ppermute x8, waiting for transfers between devices, shift(): return lax.ppermute(x, axis, [(i, (i + step) % size) for i in range(size)])  4.82 us
    pallas_call x1, Pallas kernels, finish(): pl.pallas_call(body, out_shape=(jax.ShapeDtypeStruct(head.shape, jnp.floa...  2.15 us
    pallas_call x1, Pallas kernels, pack(): pl.pallas_call(body, out_shape=out, in_specs=[smem] * len(classes) + [vme...  1.71 us
  transfers between devices with their start and end apart: 8, of which 3 were waited for; matrix products, arithmetic and copies ran while one was open for 0% of the time, Pallas kernels for 20%

profile of v7, /device:TPU:1, one launch (start us, length us, event | category | flops | bytes accessed | tf_op | source)
XLA Modules:
  0.0 28.3 jit_solution(10758489986626426545)
XLA Ops:
  0.6 1.7 %pack.1 = (f32[8,128]{1,0:T(8,128)S(1)}, f32[8,768]{1,0:T(8,128)S(1)}, f32[2,8,24,128]{3,2,1,0:T(8,128)S(1)}, f32[2,8,24,128]{3,2,1,0:T(8,128)S(1)}, f32[224,128...) custom-call(f32[12]{0:T(128)} %refs_0_.1, f32[12]{0:T(128)} %refs_1_.1, f32[12]{0:T(128)} %refs_2_.1, ...), custom_call_target="tpu_custom_call" | custom-call | tf_op jit(solution)/shard_map/pack/pallas_call | solution.py:437
  2.4 2.1 %collective-permute-start = (f32[8,768]{1,0:T(8,128)S(1)}, f32[8,768]{1,0:T(8,128)S(1)}, u32[]{:S(2)}, u32[]{:S(2)}) collective-permute-start(f32[8,768]{1,0:T(8,128)S(1)} %get-tuple-element.23.refs_4_.sent_in), channel_id=1, source_target_pairs={{0,4},{4,0},{1,5},{5,1},{2,6},{6,2},{3,7},{7,3},{8,12},{12,8},{9,1... | collective-permute-start | bytes 73736 | tf_op jit(solution)/shard_map/ppermute | solution.py:25
  4.5 1.2 %collective-permute-done.refs_0_.refs_3_.got_in = f32[8,768]{1,0:T(8,128)S(1)} collective-permute-done((f32[8,768]{1,0:T(8,128)S(1)}, f32[8,768]{1,0:T(8,128)S(1)}, u32[]{:S(2)}, u32[]{:S(2)}) %collective-permute-start) | collective-permute-done | bytes 24608 | tf_op jit(solution)/shard_map/ppermute | solution.py:25
  5.7 0.3 corners.1
  6.0 1.6 %collective-permute-start.6 = (f32[2,9,24,128]{3,2,1,0:T(8,128)S(1)}, f32[2,9,24,128]{3,2,1,0:T(8,128)S(1)}, u32[]{:S(2)}, u32[]{:S(2)}) collective-permute-start(f32[2,9,24,128]{3,2,1,0:T(8,128)S(1)} %get-tuple-element.34), channel_id=1, source_target_pairs={{0,1},{1,2},{2,3},{3,8},{8,9},{9,10},{10,11},{11,16},{16,17},{17,1... | collective-permute-start | bytes 663560 | tf_op jit(solution)/shard_map/ppermute | solution.py:25
  7.6 3.8 %collective-permute-start.7 = (f32[2,9,24,128]{3,2,1,0:T(8,128)S(1)}, f32[2,9,24,128]{3,2,1,0:T(8,128)S(1)}, u32[]{:S(2)}, u32[]{:S(2)}) collective-permute-start(f32[2,9,24,128]{3,2,1,0:T(8,128)S(1)} %get-tuple-element.35), channel_id=1, source_target_pairs={{0,27},{1,0},{2,1},{3,2},{8,3},{9,8},{10,9},{11,10},{16,11},{17,16... | collective-permute-start | bytes 663560 | tf_op jit(solution)/shard_map/ppermute | solution.py:25
  11.4 2.3 %collective-permute-start.1 = (f32[56,128]{1,0:T(8,128)S(1)}, f32[56,128]{1,0:T(8,128)S(1)}, u32[]{:S(2)}, u32[]{:S(2)}) collective-permute-start(f32[56,128]{1,0:T(8,128)S(1)} %get-tuple-element.28), channel_id=1, source_target_pairs={{0,8},{8,16},{16,24},{24,0},{1,9},{9,17},{17,25},{25,1},{2,10},{10... | collective-permute-start | bytes 86024 | tf_op jit(solution)/shard_map/ppermute | solution.py:25
  13.6 0.0 collective-permute-start.2
  13.6 1.0 %collective-permute-done.1.refs_1_.refs_2_ = f32[56,128]{1,0:T(8,128)S(1)} collective-permute-done((f32[56,128]{1,0:T(8,128)S(1)}, f32[56,128]{1,0:T(8,128)S(1)}, u32[]{:S(2)}, u32[]{:S(2)}) %collective-permute-start.1) | collective-permute-done | bytes 28704 | tf_op jit(solution)/shard_map/ppermute | solution.py:25
  14.6 2.6 %collective-permute-done.2.refs_2_.refs_3_ = f32[56,128]{1,0:T(8,128)S(1)} collective-permute-done((f32[56,128]{1,0:T(8,128)S(1)}, f32[56,128]{1,0:T(8,128)S(1)}, u32[]{:S(2)}, u32[]{:S(2)}) %collective-permute-start.2) | collective-permute-done | bytes 28704 | tf_op jit(solution)/shard_map/ppermute | solution.py:25
  17.2 0.2 windows.1
  17.4 0.1 collective-permute-start.3
  17.4 1.2 %collective-permute-start.4 = (f32[136,128]{1,0:T(8,128)S(1)}, f32[136,128]{1,0:T(8,128)S(1)}, u32[]{:S(2)}, u32[]{:S(2)}) collective-permute-start(f32[136,128]{1,0:T(8,128)S(1)} %get-tuple-element.32), channel_id=1, source_target_pairs={{0,2},{1,3},{2,0},{3,1},{4,6},{5,7},{6,4},{7,5},{8,10},{9,11},{10,... | collective-permute-start | bytes 208904 | tf_op jit(solution)/shard_map/ppermute | solution.py:25
  18.6 2.1 %collective-permute-start.5 = (f32[136,128]{1,0:T(8,128)S(1)}, f32[136,128]{1,0:T(8,128)S(1)}, u32[]{:S(2)}, u32[]{:S(2)}) collective-permute-start(f32[136,128]{1,0:T(8,128)S(1)} %get-tuple-element.33), channel_id=1, source_target_pairs={{0,3},{1,0},{2,1},{3,2},{4,7},{5,4},{6,5},{7,6},{8,11},{9,8},{10,9... | collective-permute-start | bytes 208904 | tf_op jit(solution)/shard_map/ppermute | solution.py:25
  20.7 0.0 collective-permute-done.6.up_in
  20.7 0.0 collective-permute-done.7.down_in
  20.7 5.4 %soil_interior.1 = (f32[24,8,512]{2,1,0:T(8,128)}, f32[5,16,640]{2,1,0:T(8,128)S(1)}, s32[16,640]{1,0:T(8,128)S(1)}, f32[6,8,512]{2,1,0:T(8,128)S(1)}) custom-call(f32[8,128]{1,0:T(8,128)S(1)} %get-tuple-element.21.tab_ref.refs_0_, f32[24,8,512]{2,1,0:T(8,128)} %p_far.1, s32[24,8,512]{2,1,0:T(8,128)} %c_far.1, ...), custom_call_target="tpu_custom_call" | custom-call | tf_op jit(solution)/shard_map/soil_interior/pallas_call | solution.py:353
  26.1 0.0 collective-permute-done.3.refs_5_
  26.1 0.0 collective-permute-done.4.refs_6_
  26.1 0.0 collective-permute-done.5.refs_7_
  26.2 2.1 %surface_and_top.1 = (f32[24,8,512]{2,1,0:T(8,128)}, f32[32,128]{1,0:T(8,128)}) custom-call(f32[8,128]{1,0:T(8,128)S(1)} %get-tuple-element.21.tab_ref.refs_0_, f32[224,128]{1,0:T(8,128)S(1)} %get-tuple-element.22.refs_0_.refs_1_, f32[56,128]{1,0:T(8,128)S(1)} %collective-permute-done.1.refs_1_.refs_2_, ...), custom_call_target="tpu_custom_call", output_to_operand_aliasing={{0}: (11, {})} | custom-call | tf_op jit(solution)/shard_map/surface_and_top/pallas_call | solution.py:754
Async XLA Ops:
  2.4 3.3 %collective-permute-start = (f32[8,768]{1,0:T(8,128)S(1)}, f32[8,768]{1,0:T(8,128)S(1)}, u32[]{:S(2)}, u32[]{:S(2)}) collective-permute-start(f32[8,768]{1,0:T(8,128)S(1)} %get-tuple-element.23.refs_4_.sent_in), channel_id=1, source_target_pairs={{0,4},{4,0},{1,5},{5,1},{2,6},{6,2},{3,7},{7,3},{8,12},{12,8},{9,1... | collective-permute-start | bytes 73736 | tf_op jit(solution)/shard_map/ppermute | solution.py:25
  6.0 14.7 %collective-permute-start.6 = (f32[2,9,24,128]{3,2,1,0:T(8,128)S(1)}, f32[2,9,24,128]{3,2,1,0:T(8,128)S(1)}, u32[]{:S(2)}, u32[]{:S(2)}) collective-permute-start(f32[2,9,24,128]{3,2,1,0:T(8,128)S(1)} %get-tuple-element.34), channel_id=1, source_target_pairs={{0,1},{1,2},{2,3},{3,8},{8,9},{9,10},{10,11},{11,16},{16,17},{17,1... | collective-permute-start | bytes 663560 | tf_op jit(solution)/shard_map/ppermute | solution.py:25
  7.6 13.2 %collective-permute-start.7 = (f32[2,9,24,128]{3,2,1,0:T(8,128)S(1)}, f32[2,9,24,128]{3,2,1,0:T(8,128)S(1)}, u32[]{:S(2)}, u32[]{:S(2)}) collective-permute-start(f32[2,9,24,128]{3,2,1,0:T(8,128)S(1)} %get-tuple-element.35), channel_id=1, source_target_pairs={{0,27},{1,0},{2,1},{3,2},{8,3},{9,8},{10,9},{11,10},{16,11},{17,16... | collective-permute-start | bytes 663560 | tf_op jit(solution)/shard_map/ppermute | solution.py:25
  11.4 3.3 %collective-permute-start.1 = (f32[56,128]{1,0:T(8,128)S(1)}, f32[56,128]{1,0:T(8,128)S(1)}, u32[]{:S(2)}, u32[]{:S(2)}) collective-permute-start(f32[56,128]{1,0:T(8,128)S(1)} %get-tuple-element.28), channel_id=1, source_target_pairs={{0,8},{8,16},{16,24},{24,0},{1,9},{9,17},{17,25},{25,1},{2,10},{10... | collective-permute-start | bytes 86024 | tf_op jit(solution)/shard_map/ppermute | solution.py:25
  13.6 3.6 %collective-permute-start.2 = (f32[56,128]{1,0:T(8,128)S(1)}, f32[56,128]{1,0:T(8,128)S(1)}, u32[]{:S(2)}, u32[]{:S(2)}) collective-permute-start(f32[56,128]{1,0:T(8,128)S(1)} %get-tuple-element.29), channel_id=1, source_target_pairs={{0,24},{8,0},{16,8},{24,16},{1,25},{9,1},{17,9},{25,17},{2,26},{10... | collective-permute-start | bytes 86024 | tf_op jit(solution)/shard_map/ppermute | solution.py:25
  17.4 8.7 %collective-permute-start.3 = (f32[136,128]{1,0:T(8,128)S(1)}, f32[136,128]{1,0:T(8,128)S(1)}, u32[]{:S(2)}, u32[]{:S(2)}) collective-permute-start(f32[136,128]{1,0:T(8,128)S(1)} %get-tuple-element.31), channel_id=1, source_target_pairs={{0,1},{1,2},{2,3},{3,0},{4,5},{5,6},{6,7},{7,4},{8,9},{9,10},{10,1... | collective-permute-start | bytes 208904 | tf_op jit(solution)/shard_map/ppermute | solution.py:25
  17.4 8.7 %collective-permute-start.4 = (f32[136,128]{1,0:T(8,128)S(1)}, f32[136,128]{1,0:T(8,128)S(1)}, u32[]{:S(2)}, u32[]{:S(2)}) collective-permute-start(f32[136,128]{1,0:T(8,128)S(1)} %get-tuple-element.32), channel_id=1, source_target_pairs={{0,2},{1,3},{2,0},{3,1},{4,6},{5,7},{6,4},{7,5},{8,10},{9,11},{10,... | collective-permute-start | bytes 208904 | tf_op jit(solution)/shard_map/ppermute | solution.py:25
  18.6 7.5 %collective-permute-start.5 = (f32[136,128]{1,0:T(8,128)S(1)}, f32[136,128]{1,0:T(8,128)S(1)}, u32[]{:S(2)}, u32[]{:S(2)}) collective-permute-start(f32[136,128]{1,0:T(8,128)S(1)} %get-tuple-element.33), channel_id=1, source_target_pairs={{0,3},{1,0},{2,1},{3,2},{4,7},{5,4},{6,5},{7,6},{8,11},{9,8},{10,9... | collective-permute-start | bytes 208904 | tf_op jit(solution)/shard_map/ppermute | solution.py:25
